TPU v7x, 16 devices: a 4x2x1 block of a 4x4x8 slice. The times are simulated.
16 devices in a mesh: dp: 2 (over y, z), ep: 8 (over x, core).
Axes of the slice: x: 4, y: 2, z: 1, core: 2. Of those that a mesh axis runs over, the one named last changes fastest.
The devices are a block of a 4x4x8 slice.
Arguments:
- x_in: bfloat16 [1024, 768], P(('dp', 'ep')), parts along dimension 0
- idx_a: int32 [1024, 8], P(('dp', 'ep')), parts along dimension 0
- idx_b: int32 [1024, 8], P(('dp', 'ep')), parts along dimension 0
- gate_a: float32 [1024, 8], P(('dp', 'ep')), parts along dimension 0
- gate_b: float32 [1024, 8], P(('dp', 'ep')), parts along dimension 0
- dy_out: bfloat16 [1024, 768], P(('dp', 'ep')), parts along dimension 0
- w1_a: bfloat16 [128, 768, 256], P('ep')
- w3_a: bfloat16 [128, 768, 256], P('ep')
- w2_a: bfloat16 [128, 256, 768], P('ep')
- w1_b: bfloat16 [128, 768, 256], P('ep')
- w3_b: bfloat16 [128, 768, 256], P('ep')
- w2_b: bfloat16 [128, 256, 768], P('ep')
Outputs:
- output 1: bfloat16 [1024, 768], P(('dp', 'ep')), parts along dimension 0
- output 2: bfloat16 [1024, 768], P(('dp', 'ep')), parts along dimension 0
- output 3: float32 [256, 768, 256], P(('dp', 'ep')), parts along dimension 0
- output 4: float32 [256, 768, 256], P(('dp', 'ep')), parts along dimension 0
- output 5: float32 [256, 256, 768], P(('dp', 'ep')), parts along dimension 0
- output 6: float32 [256, 768, 256], P(('dp', 'ep')), parts along dimension 0
- output 7: float32 [256, 768, 256], P(('dp', 'ep')), parts along dimension 0
- output 8: float32 [256, 256, 768], P(('dp', 'ep')), parts along dimension 0
- output 9: float32 [1024, 8], P(('dp', 'ep')), parts along dimension 0
- output 10: float32 [1024, 8], P(('dp', 'ep')), parts along dimension 0
There are 2 independent parts. A program takes and returns all parts, laid end to end along the dimension named above; an argument that names none is the same for every part.
All inputs are finite; a program needn't handle non-finite values.
Results may differ from a plain program's by a relative error of at most 0.00668.
Values are sent between devices in bfloat16 or wider.
A program may use at most 768 MiB of HBM per device.

v0:
```python
import jax
import jax.numpy as jnp
from jax import lax
from jax.sharding import PartitionSpec as P

CAP_FACTOR = 4


def slot_maps(dev_ids, experts, capacity):
    pair_total = dev_ids.shape[0] * dev_ids.shape[1]
    flat_ids = dev_ids.reshape(-1)
    onehot = (flat_ids[:, None] == jnp.arange(experts, dtype=jnp.int32)[None, :]).astype(jnp.int32)
    pair_slot = jnp.sum(jnp.cumsum(onehot, axis=0) * onehot, axis=1) - 1
    pair_row = flat_ids * capacity + pair_slot
    pair_ids = jnp.arange(pair_total, dtype=jnp.int32)
    row_pair = jnp.full((experts * capacity,), pair_total, jnp.int32).at[pair_row].set(pair_ids)
    return pair_row, row_pair


def send_rows(rows, index, capacity):
    send_buf = jnp.take(rows, index, axis=0, mode="fill", fill_value=0)
    send_buf = send_buf.reshape((index.shape[0] // capacity, capacity) + send_buf.shape[1:])
    return lax.all_to_all(send_buf, "ep", 0, 1, tiled=True)


def send_back(rows):
    back_rows = lax.all_to_all(rows, "ep", 1, 0, tiled=True)
    return back_rows.reshape((back_rows.shape[0] * back_rows.shape[1],) + back_rows.shape[2:])


def expert_forward(u_rows, w_gate, w_up, w_down):
    pre_gate = jnp.einsum("erd,edf->erf", u_rows, w_gate, preferred_element_type=jnp.float32)
    pre_up = jnp.einsum("erd,edf->erf", u_rows, w_up, preferred_element_type=jnp.float32)
    hidden = (jax.nn.silu(pre_gate) * pre_up).astype(jnp.bfloat16)
    out_rows = jnp.einsum("erf,efd->erd", hidden, w_down, preferred_element_type=jnp.float32).astype(jnp.bfloat16)
    return pre_gate, pre_up, hidden, out_rows


def expert_backward(u_rows, dy_rows, gate_rows, w_gate, w_up, w_down):
    pre_gate, pre_up, hidden, out_rows = expert_forward(u_rows, w_gate, w_up, w_down)
    dgate_rows = jnp.einsum("erd,erd->er", dy_rows, out_rows, preferred_element_type=jnp.float32)
    d_out = (gate_rows[:, :, None] * dy_rows).astype(jnp.bfloat16)
    dw_down = jnp.einsum("erf,erd->efd", hidden, d_out, preferred_element_type=jnp.float32)
    d_hidden = jnp.einsum("erd,efd->erf", d_out, w_down, preferred_element_type=jnp.float32)
    gate_sig = jax.nn.sigmoid(pre_gate)
    d_pre_gate = (d_hidden * pre_up * gate_sig * (1.0 + pre_gate * (1.0 - gate_sig))).astype(jnp.bfloat16)
    d_pre_up = (d_hidden * jax.nn.silu(pre_gate)).astype(jnp.bfloat16)
    dw_gate = jnp.einsum("erd,erf->edf", u_rows, d_pre_gate, preferred_element_type=jnp.float32)
    dw_up = jnp.einsum("erd,erf->edf", u_rows, d_pre_up, preferred_element_type=jnp.float32)
    du_rows = (jnp.einsum("erf,edf->erd", d_pre_gate, w_gate, preferred_element_type=jnp.float32) + jnp.einsum("erf,edf->erd", d_pre_up, w_up, preferred_element_type=jnp.float32)).astype(jnp.bfloat16)
    return du_rows, dgate_rows, dw_gate, dw_up, dw_down


def combine(x_rows, gates, back_rows, pair_row):
    tok_dev, top_k = gates.shape
    out_pairs = jnp.take(back_rows, pair_row, axis=0).reshape(tok_dev, top_k, -1)
    branch = jnp.sum(gates[:, :, None] * out_pairs, axis=1)
    return (x_rows.astype(jnp.float32) + branch).astype(jnp.bfloat16)


def layer_backward(dy_rows, u_rows, gates, row_maps, capacity, w_gate, w_up, w_down):
    pair_row, row_pair = row_maps
    tok_dev, top_k = gates.shape
    dy_sent = send_rows(dy_rows, row_pair // top_k, capacity)
    gate_sent = send_rows(gates.reshape(-1), row_pair, capacity)
    u_rows, dy_sent = lax.optimization_barrier((u_rows, dy_sent))
    du_rows, dgate_rows, dw_gate, dw_up, dw_down = expert_backward(u_rows, dy_sent, gate_sent, w_gate, w_up, w_down)
    du_pairs = jnp.take(send_back(du_rows), pair_row, axis=0).reshape(tok_dev, top_k, -1)
    dx_rows = (dy_rows.astype(jnp.float32) + jnp.sum(du_pairs, axis=1, dtype=jnp.float32)).astype(jnp.bfloat16)
    dgate_out = jnp.take(send_back(dgate_rows), pair_row, axis=0).reshape(tok_dev, top_k)
    return dx_rows, dgate_out, (dw_gate, dw_up, dw_down)


def solution(mesh):
    n_group = mesh.shape["ep"]
    tok_spec = P(("dp", "ep"))
    w_spec = P("ep")

    def device_program(x_in, idx_a, idx_b, gate_a, gate_b, dy_out, w1_a, w3_a, w2_a, w1_b, w3_b, w2_b):
        tok_dev, top_k = idx_a.shape
        experts = w1_a.shape[0] * n_group
        capacity = CAP_FACTOR * tok_dev * top_k // experts
        maps_a = slot_maps(idx_a, experts, capacity)
        maps_b = slot_maps(idx_b, experts, capacity)
        u_rows_a = send_rows(x_in, maps_a[1] // top_k, capacity)
        out_a = expert_forward(u_rows_a, w1_a, w3_a, w2_a)[3]
        x_mid = combine(x_in, gate_a, send_back(out_a), maps_a[0])
        u_rows_b = send_rows(x_mid, maps_b[1] // top_k, capacity)
        out_b = expert_forward(u_rows_b, w1_b, w3_b, w2_b)[3]
        x_out = combine(x_mid, gate_b, send_back(out_b), maps_b[0])
        dx_mid, dgate_b, grads_b = layer_backward(dy_out, u_rows_b, gate_b, maps_b, capacity, w1_b, w3_b, w2_b)
        x_again, dx_mid = lax.optimization_barrier((x_in, dx_mid))
        u_again = send_rows(x_again, maps_a[1] // top_k, capacity)
        dx_in, dgate_a, grads_a = layer_backward(dx_mid, u_again, gate_a, maps_a, capacity, w1_a, w3_a, w2_a)
        return (x_out, dx_in) + grads_a + grads_b + (dgate_a, dgate_b)

    return jax.shard_map(device_program, mesh=mesh, in_specs=(tok_spec,) * 6 + (w_spec,) * 6, out_specs=(tok_spec,) * 10, check_vma=False)
```

profile of v0, /device:TPU:113, one launch (start us, length us, event | category | flops | bytes accessed | tf_op | source)
XLA Modules:
  0.0 567.3 jit_solution(1756488589705780000)
XLA Ops:
  5.7 7.6 %gather_fusion = bf16[2048,768]{1,0:T(8,128)(2,1)S(1)} fusion(bf16[64,768]{1,0:T(8,128)(2,1)S(1)} %copy-done, s32[2048]{0:T(1024)S(1)} %get-tuple-element.69), kind=kCustom, calls=%fused_computation.clone | custom fusion | bytes 6299648 | tf_op jit(solution)/shard_map/jit(_take)/gather | solution.py:21
  13.8 43.5 %all_to_all.214 = bf16[128,16,768]{2,1,0:T(8,128)(2,1)S(1)} all-to-all(bf16[128,16,768]{2,1,0:T(8,128)(2,1)S(1)} %bitcast.167), channel_id=1, replica_groups=mesh['dp'=2,'ep'=8] {'ep'}, dimensions={0} | all-to-all | bytes 6291456 | tf_op jit(solution)/shard_map/all_to_all | solution.py:23
  60.0 9.1 %convolution_convert_fusion.1 = bf16[16,128,768]{2,1,0:T(8,128)(2,1)} fusion(bf16[16,256,768]{2,1,0:T(8,128)(2,1)} %param.28, f32[16,128,256]{2,1,0:T(8,128)} %fusion.38, bf16[16,128,768]{2,1,0:T(8,128)(2,1)S(1)} %bitcast.164, bf16[16,768,256]{2,1,0:T(8,128)(2,1)} %param.27), kind=kOutput, calls=%fused_computation.35 | convolution fusion | flops 1615331328 | bytes 20971520 | tf_op jit(solution)/shard_map/erf,efd->erd/dot_general | solution.py:35
  84.5 13.2 %gather_fusion.4 = f32[2048]{0:T(1024)S(1)} fusion(f32[512]{0:T(512)S(1)} %reshape.233, s32[2048]{0:T(1024)S(1)} %get-tuple-element.70), kind=kCustom, calls=%fused_computation.2.clone | custom fusion | bytes 24576 | tf_op jit(solution)/shard_map/jit(_take)/gather | solution.py:21
  98.5 9.4 %gather_fusion.5 = bf16[2048,768]{1,0:T(8,128)(2,1)} fusion(bf16[64,768]{1,0:T(8,128)(2,1)S(1)} %copy-done.1, s32[2048]{0:T(1024)S(1)} %get-tuple-element.71), kind=kCustom, calls=%fused_computation.5.clone | custom fusion | bytes 6299648 | tf_op jit(solution)/shard_map/jit(_take)/gather | solution.py:21
  108.5 8.9 %all-to-all-done.1 = bf16[16,128,768]{2,0,1:T(8,128)(2,1)} async-done(((bf16[16,128,768]{2,0,1:T(8,128)(2,1)}), bf16[16,128,768]{2,0,1:T(8,128)(2,1)}, u32[]{:S(2)}, u32[]{:S(2)}) %all-to-all-start.1) | async-done | bytes 3145760 | tf_op jit(solution)/shard_map/all_to_all | solution.py:27
  129.6 9.4 %gather_fusion.2 = bf16[2048,768]{1,0:T(8,128)(2,1)} fusion(bf16[64,768]{1,0:T(8,128)(2,1)S(1)} %add_convert_fusion.5, s32[2048]{0:T(1024)S(1)} %get-tuple-element.71), kind=kCustom, calls=%fused_computation.4.clone | custom fusion | bytes 6299648 | tf_op jit(solution)/shard_map/jit(_take)/gather | solution.py:21
  143.3 42.1 %all_to_all.215 = bf16[128,16,768]{2,1,0:T(8,128)(2,1)} all-to-all(bf16[128,16,768]{2,1,0:T(8,128)(2,1)S(1)} %bitcast.170), channel_id=1, replica_groups=mesh['dp'=2,'ep'=8] {'ep'}, dimensions={0} | all-to-all | bytes 6291456 | tf_op jit(solution)/shard_map/all_to_all | solution.py:23
  194.4 33.9 %all-to-all-done.5 = bf16[128,16,768]{2,1,0:T(8,128)(2,1)} async-done(((bf16[128,16,768]{2,1,0:T(8,128)(2,1)}), bf16[128,16,768]{2,1,0:T(8,128)(2,1)}, u32[]{:S(2)}, u32[]{:S(2)}) %all-to-all-start.5) | async-done | bytes 3145760 | tf_op jit(solution)/shard_map/all_to_all | solution.py:23
  276.7 9.1 %convolution_convert_fusion = bf16[16,128,768]{2,1,0:T(8,128)(2,1)} fusion(bf16[16,256,768]{2,1,0:T(8,128)(2,1)} %param.31, f32[16,128,256]{2,1,0:T(8,128)} %fusion.39, bf16[16,128,768]{2,1,0:T(8,128)(2,1)S(1)} %bitcast.140, bf16[16,768,256]{2,1,0:T(8,128)(2,1)} %param.30), kind=kOutput, calls=%fused_computation.34 | convolution fusion | flops 1615331328 | bytes 20971520 | tf_op jit(solution)/shard_map/erf,efd->erd/dot_general | solution.py:35
  291.0 17.9 %all-to-all-done.6 = bf16[16,128,768]{2,0,1:T(8,128)(2,1)} async-done(((bf16[16,128,768]{2,0,1:T(8,128)(2,1)}), bf16[16,128,768]{2,0,1:T(8,128)(2,1)}, u32[]{:S(2)}, u32[]{:S(2)}) %all-to-all-start.6) | async-done | bytes 3145760 | tf_op jit(solution)/shard_map/all_to_all | solution.py:27
  308.9 5.8 %all-to-all-start.3 = ((bf16[16,128,768]{2,0,1:T(8,128)(2,1)}), bf16[16,128,768]{2,0,1:T(8,128)(2,1)}, u32[]{:S(2)}, u32[]{:S(2)}) async-start(bf16[16,128,768]{2,0,1:T(8,128)(2,1)} %copy.118), calls=%async_computation.3 | async-start | bytes 6291456 | tf_op jit(solution)/shard_map/all_to_all | solution.py:27
  314.8 13.2 %gather_fusion.7 = f32[2048]{0:T(1024)S(1)} fusion(f32[512]{0:T(512)S(1)} %reshape.236, s32[2048]{0:T(1024)S(1)} %get-tuple-element.68), kind=kCustom, calls=%fused_computation.11.clone | custom fusion | bytes 24576 | tf_op jit(solution)/shard_map/jit(_take)/gather | solution.py:21
  369.5 9.4 %gather_fusion.8 = bf16[2048,768]{1,0:T(8,128)(2,1)} fusion(bf16[64,768]{1,0:T(8,128)(2,1)S(1)} %copy-done, s32[2048]{0:T(1024)S(1)} %get-tuple-element.69), kind=kCustom, calls=%fused_computation.6.clone | custom fusion | bytes 6299648 | tf_op jit(solution)/shard_map/jit(_take)/gather | solution.py:21
  378.9 9.4 %gather_fusion.9 = bf16[2048,768]{1,0:T(8,128)(2,1)} fusion(bf16[64,768]{1,0:T(8,128)(2,1)S(1)} %get-tuple-element.22, s32[2048]{0:T(1024)S(1)} %get-tuple-element.69), kind=kCustom, calls=%fused_computation.7.clone | custom fusion | bytes 6299648 | tf_op jit(solution)/shard_map/jit(_take)/gather | solution.py:21
  393.1 42.1 %all_to_all.216 = bf16[128,16,768]{2,1,0:T(8,128)(2,1)} all-to-all(bf16[128,16,768]{2,1,0:T(8,128)(2,1)} %bitcast.171), channel_id=1, replica_groups=mesh['dp'=2,'ep'=8] {'ep'}, dimensions={0} | all-to-all | bytes 6291456 | tf_op jit(solution)/shard_map/all_to_all | solution.py:23
  435.2 5.8 %all-to-all-start.9 = ((bf16[128,16,768]{2,1,0:T(8,128)(2,1)}), bf16[128,16,768]{2,1,0:T(8,128)(2,1)}, u32[]{:S(2)}, u32[]{:S(2)}) async-start(bf16[128,16,768]{2,1,0:T(8,128)(2,1)} %bitcast.169), calls=%async_computation.9 | async-start | bytes 6291456 | tf_op jit(solution)/shard_map/all_to_all | solution.py:23
  441.9 8.0 %fusion.46 = f32[16,768,256]{2,1,0:T(8,128)} fusion(bf16[16,128,768]{2,1,0:T(8,128)(2,1)S(1)} %bitcast.141, bf16[16,128,256]{2,1,0:T(8,128)(2,1)} %get-tuple-element.66), kind=kOutput, calls=%fused_computation.136 | convolution fusion | flops 805306368 | bytes 16777216 | tf_op jit(solution)/shard_map/erd,erf->edf/dot_general | solution.py:48
  449.9 6.7 %fusion.8 = f32[16,256,768]{2,1,0:T(8,128)} fusion(bf16[16,128,256]{2,1,0:T(8,128)(2,1)S(1)} %copy-done.13, bf16[16,128,768]{2,1,0:T(8,128)(2,1)S(1)} %bitcast.151, f32[16,128]{1,0:T(8,128)S(1)} %copy-done.17), kind=kOutput, calls=%fused_computation.32 | convolution fusion | flops 810024960 | bytes 16785408 | tf_op jit(solution)/shard_map/erf,erd->efd/dot_general | solution.py:43
  458.5 19.8 %all-to-all-done.9 = bf16[128,16,768]{2,1,0:T(8,128)(2,1)} async-done(((bf16[128,16,768]{2,1,0:T(8,128)(2,1)}), bf16[128,16,768]{2,1,0:T(8,128)(2,1)}, u32[]{:S(2)}, u32[]{:S(2)}) %all-to-all-start.9) | async-done | bytes 3145760 | tf_op jit(solution)/shard_map/all_to_all | solution.py:23
  521.6 7.9 %fusion.47 = f32[16,768,256]{2,1,0:T(8,128)} fusion(bf16[16,128,768]{2,1,0:T(8,128)(2,1)S(1)} %bitcast.142, bf16[16,128,256]{2,1,0:T(8,128)(2,1)} %get-tuple-element.67), kind=kOutput, calls=%fused_computation.137 | convolution fusion | flops 805306368 | bytes 16777216 | tf_op jit(solution)/shard_map/erd,erf->edf/dot_general | solution.py:49
  530.2 8.9 %fusion.45 = f32[16,768,256]{2,1,0:T(8,128)} fusion(bf16[16,128,768]{2,1,0:T(8,128)(2,1)} %bitcast.145, bf16[16,128,256]{2,1,0:T(8,128)(2,1)} %get-tuple-element.64), kind=kOutput, calls=%fused_computation.135 | convolution fusion | flops 805306368 | bytes 16777216 | tf_op jit(solution)/shard_map/erd,erf->edf/dot_general | solution.py:49
  539.2 6.6 %fusion.44 = f32[16,768,256]{2,1,0:T(8,128)} fusion(bf16[16,128,768]{2,1,0:T(8,128)(2,1)S(1)} %bitcast.148, bf16[16,128,256]{2,1,0:T(8,128)(2,1)S(1)} %copy-done.11), kind=kOutput, calls=%fused_computation.134 | convolution fusion | flops 805306368 | bytes 16777216 | tf_op jit(solution)/shard_map/erd,erf->edf/dot_general | solution.py:48
  545.8 6.7 %fusion.4 = f32[16,256,768]{2,1,0:T(8,128)} fusion(bf16[16,128,256]{2,1,0:T(8,128)(2,1)S(1)} %copy-done.15, bf16[16,128,768]{2,1,0:T(8,128)(2,1)S(1)} %bitcast.154, f32[16,128]{1,0:T(8,128)S(1)} %mul.154), kind=kOutput, calls=%fused_computation.30 | convolution fusion | flops 810024960 | bytes 16785408 | tf_op jit(solution)/shard_map/erf,erd->efd/dot_general | solution.py:43
  (227 shorter events, 211.3 us)
Async XLA Ops:
  13.4 44.3 %slice-start = ((s8[6291456]{0:T(1024)(128)(4,1)}), s8[4194304]{0:T(1024)(128)(4,1)S(1)}, s32[]{:S(2)}) async-start(s8[6291456]{0:T(1024)(128)(4,1)} %bitcast.143), calls=%async_computation.13 | async-start | bytes 8388608
  13.8 43.8 %slice-start.1 = ((s8[6291456]{0:T(1024)(128)(4,1)}), s8[2097152]{0:T(1024)(128)(4,1)S(1)}, s32[]{:S(2)}) async-start(s8[6291456]{0:T(1024)(128)(4,1)} %bitcast.143), calls=%async_computation.14 | async-start | bytes 4194304
  74.4 43.1 %all-to-all-start.1 = ((bf16[16,128,768]{2,0,1:T(8,128)(2,1)}), bf16[16,128,768]{2,0,1:T(8,128)(2,1)}, u32[]{:S(2)}, u32[]{:S(2)}) async-start(bf16[16,128,768]{2,0,1:T(8,128)(2,1)} %copy.109), calls=%async_computation.1 | async-start | bytes 6291456 | tf_op jit(solution)/shard_map/all_to_all | solution.py:27
  84.5 14.0 %copy-start.1 = (bf16[64,768]{1,0:T(8,128)(2,1)S(1)}, bf16[64,768]{1,0:T(8,128)(2,1)}, u32[]{:S(2)}) copy-start(bf16[64,768]{1,0:T(8,128)(2,1)} %param.25) | copy-start | bytes 294916
  107.9 19.9 %copy-start.25 = (pred[512]{0:T(512)(128)(4,1)}, pred[512]{0:T(512)(128)(4,1)S(1)}, u32[]{:S(2)}) copy-start(pred[512]{0:T(512)(128)(4,1)S(1)} %get-tuple-element.60) | copy-start | bytes 1540
  107.9 17.2 %copy-start.19 = (s32[1024]{0:T(1024)}, s32[1024]{0:T(1024)S(1)}, u32[]{:S(2)}) copy-start(s32[1024]{0:T(1024)S(1)} %pad_clamp_fusion.1) | copy-start | bytes 12292
  117.4 25.9 %all-to-all-start.4 = ((f32[8,1,256]{2,1,0:T(1,128)}), f32[8,1,256]{2,1,0:T(1,128)S(1)}, u32[]{:S(2)}, u32[]{:S(2)}) async-start(f32[8,1,256]{2,1,0:T(1,128)} %reshape.417), calls=%async_computation.4 | async-start | bytes 16384 | tf_op jit(solution)/shard_map/all_to_all | solution.py:23
  129.6 9.4 %copy-start.28 = (pred[2048]{0:T(1024)(128)(4,1)S(1)}, pred[2048]{0:T(1024)(128)(4,1)}, u32[]{:S(2)}) copy-start(pred[2048]{0:T(1024)(128)(4,1)} %compare_and_fusion) | copy-start | bytes 6148
  185.4 42.9 %all-to-all-start.5 = ((bf16[128,16,768]{2,1,0:T(8,128)(2,1)}), bf16[128,16,768]{2,1,0:T(8,128)(2,1)}, u32[]{:S(2)}, u32[]{:S(2)}) async-start(bf16[128,16,768]{2,1,0:T(8,128)(2,1)} %bitcast.27), calls=%async_computation.5 | async-start | bytes 6291456 | tf_op jit(solution)/shard_map/all_to_all | solution.py:23
  192.2 44.2 %copy-start.16 = (f32[16,128]{1,0:T(8,128)}, f32[16,128]{1,0:T(8,128)S(1)}, u32[]{:S(2)}) copy-start(f32[16,128]{1,0:T(8,128)S(1)} %mul.145) | copy-start | bytes 24580
  228.3 10.3 %slice-start.6 = ((s8[6291456]{0:T(1024)(128)(4,1)}), s8[4194304]{0:T(1024)(128)(4,1)S(1)}, s32[]{:S(2)}) async-start(s8[6291456]{0:T(1024)(128)(4,1)} %bitcast.172), calls=%async_computation.19 | async-start | bytes 8388608
  230.7 10.8 %copy-start.4 = (bf16[8,16,16,768]{3,2,0,1:T(8,128)(2,1)}, bf16[8,16,16,768]{3,2,0,1:T(8,128)(2,1)S(1)}, u32[]{:S(2)}) copy-start(bf16[8,16,16,768]{3,2,0,1:T(8,128)(2,1)S(1)} %copy.122) | copy-start | bytes 9437188
  247.3 18.8 %all-to-all-start.12 = ((f32[8,1,256]{2,1,0:T(1,128)}), f32[8,1,256]{2,1,0:T(1,128)S(1)}, u32[]{:S(2)}, u32[]{:S(2)}) async-start(f32[8,1,256]{2,1,0:T(1,128)} %reshape.423), calls=%async_computation.12 | async-start | bytes 16384 | tf_op jit(solution)/shard_map/all_to_all | solution.py:27
  266.7 42.2 %all-to-all-start.6 = ((bf16[16,128,768]{2,0,1:T(8,128)(2,1)}), bf16[16,128,768]{2,0,1:T(8,128)(2,1)}, u32[]{:S(2)}, u32[]{:S(2)}) async-start(bf16[16,128,768]{2,0,1:T(8,128)(2,1)} %copy.123), calls=%async_computation.6 | async-start | bytes 6291456 | tf_op jit(solution)/shard_map/all_to_all | solution.py:27
  308.9 43.1 %all-to-all-start.3 = ((bf16[16,128,768]{2,0,1:T(8,128)(2,1)}), bf16[16,128,768]{2,0,1:T(8,128)(2,1)}, u32[]{:S(2)}, u32[]{:S(2)}) async-start(bf16[16,128,768]{2,0,1:T(8,128)(2,1)} %copy.118), calls=%async_computation.3 | async-start | bytes 6291456 | tf_op jit(solution)/shard_map/all_to_all | solution.py:27
  352.0 41.2 %all-to-all-start.7 = ((f32[8,1,256]{2,1,0:T(1,128)}), f32[8,1,256]{2,1,0:T(1,128)S(1)}, u32[]{:S(2)}, u32[]{:S(2)}) async-start(f32[8,1,256]{2,1,0:T(1,128)} %reshape.419), calls=%async_computation.7 | async-start | bytes 16384 | tf_op jit(solution)/shard_map/all_to_all | solution.py:23
  378.9 9.4 %copy-start.23 = (pred[2048]{0:T(1024)(128)(4,1)S(1)}, pred[2048]{0:T(1024)(128)(4,1)}, u32[]{:S(2)}) copy-start(pred[2048]{0:T(1024)(128)(4,1)} %copy-done.22) | copy-start | bytes 6148
  435.2 43.2 %all-to-all-start.9 = ((bf16[128,16,768]{2,1,0:T(8,128)(2,1)}), bf16[128,16,768]{2,1,0:T(8,128)(2,1)}, u32[]{:S(2)}, u32[]{:S(2)}) async-start(bf16[128,16,768]{2,1,0:T(8,128)(2,1)} %bitcast.169), calls=%async_computation.9 | async-start | bytes 6291456 | tf_op jit(solution)/shard_map/all_to_all | solution.py:23
  478.3 12.3 %slice-start.8 = ((s8[6291456]{0:T(1024)(128)(4,1)}), s8[4194304]{0:T(1024)(128)(4,1)S(1)}, s32[]{:S(2)}) async-start(s8[6291456]{0:T(1024)(128)(4,1)} %bitcast.174), calls=%async_computation.21 | async-start | bytes 8388608
  480.7 14.4 %copy-start.6 = (bf16[8,16,16,768]{3,2,0,1:T(8,128)(2,1)}, bf16[8,16,16,768]{3,2,0,1:T(8,128)(2,1)S(1)}, u32[]{:S(2)}) copy-start(bf16[8,16,16,768]{3,2,0,1:T(8,128)(2,1)S(1)} %copy.128) | copy-start | bytes 9437188
  481.2 9.5 %slice-start.9 = ((s8[6291456]{0:T(1024)(128)(4,1)}), s8[2097152]{0:T(1024)(128)(4,1)S(1)}, s32[]{:S(2)}) async-start(s8[6291456]{0:T(1024)(128)(4,1)} %bitcast.174), calls=%async_computation.22 | async-start | bytes 4194304
  498.1 18.2 %all-to-all-start.11 = ((f32[8,1,256]{2,1,0:T(1,128)}), f32[8,1,256]{2,1,0:T(1,128)S(1)}, u32[]{:S(2)}, u32[]{:S(2)}) async-start(f32[8,1,256]{2,1,0:T(1,128)} %reshape.421), calls=%async_computation.11 | async-start | bytes 16384 | tf_op jit(solution)/shard_map/all_to_all | solution.py:27
  516.3 42.5 %all-to-all-start.10 = ((bf16[16,128,768]{2,0,1:T(8,128)(2,1)}), bf16[16,128,768]{2,0,1:T(8,128)(2,1)}, u32[]{:S(2)}, u32[]{:S(2)}) async-start(bf16[16,128,768]{2,0,1:T(8,128)(2,1)} %copy.129), calls=%async_computation.10 | async-start | bytes 6291456 | tf_op jit(solution)/shard_map/all_to_all | solution.py:27
  545.8 10.6 %copy-start.26 = (pred[512]{0:T(512)(128)(4,1)S(1)}, pred[512]{0:T(512)(128)(4,1)}, u32[]{:S(2)}) copy-start(pred[512]{0:T(512)(128)(4,1)} %copy-done.25) | copy-start | bytes 1540
  (27 other events, 164.9 us)
where the time goes:
time: 577 us; the launch traced here: 567 us
  local copies, waits for them, and re-layouts  157 us (27%)
  blocking collectives  128 us (22%)
  matrix products  118 us (20%)
  waiting for transfers between devices  86.4 us (15%)
  starting transfers between devices  51 us (9%)
  other arithmetic  25.4 us (4%)
    all_to_all x3, blocking collectives, send_rows(): return lax.all_to_all(send_buf, 'ep', 0, 1, tiled=True)  128 us
    gather x7, local copies, waits for them, and re-layouts, send_rows(): send_buf = jnp.take(rows, index, axis=0, mode='fill', fill_value=0)  71.6 us
    all_to_all x4, waiting for transfers between devices, send_rows(): return lax.all_to_all(send_buf, 'ep', 0, 1, tiled=True)  53.7 us
    all_to_all x6, waiting for transfers between devices, send_back(): back_rows = lax.all_to_all(rows, 'ep', 1, 0, tiled=True)  32.8 us
    all_to_all x6, starting transfers between devices, send_back(): back_rows = lax.all_to_all(rows, 'ep', 1, 0, tiled=True)  30.7 us
    dot_general x4, matrix products, expert_forward(): jnp.einsum('erf,efd->erd', hidden, w_down, preferred_element_type=jnp.flo...  20.3 us
    all_to_all x4, starting transfers between devices, send_rows(): return lax.all_to_all(send_buf, 'ep', 0, 1, tiled=True)  20.3 us
    dot_general x4, matrix products, expert_forward(): jnp.einsum('erd,edf->erf', u_rows, w_gate, preferred_element_type=jnp.flo...  18.5 us
  transfers between devices with their start and end apart: 10, of which 6 were waited for; matrix products, arithmetic and copies ran while one was open for 39% of the time, Pallas kernels for 0%

commit v1 on v0

v1 whole, which is shorter than its diff:
```python
import functools

import jax
import jax.numpy as jnp
from jax import lax
from jax.experimental import pallas as pl
from jax.experimental.pallas import tpu as pltpu
from jax.sharding import PartitionSpec as P

BF16 = jnp.bfloat16
F32 = jnp.float32
MESH = pl.DeviceIdType.MESH
LANES = 128
CAP_FACTOR = 4
BF16_MAX = 3.3895313892515355e38
VMEM_LIMIT = 60 * 1024 * 1024
VMEM = pl.BlockSpec(memory_space=pltpu.VMEM)
ANY = pl.BlockSpec(memory_space=pl.ANY)


def mm(lhs, rhs):
    return jnp.dot(lhs, rhs, preferred_element_type=F32)


def mm_tn(lhs, rhs):
    return lax.dot_general(lhs, rhs, (((0,), (0,)), ((), ())), preferred_element_type=F32)


def mm_nt(lhs, rhs):
    return lax.dot_general(lhs, rhs, (((1,), (1,)), ((), ())), preferred_element_type=F32)


def iota(shape, dim):
    return lax.broadcasted_iota(jnp.int32, shape, dim)


def routing_maps(me, meta, layer, s_ref, g_ref, rel_ref, top_k, local):
    n_dev = meta.shape[0]
    base = (me * local).astype(F32)
    row = 2 * layer * top_k
    rel_ref[...] = meta[:, row : row + top_k, :] - base
    hit = [jnp.zeros((n_dev, LANES), F32) for _ in range(local)]
    gate = [jnp.zeros((n_dev, LANES), F32) for _ in range(local)]
    for j in range(top_k):
        rel_j = meta[:, row + j, :] - base
        gate_j = meta[:, row + top_k + j, :]
        for e in range(local):
            match = rel_j == float(e)
            hit[e] = jnp.where(match, 1.0, hit[e])
            gate[e] = jnp.where(match, gate_j, gate[e])
    hit = jnp.concatenate(hit, axis=0)
    earlier = (iota((LANES, LANES), 0) < iota((LANES, LANES), 1)).astype(F32).astype(BF16)
    slot = jnp.where(hit > 0.0, mm(hit.astype(BF16), earlier), -1.0)
    s_ref[...] = slot.reshape(local, n_dev, LANES)
    for e in range(local):
        g_ref[e] = gate[e]


def expert_rows(s_map, d, rows, cap):
    pairs, lanes = s_map.shape
    local, n_dev, tok = pairs // 8, 8, rows.shape[0]
    pick = (iota((local * cap, pairs), 1) == iota((local * cap, pairs), 0) // cap * n_dev + d)
    slot = mm(pick.astype(F32).astype(BF16), s_map.astype(BF16))
    onehot = jnp.where(slot == (iota((local * cap, lanes), 0) % cap).astype(F32), 1.0, 0.0).astype(BF16)
    return mm(onehot[:, :tok], rows).astype(BF16)


def limbs(gate):
    hi = jnp.minimum(gate, BF16_MAX).astype(BF16)
    rest = gate - hi.astype(F32)
    mid = rest.astype(BF16)
    return hi, mid, (rest - mid.astype(F32)).astype(BF16)


def scatter_lhs(s_map, g_map, tok):
    stack = [s_map.T[:tok].astype(BF16)]
    if g_map is not None:
        stack += [limb.T[:tok].astype(BF16) for limb in (x.astype(F32) for x in limbs(g_map))]
    return jnp.concatenate(stack, axis=0)


def token_sums(stack, d, out_rows, tok, cap):
    pairs = stack.shape[1]
    n_rows = out_rows.shape[0]
    spread = iota((pairs, n_rows), 0) == iota((pairs, n_rows), 1) // cap * 8 + d
    maps = mm(stack, spread.astype(F32).astype(BF16))
    match = maps[:tok] == (iota((tok, n_rows), 1) % cap).astype(F32)
    if stack.shape[0] == tok:
        return mm(jnp.where(match, 1.0, 0.0).astype(BF16), out_rows)
    terms = (stack.shape[0] - tok) // tok
    lhs = [jnp.where(match, maps[(i + 1) * tok : (i + 2) * tok], 0.0).astype(BF16) for i in range(terms)]
    sums = mm(jnp.concatenate(lhs, axis=0), out_rows)
    total = sums[:tok]
    for i in range(1, terms):
        total = total + sums[i * tok : (i + 1) * tok]
    return total


def forward_rows(u, w_gate, w_up, w_down):
    pre_gate = mm(u, w_gate)
    pre_up = mm(u, w_up)
    sig = jax.nn.sigmoid(pre_gate)
    act = pre_gate * sig
    hidden = (act * pre_up).astype(BF16)
    return pre_gate, pre_up, sig, act, hidden, mm(hidden, w_down).astype(BF16)


class Links:
    def __init__(self, n_dev, send_sems, recv_sems):
        me = lax.axis_index("ep")
        self.n = n_dev
        self.me = me
        self.core = lax.rem(me, 2)
        self.partner = me + 1 - 2 * self.core
        self.right = lax.rem(me + 2, n_dev)
        self.left = lax.rem(me + n_dev - 2, n_dev)
        self.opp = lax.rem(me + 4, n_dev)
        self.send_sems, self.recv_sems = send_sems, recv_sems
        self.used = 0
        self.started = []

    def greet(self):
        barrier = pltpu.get_barrier_semaphore()
        for peer in (self.partner, self.left, self.right):
            pl.semaphore_signal(barrier, inc=1, device_id={"ep": peer}, device_id_type=MESH)
        pl.semaphore_wait(barrier, 3)

    def copy(self, src, dst, peer):
        slot = self.used
        self.used += 1
        rdma = pltpu.make_async_remote_copy(
            src_ref=src, dst_ref=dst, send_sem=self.send_sems.at[slot], recv_sem=self.recv_sems.at[slot],
            device_id={"ep": peer}, device_id_type=MESH)
        rdma.start()
        self.started.append(rdma)
        return rdma

    def drain(self):
        for rdma in self.started:
            rdma.wait_send()


class Gather:
    COPIES = 9

    def __init__(self, links, own, full):
        k, self.k, self.full = links, links, full
        self.half = own.shape[0] // 2
        self.to_right = k.copy(own, full.at[k.me], k.right)
        self.to_left = k.copy(own, full.at[k.me], k.left)
        self.to_partner = k.copy(own, full.at[k.me], k.partner)

    def pass_on(self):
        k, full, half = self.k, self.full, self.half
        self.to_right.wait_recv()
        self.far_a = k.copy(full.at[k.left, pl.ds(0, half)], full.at[k.left, pl.ds(0, half)], k.right)
        self.side_a = k.copy(full.at[k.left], full.at[k.left], k.partner)
        self.to_left.wait_recv()
        self.far_b = k.copy(full.at[k.right, pl.ds(half, half)], full.at[k.right, pl.ds(half, half)], k.left)
        self.side_b = k.copy(full.at[k.right], full.at[k.right], k.partner)

    def pass_far(self):
        k, full, half = self.k, self.full, self.half
        self.far_a.wait_recv()
        self.last_a = k.copy(full.at[k.opp, pl.ds(0, half)], full.at[k.opp, pl.ds(0, half)], k.partner)
        self.far_b.wait_recv()
        self.last_b = k.copy(full.at[k.opp, pl.ds(half, half)], full.at[k.opp, pl.ds(half, half)], k.partner)

    def wait_partner(self):
        self.to_partner.wait_recv()

    def wait_sides(self):
        self.side_a.wait_recv()
        self.side_b.wait_recv()

    def wait_last(self):
        self.last_a.wait_recv()
        self.last_b.wait_recv()

    def finish(self):
        self.wait_partner()
        self.wait_sides()
        self.wait_last()


class Reduce:
    COPIES = 10

    @staticmethod
    def scratch(rows, width):
        return [pltpu.VMEM((4, rows, width), F32), pltpu.VMEM((4, rows, width), F32), pltpu.VMEM((3, rows, width), F32)]

    def __init__(self, links, part, bufs, split=True):
        self.k, self.part = links, part
        self.near, self.mine, self.got = bufs
        rows = part.shape[1]
        self.rows = rows
        self.half = rows // 2 if split else rows
        self.side = {}

    def block(self, hop, core):
        k = self.k
        return lax.rem(k.me - k.core + 2 * hop, k.n) + core

    def start_side(self, hop):
        k = self.k
        self.side[hop] = k.copy(self.part.at[self.block(hop, 1 - k.core)], self.near.at[hop], k.partner)

    def start(self):
        for hop in (2, 1, 3, 0):
            self.start_side(hop)

    def add(self, hop, lo, hi, extra=None):
        own = self.part[self.block(hop, self.k.core), lo:hi, :]
        total = own + self.near[hop, lo:hi, :]
        if extra is not None:
            total = total + extra
        self.mine[hop, lo:hi, :] = total

    def far(self):
        k, half, rows = self.k, self.half, self.rows
        self.side[2].wait_recv()
        self.add(2, 0, rows)
        a = pl.ds(0, half)
        self.far_a = k.copy(self.mine.at[2, a], self.got.at[2, a], k.right)
        if half < rows:
            b = pl.ds(half, rows - half)
            self.far_b = k.copy(self.mine.at[2, b], self.got.at[2, b], k.left)

    def near_sends(self):
        k, half, rows = self.k, self.half, self.rows
        self.side[1].wait_recv()
        if half < rows:
            b = pl.ds(half, rows - half)
            self.add(1, half, rows)
            self.right_b = k.copy(self.mine.at[1, b], self.got.at[0, b], k.right)
        self.side[3].wait_recv()
        self.add(3, 0, half)
        a = pl.ds(0, half)
        self.left_a = k.copy(self.mine.at[3, a], self.got.at[1, a], k.left)

    def relay(self):
        k, half, rows = self.k, self.half, self.rows
        a = pl.ds(0, half)
        self.far_a.wait_recv()
        self.add(1, 0, half, self.got[2, :half, :])
        self.right_a = k.copy(self.mine.at[1, a], self.got.at[0, a], k.right)
        if half < rows:
            b = pl.ds(half, rows - half)
            self.far_b.wait_recv()
            self.add(3, half, rows, self.got[2, half:, :])
            self.left_b = k.copy(self.mine.at[3, b], self.got.at[1, b], k.left)

    def result(self):
        half, rows = self.half, self.rows
        self.side[0].wait_recv()
        if half < rows:
            self.right_b.wait_recv()
        self.left_a.wait_recv()
        self.right_a.wait_recv()
        if half < rows:
            self.left_b.wait_recv()
        return self.part[self.k.me] + self.near[0] + self.got[0] + self.got[1]


def load_weights(pairs, sems, local):
    def start(e, carry):
        for i, (src, dst) in enumerate(pairs):
            pltpu.make_async_copy(src.at[e], dst.at[e], sems.at[i, e]).start()
        return carry
    lax.fori_loop(0, local, start, 0)


def wait_weights(pairs, sems, e):
    for i, (src, dst) in enumerate(pairs):
        pltpu.make_async_copy(src.at[e], dst.at[e], sems.at[i, e]).wait()


def forward_experts(pairs, sems, u_ref, o_ref, cap):
    n_dev, local, _, width = u_ref.shape

    def step(e, carry):
        wait_weights(pairs, sems, e)
        u = u_ref[:, e].reshape(n_dev * cap, width)
        out = forward_rows(u, *(dst[e] for _, dst in pairs))[-1]
        o_ref[:, e] = out.reshape(n_dev, cap, width)
        return carry
    lax.fori_loop(0, local, step, 0)


def first_kernel(dims, x_ref, dy_ref, meta_ref, w1, w3, w2,
                 mid_all, dy_all, mid_own, sa, ga, rela, sb, gb, relb,
                 x_all, y_all, m_all, meta_all, u_ref, o_ref, part, near, mine, got, mid_buf, w1_v, w3_v, w2_v,
                 w_sems, send_sems, recv_sems):
    n_dev, tok, width, local, cap, top_k = dims
    pairs = ((w1, w1_v), (w3, w3_v), (w2, w2_v))
    load_weights(pairs, w_sems, local)
    links = Links(n_dev, send_sems, recv_sems)
    me = links.me
    links.greet()
    meta_g = Gather(links, meta_ref, meta_all)
    x_g = Gather(links, x_ref, x_all)
    y_g = Gather(links, dy_ref, y_all)
    meta_all[me] = meta_ref[...]
    x_all[me] = x_ref[...]
    y_all[me] = dy_ref[...]
    meta_g.pass_on()
    x_g.pass_on()
    meta_g.pass_far()
    x_g.pass_far()
    meta_g.finish()
    meta = meta_all[...]
    routing_maps(me, meta, 0, sa, ga, rela, top_k, local)
    routing_maps(me, meta, 1, sb, gb, relb, top_k, local)
    s_map = sa[...].reshape(local * n_dev, LANES)

    def rows_of(d):
        u_ref[d] = expert_rows(s_map, d, x_all[d], cap).reshape(local, cap, width)

    rows_of(me)
    rows_of(links.left)
    rows_of(links.right)
    rows_of(links.opp)
    y_g.pass_on()
    x_g.wait_partner()
    rows_of(links.partner)
    x_g.wait_sides()
    side = 1 - 2 * links.core
    rows_of(links.left + side)
    rows_of(links.right + side)
    x_g.wait_last()
    rows_of(links.opp + side)
    forward_experts(pairs, w_sems, u_ref, o_ref, cap)
    y_g.pass_far()
    stack = scatter_lhs(s_map, ga[...].reshape(local * n_dev, LANES), tok)
    red = Reduce(links, part, (near, mine, got))

    def sums_of(d):
        part[d] = token_sums(stack, d, o_ref[d].reshape(local * cap, width), tok, cap)

    for hop in (2, 1, 3, 0):
        sums_of(red.block(hop, 1 - links.core))
        red.start_side(hop)
    for hop in (2, 1, 3, 0):
        sums_of(red.block(hop, links.core))
    red.far()
    red.near_sends()
    red.relay()
    x_mid = (x_ref[...].astype(F32) + red.result()).astype(BF16)
    mid_buf[...] = x_mid
    mid_own[...] = x_mid
    m_all[me] = x_mid
    m_g = Gather(links, mid_buf, m_all)
    m_g.pass_on()
    m_g.pass_far()
    y_g.finish()
    dy_all[...] = y_all[...]
    m_g.finish()
    mid_all[...] = m_all[...]
    links.drain()


def backward_kernel(dims, x_all, dy_all, s_ref, g_ref, rel_ref, w1, w3, w2,
                    dw1, dw3, dw2, part, dgate, u_ref, y_ref, du_ref, dg_ref):
    n_dev, tok, width, local, cap, top_k = dims
    e = pl.program_id(0)
    n_rows = n_dev * cap

    @pl.when(e == 0)
    def _():
        s_map = s_ref[...].reshape(local * n_dev, LANES)

        def rows_of(d, carry):
            u_ref[d] = expert_rows(s_map, d, x_all[d], cap).reshape(local, cap, width)
            y_ref[d] = expert_rows(s_map, d, dy_all[d], cap).reshape(local, cap, width)
            return carry
        lax.fori_loop(0, n_dev, rows_of, 0)

    u = u_ref[:, e].reshape(n_rows, width)
    dy = y_ref[:, e].reshape(n_rows, width).astype(F32)
    w_gate, w_up, w_down = w1[0], w3[0], w2[0]
    pre_gate, pre_up, sig, act, hidden, out = forward_rows(u, w_gate, w_up, w_down)
    slot = s_ref[e][:, None, :] == iota((n_dev, cap, LANES), 1).astype(F32)
    gate_row = jnp.sum(jnp.where(slot, g_ref[e][:, None, :], 0.0), axis=2, keepdims=True).reshape(n_rows, 1)
    dg_row = jnp.sum(dy * out.astype(F32), axis=1, keepdims=True).reshape(n_dev, cap, 1)
    dg_ref[e] = jnp.sum(jnp.where(slot, dg_row, 0.0), axis=1)
    q = (gate_row * dy).astype(BF16)
    dw2[0] = mm_tn(hidden, q)
    d_hidden = mm_nt(q, w_down)
    d_gate = (d_hidden * pre_up * sig * (1.0 + pre_gate * (1.0 - sig))).astype(BF16)
    d_up = (d_hidden * act).astype(BF16)
    dw1[0] = mm_tn(u, d_gate)
    dw3[0] = mm_tn(u, d_up)
    du = (mm_nt(d_gate, w_gate) + mm_nt(d_up, w_up)).astype(BF16)
    du_ref[:, e] = du.reshape(n_dev, cap, width)

    @pl.when(e == local - 1)
    def _():
        s_map = s_ref[...].reshape(local * n_dev, LANES)
        stack = scatter_lhs(s_map, None, tok)

        def sums_of(d, carry):
            part[d] = token_sums(stack, d, du_ref[d].reshape(local * cap, width), tok, cap)
            return carry
        lax.fori_loop(0, n_dev, sums_of, 0)
        for d in range(n_dev):
            total = jnp.zeros((top_k, LANES), F32)
            for i in range(local):
                total = jnp.where(rel_ref[d] == float(i), dg_ref[i, d : d + 1, :], total)
            dgate[d] = total


def middle_kernel(dims, part_b, dg_part, dy_ref, x_ref, mid_all, sb, gb, w1, w3, w2,
                  dmid_all, x_again, dmid_own, dgate, part_x,
                  d_all, x_all, u_ref, o_ref, near, mine, got, dg_near, dg_mine, dg_got, d_buf, w1_v, w3_v, w2_v,
                  w_sems, send_sems, recv_sems):
    n_dev, tok, width, local, cap, top_k = dims
    pairs = ((w1, w1_v), (w3, w3_v), (w2, w2_v))
    load_weights(pairs, w_sems, local)
    links = Links(n_dev, send_sems, recv_sems)
    me = links.me
    links.greet()
    red = Reduce(links, part_b, (near, mine, got))
    dg = Reduce(links, dg_part, (dg_near, dg_mine, dg_got), split=False)
    red.start()
    dg.start()
    x_g = Gather(links, x_ref, x_all)
    x_all[me] = x_ref[...]
    red.far()
    red.near_sends()
    red.relay()
    dg.far()
    dg.near_sends()
    x_g.pass_on()
    dx = (dy_ref[...].astype(F32) + red.result()).astype(BF16)
    d_buf[...] = dx
    dmid_own[...] = dx
    d_all[me] = dx
    d_g = Gather(links, d_buf, d_all)
    dg.relay()
    x_g.pass_far()
    d_g.pass_on()
    d_g.pass_far()

    s_map = sb[...].reshape(local * n_dev, LANES)

    def rows_of(d, carry):
        u_ref[d] = expert_rows(s_map, d, mid_all[d], cap).reshape(local, cap, width)
        return carry
    lax.fori_loop(0, n_dev, rows_of, 0)
    forward_experts(pairs, w_sems, u_ref, o_ref, cap)
    stack = scatter_lhs(s_map, gb[...].reshape(local * n_dev, LANES), tok)

    def sums_of(d, carry):
        part_x[d] = token_sums(stack, d, o_ref[d].reshape(local * cap, width), tok, cap)
        return carry
    lax.fori_loop(0, n_dev, sums_of, 0)
    dgate[...] = dg.result()
    x_g.finish()
    x_again[...] = x_all[...]
    d_g.finish()
    dmid_all[...] = d_all[...]
    links.drain()


def last_kernel(dims, part_a, dg_part, part_x, dmid_ref, mid_ref, dx_out, dgate, x_out,
                near, mine, got, dg_near, dg_mine, dg_got, x_near, x_mine, x_got, send_sems, recv_sems):
    links = Links(dims[0], send_sems, recv_sems)
    links.greet()
    reds = (Reduce(links, part_a, (near, mine, got)), Reduce(links, part_x, (x_near, x_mine, x_got)),
            Reduce(links, dg_part, (dg_near, dg_mine, dg_got), split=False))
    for red in reds:
        red.start()
    for red in reds:
        red.far()
        red.near_sends()
    for red in reds:
        red.relay()
    dx_out[...] = (dmid_ref[...].astype(F32) + reds[0].result()).astype(BF16)
    x_out[...] = (mid_ref[...].astype(F32) + reds[1].result()).astype(BF16)
    dgate[...] = reds[2].result()
    links.drain()


def remote_params(ident):
    return pltpu.CompilerParams(collective_id=ident, has_side_effects=True, vmem_limit_bytes=VMEM_LIMIT)


def dma_sems(count):
    return [pltpu.SemaphoreType.DMA((count,)), pltpu.SemaphoreType.DMA((count,))]


def solution(mesh):
    n_dev = mesh.shape["ep"]
    tok_spec = P(("dp", "ep"))
    w_spec = P("ep")

    def device_program(x_in, idx_a, idx_b, gate_a, gate_b, dy_out, w1_a, w3_a, w2_a, w1_b, w3_b, w2_b):
        tok, top_k = idx_a.shape
        width = x_in.shape[1]
        local, _, inner = w1_a.shape
        cap = CAP_FACTOR * tok * top_k // (local * n_dev)
        dims = (n_dev, tok, width, local, cap, top_k)
        sds = jax.ShapeDtypeStruct
        rows_all = sds((n_dev, tok, width), BF16)
        part_all = sds((n_dev, tok, width), F32)
        dg_all = sds((n_dev, top_k, LANES), F32)
        map_s = sds((local, n_dev, LANES), F32)
        own = sds((tok, width), BF16)

        def lanes(rows, fill):
            return jnp.pad(rows.T.astype(F32), ((0, 0), (0, LANES - tok)), constant_values=fill)

        meta = jnp.concatenate([lanes(idx_a, -1.0), lanes(gate_a, 0.0), lanes(idx_b, -1.0), lanes(gate_b, 0.0)])
        weights_v = [pltpu.VMEM((local, width, inner), BF16)] * 2 + [pltpu.VMEM((local, inner, width), BF16)]
        w_sems = pltpu.SemaphoreType.DMA((3, local))
        rows_v = pltpu.VMEM((n_dev, tok, width), BF16)
        expert_v = pltpu.VMEM((n_dev, local, cap, width), BF16)

        count = 4 * Gather.COPIES + Reduce.COPIES
        mid_all, dy_all, mid_own, sa, ga, rela, sb, gb, relb = pl.pallas_call(
            functools.partial(first_kernel, dims),
            out_shape=(rows_all, rows_all, own, map_s, map_s, dg_all, map_s, map_s, dg_all),
            in_specs=[VMEM] * 3 + [ANY] * 3,
            out_specs=[VMEM] * 9,
            scratch_shapes=[rows_v, rows_v, rows_v, pltpu.VMEM((n_dev, 4 * top_k, LANES), F32), expert_v, expert_v,
                            pltpu.VMEM((n_dev, tok, width), F32), *Reduce.scratch(tok, width),
                            pltpu.VMEM((tok, width), BF16), *weights_v, w_sems, *dma_sems(count)],
            compiler_params=remote_params(0), name="first",
        )(x_in, dy_out, meta, w1_a, w3_a, w2_a)

        def backward(x_all, d_all, s, g, rel, w1, w3, w2):
            whole = pl.BlockSpec(memory_space=pltpu.VMEM)
            w_in = pl.BlockSpec((1, width, inner), lambda e: (e, 0, 0))
            w_out = pl.BlockSpec((1, inner, width), lambda e: (e, 0, 0))
            return pl.pallas_call(
                functools.partial(backward_kernel, dims),
                grid=(local,),
                out_shape=(sds((local, width, inner), F32), sds((local, width, inner), F32),
                           sds((local, inner, width), F32), part_all, dg_all),
                in_specs=[whole] * 5 + [w_in, w_in, w_out],
                out_specs=[w_in, w_in, w_out, whole, whole],
                scratch_shapes=[expert_v, expert_v, expert_v, pltpu.VMEM((local, n_dev, LANES), F32)],
                compiler_params=pltpu.CompilerParams(dimension_semantics=("arbitrary",), vmem_limit_bytes=VMEM_LIMIT),
                name="backward",
            )(x_all, d_all, s, g, rel, w1, w3, w2)

        *grads_b, part_b, dg_b = backward(mid_all, dy_all, sb, gb, relb, w1_b, w3_b, w2_b)

        count = 2 * Gather.COPIES + 2 * Reduce.COPIES
        dmid_all, x_again, dmid_own, dgate_b, part_x = pl.pallas_call(
            functools.partial(middle_kernel, dims),
            out_shape=(rows_all, rows_all, own, sds((top_k, LANES), F32), part_all),
            in_specs=[VMEM] * 7 + [ANY] * 3,
            out_specs=[VMEM] * 5,
            scratch_shapes=[rows_v, rows_v, expert_v, expert_v, *Reduce.scratch(tok, width),
                            *Reduce.scratch(top_k, LANES), pltpu.VMEM((tok, width), BF16), *weights_v, w_sems,
                            *dma_sems(count)],
            compiler_params=remote_params(1), name="middle",
        )(part_b, dg_b, dy_out, x_in, mid_all, sb, gb, w1_b, w3_b, w2_b)

        *grads_a, part_a, dg_a = backward(x_again, dmid_all, sa, ga, rela, w1_a, w3_a, w2_a)

        count = 3 * Reduce.COPIES
        dx_in, dgate_a, x_out = pl.pallas_call(
            functools.partial(last_kernel, dims),
            out_shape=(own, sds((top_k, LANES), F32), own),
            in_specs=[VMEM] * 5,
            out_specs=[VMEM] * 3,
            scratch_shapes=[*Reduce.scratch(tok, width), *Reduce.scratch(top_k, LANES), *Reduce.scratch(tok, width),
                            *dma_sems(count)],
            compiler_params=remote_params(2), name="last",
        )(part_a, dg_a, part_x, dmid_own, mid_own)
        return (x_out, dx_in, *grads_a, *grads_b, dgate_a[:, :tok].T, dgate_b[:, :tok].T)

    return jax.shard_map(device_program, mesh=mesh, in_specs=(tok_spec,) * 6 + (w_spec,) * 6, out_specs=(tok_spec,) * 10, check_vma=False)
```

time: 577 us -> 193 us (0.33); the launches traced: 567 us -> 191 us
  Pallas kernels: 0 us -> 183 us
  local copies, waits for them, and re-layouts: 157 us -> 5.61 us
  blocking collectives: 128 us -> 0 us
  matrix products: 118 us -> 0 us
  waiting for transfers between devices: 86.4 us -> 0 us
  starting transfers between devices: 51 us -> 0 us
  other arithmetic: 25.4 us -> 2.02 us
    pallas_call x0 -> x5, Pallas kernels: none -> 183 us  [the longest x2 74.7 us: backward(): pl.pallas_call(functools.partial(backward_kernel, dims), grid=(local,), o...]
    all_to_all x3 -> x0, blocking collectives: 128 us -> none  [send_rows(): return lax.all_to_all(send_buf, 'ep', 0, 1, tiled=True)]
    dot_general x22 -> x0, matrix products: 118 us -> none  [the longest x4 20.3 us: expert_forward(): jnp.einsum('erf,efd->erd', hidden, w_down, preferred_element_type=jnp.flo...]
    gather x13 -> x0, local copies, waits for them, and re-layouts: 94.2 us -> none  [the longest x7 71.6 us: send_rows(): send_buf = jnp.take(rows, index, axis=0, mode='fill', fill_value=0)]
    all_to_all x10 -> x0, waiting for transfers between devices: 86.4 us -> none  [the longest x4 53.7 us: send_rows(): return lax.all_to_all(send_buf, 'ep', 0, 1, tiled=True)]
    all_to_all x10 -> x0, starting transfers between devices: 51 us -> none  [the longest x6 30.7 us: send_back(): back_rows = lax.all_to_all(rows, 'ep', 1, 0, tiled=True)]
    all_to_all x20 -> x0, local copies, waits for them, and re-layouts: 28.4 us -> none  [the longest x10 18.4 us: send_back(): back_rows = lax.all_to_all(rows, 'ep', 1, 0, tiled=True)]
    convert_element_type x4 -> x0, local copies, waits for them, and re-layouts: 17.4 us -> none  [the longest x2 10.6 us: expert_forward(): jnp.einsum('erf,efd->erd', hidden, w_down, preferred_element_type=jnp.flo...]
  transfers between devices with their start and end apart: 10 -> 0, of which waited for: 6 -> 0; matrix products, arithmetic and copies ran while one was open for 39% -> 0% of each run, Pallas kernels for 0% -> 0%
where the time goes in v1:
time: 193 us; the launch traced here: 191 us
  Pallas kernels  183 us (95%)
  local copies, waits for them, and re-layouts  5.61 us (3%)
  other arithmetic  2.02 us (1%)
    pallas_call x2, Pallas kernels, backward(): pl.pallas_call(functools.partial(backward_kernel, dims), grid=(local,), o...  74.7 us
    pallas_call x1, Pallas kernels, device_program(): pl.pallas_call(functools.partial(first_kernel, dims), out_shape=(rows_all...  47.6 us
    pallas_call x1, Pallas kernels, device_program(): pl.pallas_call(functools.partial(middle_kernel, dims), out_shape=(rows_al...  37 us
    pallas_call x1, Pallas kernels, device_program(): pl.pallas_call(functools.partial(last_kernel, dims), out_shape=(own, sds(...  23.2 us

profile of v1, /device:TPU:113, one launch (start us, length us, event | category | flops | bytes accessed | tf_op | source)
XLA Modules:
  0.0 190.9 jit_solution(16525829802933638915)
XLA Ops:
  0.6 0.7 convert_bitcast_fusion
  1.3 1.3 select_maximum_fusion.meta_ref
  2.7 47.6 %first.1 = (bf16[8,64,768]{2,1,0:T(8,128)(2,1)}, bf16[8,64,768]{2,1,0:T(8,128)(2,1)}, bf16[64,768]{1,0:T(8,128)(2,1)}, f32[16,8,128]{2,1,0:T(8,128)}, f32[16,8,1...) custom-call(bf16[64,768]{1,0:T(8,128)(2,1)} %x_ref.3, ...), custom_call_target="tpu_custom_call" | custom-call | tf_op jit(solution)/shard_map/first/pallas_call | solution.py:521
  50.3 37.4 %backward.2 = (f32[16,768,256]{2,1,0:T(8,128)}, f32[16,768,256]{2,1,0:T(8,128)}, f32[16,256,768]{2,1,0:T(8,128)}, f32[8,64,768]{2,1,0:T(8,128)}, f32[8,8,128]{2,1,0:T(8,128)}) custom-call(bf16[8,64,768]{2,1,0:T(8,128)(2,1)} %get-tuple-element.37.x_all.mid_all, bf16[8,64,768]{2,1,0:T(8,128)(2,1)} %get-tuple-element.38.dy_all, ...), custom_call_target="tpu_custom_call" | custom-call | tf_op jit(solution)/shard_map/backward/pallas_call | solution.py:536
  87.6 37.0 %middle.1 = (bf16[8,64,768]{2,1,0:T(8,128)(2,1)}, bf16[8,64,768]{2,1,0:T(8,128)(2,1)}, bf16[64,768]{1,0:T(8,128)(2,1)}, f32[8,128]{1,0:T(8,128)}, f32[8,64,768]{2,1,0:T(8,128)}) custom-call(f32[8,64,768]{2,1,0:T(8,128)} %get-tuple-element.42.part_b, f32[8,8,128]{2,1,0:T(8,128)} %get-tuple-element.43.dg_part, bf16[64,768]{1,0:T(8,128)(2,1)} %dy_ref.3, ...), custom_call_target="tpu_custom_call" | custom-call | tf_op jit(solution)/shard_map/middle/pallas_call | solution.py:551
  124.7 1.3 slice_bitcast_fusion
  125.9 37.3 %backward.3 = (f32[16,768,256]{2,1,0:T(8,128)}, f32[16,768,256]{2,1,0:T(8,128)}, f32[16,256,768]{2,1,0:T(8,128)}, f32[8,64,768]{2,1,0:T(8,128)}, f32[8,8,128]{2,1,0:T(8,128)}) custom-call(bf16[8,64,768]{2,1,0:T(8,128)(2,1)} %get-tuple-element.44.x_all, bf16[8,64,768]{2,1,0:T(8,128)(2,1)} %get-tuple-element.45.dy_all, f32[16,8,128]{2,1,0:T(8,128)} %get-tuple-element.46.s_ref, ...), custom_call_target="tpu_custom_call" | custom-call | tf_op jit(solution)/shard_map/backward/pallas_call | solution.py:536
  163.3 23.2 %last.1 = (bf16[64,768]{1,0:T(8,128)(2,1)}, f32[8,128]{1,0:T(8,128)}, bf16[64,768]{1,0:T(8,128)(2,1)}) custom-call(f32[8,64,768]{2,1,0:T(8,128)} %get-tuple-element.49.part_a, f32[8,8,128]{2,1,0:T(8,128)} %get-tuple-element.50.dg_part, f32[8,64,768]{2,1,0:T(8,128)} %get-tuple-element.51.part_x, bf16[64,768]{1,0:T(8,128)(2,1)} %get-tuple-element.52.dmid_ref, ...), custom_call_target="tpu_custom_call" | custom-call | tf_op jit(solution)/shard_map/last/pallas_call | solution.py:565
  186.5 1.3 slice_bitcast_fusion.1
  187.8 1.5 copy.24
  189.3 1.5 copy.25

commit v2 on v1

--- a/solution.py
+++ b/solution.py
@@ -13,6 +13,7 @@
 LANES = 128
 CAP_FACTOR = 4
 BF16_MAX = 3.3895313892515355e38
+GROUPED = 2
 VMEM_LIMIT = 60 * 1024 * 1024
 VMEM = pl.BlockSpec(memory_space=pltpu.VMEM)
 ANY = pl.BlockSpec(memory_space=pl.ANY)
@@ -56,13 +57,18 @@
         g_ref[e] = gate[e]
 
 
-def expert_rows(s_map, d, rows, cap):
+def row_picks(s_map, d, tok, n_dev, cap):
     pairs, lanes = s_map.shape
-    local, n_dev, tok = pairs // 8, 8, rows.shape[0]
-    pick = (iota((local * cap, pairs), 1) == iota((local * cap, pairs), 0) // cap * n_dev + d)
-    slot = mm(pick.astype(F32).astype(BF16), s_map.astype(BF16))
-    onehot = jnp.where(slot == (iota((local * cap, lanes), 0) % cap).astype(F32), 1.0, 0.0).astype(BF16)
-    return mm(onehot[:, :tok], rows).astype(BF16)
+    n_rows = pairs // n_dev * cap
+    spread = iota((n_rows, pairs), 1) == iota((n_rows, pairs), 0) // cap * n_dev + d
+    slot = mm(spread.astype(F32).astype(BF16), s_map.astype(BF16))
+    return jnp.where(slot == (iota((n_rows, lanes), 0) % cap).astype(F32), 1.0, 0.0).astype(BF16)[:, :tok]
+
+
+def fill_rows(s_map, d, sources, cap):
+    picks = row_picks(s_map, d, sources[0][0].shape[1], sources[0][0].shape[0], cap)
+    for rows, out in sources:
+        out[d] = mm(picks, rows[d]).astype(BF16).reshape(out.shape[1:])
 
 
 def limbs(gate):
@@ -96,15 +102,6 @@
     return total
 
 
-def forward_rows(u, w_gate, w_up, w_down):
-    pre_gate = mm(u, w_gate)
-    pre_up = mm(u, w_up)
-    sig = jax.nn.sigmoid(pre_gate)
-    act = pre_gate * sig
-    hidden = (act * pre_up).astype(BF16)
-    return pre_gate, pre_up, sig, act, hidden, mm(hidden, w_down).astype(BF16)
-
-
 class Links:
     def __init__(self, n_dev, send_sems, recv_sems):
         me = lax.axis_index("ep")
@@ -276,25 +273,33 @@
         pltpu.make_async_copy(src.at[e], dst.at[e], sems.at[i, e]).wait()
 
 
-def forward_experts(pairs, sems, u_ref, o_ref, cap):
-    n_dev, local, _, width = u_ref.shape
-
-    def step(e, carry):
-        wait_weights(pairs, sems, e)
-        u = u_ref[:, e].reshape(n_dev * cap, width)
-        out = forward_rows(u, *(dst[e] for _, dst in pairs))[-1]
-        o_ref[:, e] = out.reshape(n_dev, cap, width)
+def forward_experts(pairs, sems, u_ref, o_ref, cap, first, last):
+    n_dev, _, _, width = u_ref.shape
+
+    def step(g, carry):
+        experts = [g * GROUPED + i for i in range(GROUPED)]
+        for e in experts:
+            wait_weights(pairs, sems, e)
+        w_gate, w_up, w_down = (dst for _, dst in pairs)
+        rows = [u_ref[:, e].reshape(n_dev * cap, width) for e in experts]
+        pre = [(mm(u, w_gate[e]), mm(u, w_up[e])) for u, e in zip(rows, experts)]
+        hidden = [(gate * jax.nn.sigmoid(gate) * up).astype(BF16) for gate, up in pre]
+        for h, e in zip(hidden, experts):
+            o_ref[:, e] = mm(h, w_down[e]).astype(BF16).reshape(n_dev, cap, width)
         return carry
-    lax.fori_loop(0, local, step, 0)
-
-
-def first_kernel(dims, x_ref, dy_ref, meta_ref, w1, w3, w2,
+    lax.fori_loop(first // GROUPED, last // GROUPED, step, 0)
+
+
+def first_kernel(dims, x_ref, dy_ref, idx_a, gate_a, idx_b, gate_b, w1, w3, w2,
                  mid_all, dy_all, mid_own, sa, ga, rela, sb, gb, relb,
-                 x_all, y_all, m_all, meta_all, u_ref, o_ref, part, near, mine, got, mid_buf, w1_v, w3_v, w2_v,
+                 x_all, y_all, m_all, meta_ref, meta_all, u_ref, o_ref, part, near, mine, got, mid_buf, w1_v, w3_v, w2_v,
                  w_sems, send_sems, recv_sems):
     n_dev, tok, width, local, cap, top_k = dims
     pairs = ((w1, w1_v), (w3, w3_v), (w2, w2_v))
     load_weights(pairs, w_sems, local)
+    meta_ref[...] = jnp.full(meta_ref.shape, -1.0, F32)
+    for i, ref in enumerate((idx_a, gate_a, idx_b, gate_b)):
+        meta_ref[i * top_k : (i + 1) * top_k, :tok] = ref[...].astype(F32)
     links = Links(n_dev, send_sems, recv_sems)
     me = links.me
     links.greet()
@@ -315,7 +320,7 @@
     s_map = sa[...].reshape(local * n_dev, LANES)
 
     def rows_of(d):
-        u_ref[d] = expert_rows(s_map, d, x_all[d], cap).reshape(local, cap, width)
+        fill_rows(s_map, d, ((x_all, u_ref),), cap)
 
     rows_of(me)
     rows_of(links.left)
@@ -330,7 +335,7 @@
     rows_of(links.right + side)
     x_g.wait_last()
     rows_of(links.opp + side)
-    forward_experts(pairs, w_sems, u_ref, o_ref, cap)
+    forward_experts(pairs, w_sems, u_ref, o_ref, cap, 0, local)
     y_g.pass_far()
     stack = scatter_lhs(s_map, ga[...].reshape(local * n_dev, LANES), tok)
     red = Reduce(links, part, (near, mine, got))
@@ -361,53 +366,80 @@
 
 
 def backward_kernel(dims, x_all, dy_all, s_ref, g_ref, rel_ref, w1, w3, w2,
-                    dw1, dw3, dw2, part, dgate, u_ref, y_ref, du_ref, dg_ref):
+                    dw1, dw3, dw2, part, dgate,
+                    u_ref, y_ref, du_ref, dg_ref, w1_v, w3_v, w2_v, dw1_v, dw3_v, dw2_v, w_sems, out_sems):
     n_dev, tok, width, local, cap, top_k = dims
-    e = pl.program_id(0)
     n_rows = n_dev * cap
-
-    @pl.when(e == 0)
-    def _():
-        s_map = s_ref[...].reshape(local * n_dev, LANES)
-
-        def rows_of(d, carry):
-            u_ref[d] = expert_rows(s_map, d, x_all[d], cap).reshape(local, cap, width)
-            y_ref[d] = expert_rows(s_map, d, dy_all[d], cap).reshape(local, cap, width)
-            return carry
-        lax.fori_loop(0, n_dev, rows_of, 0)
-
-    u = u_ref[:, e].reshape(n_rows, width)
-    dy = y_ref[:, e].reshape(n_rows, width).astype(F32)
-    w_gate, w_up, w_down = w1[0], w3[0], w2[0]
-    pre_gate, pre_up, sig, act, hidden, out = forward_rows(u, w_gate, w_up, w_down)
-    slot = s_ref[e][:, None, :] == iota((n_dev, cap, LANES), 1).astype(F32)
-    gate_row = jnp.sum(jnp.where(slot, g_ref[e][:, None, :], 0.0), axis=2, keepdims=True).reshape(n_rows, 1)
-    dg_row = jnp.sum(dy * out.astype(F32), axis=1, keepdims=True).reshape(n_dev, cap, 1)
-    dg_ref[e] = jnp.sum(jnp.where(slot, dg_row, 0.0), axis=1)
-    q = (gate_row * dy).astype(BF16)
-    dw2[0] = mm_tn(hidden, q)
-    d_hidden = mm_nt(q, w_down)
-    d_gate = (d_hidden * pre_up * sig * (1.0 + pre_gate * (1.0 - sig))).astype(BF16)
-    d_up = (d_hidden * act).astype(BF16)
-    dw1[0] = mm_tn(u, d_gate)
-    dw3[0] = mm_tn(u, d_up)
-    du = (mm_nt(d_gate, w_gate) + mm_nt(d_up, w_up)).astype(BF16)
-    du_ref[:, e] = du.reshape(n_dev, cap, width)
-
-    @pl.when(e == local - 1)
-    def _():
-        s_map = s_ref[...].reshape(local * n_dev, LANES)
-        stack = scatter_lhs(s_map, None, tok)
-
-        def sums_of(d, carry):
-            part[d] = token_sums(stack, d, du_ref[d].reshape(local * cap, width), tok, cap)
-            return carry
-        lax.fori_loop(0, n_dev, sums_of, 0)
-        for d in range(n_dev):
-            total = jnp.zeros((top_k, LANES), F32)
-            for i in range(local):
-                total = jnp.where(rel_ref[d] == float(i), dg_ref[i, d : d + 1, :], total)
-            dgate[d] = total
+    pairs = ((w1, w1_v), (w3, w3_v), (w2, w2_v))
+    outs = ((dw1_v, dw1), (dw3_v, dw3), (dw2_v, dw2))
+    load_weights(pairs, w_sems, local)
+    s_map = s_ref[...].reshape(local * n_dev, LANES)
+
+    def rows_of(d, carry):
+        fill_rows(s_map, d, ((x_all, u_ref), (dy_all, y_ref)), cap)
+        return carry
+    lax.fori_loop(0, n_dev, rows_of, 0, unroll=2)
+
+    def store(g, i, slot):
+        src, dst = outs[i]
+        return pltpu.make_async_copy(src.at[slot], dst.at[pl.ds(g * GROUPED, GROUPED)], out_sems.at[i, slot])
+
+    def step(g, carry):
+        slot = lax.rem(g, 2)
+        experts = [g * GROUPED + i for i in range(GROUPED)]
+        each = range(GROUPED)
+        for e in experts:
+            wait_weights(pairs, w_sems, e)
+
+        @pl.when(g >= 2)
+        def _():
+            for i in range(3):
+                store(g - 2, i, slot).wait()
+        u = [u_ref[:, e].reshape(n_rows, width) for e in experts]
+        dy = [y_ref[:, e].reshape(n_rows, width) for e in experts]
+        holds = [s_ref[e][:, None, :] == iota((n_dev, cap, LANES), 1).astype(F32) for e in experts]
+        gate_row = [jnp.sum(jnp.where(holds[i], g_ref[e][:, None, :], 0.0), axis=2, keepdims=True).reshape(n_rows, 1)
+                    for i, e in enumerate(experts)]
+        q = [(gate_row[i] * dy[i].astype(F32)).astype(BF16) for i in each]
+        pre = [(mm(u[i], w1_v[e]), mm(u[i], w3_v[e])) for i, e in enumerate(experts)]
+        d_hidden = [mm_nt(q[i], w2_v[e]) for i, e in enumerate(experts)]
+        sig = [jax.nn.sigmoid(a) for a, _ in pre]
+        act = [pre[i][0] * sig[i] for i in each]
+        hidden = [(act[i] * pre[i][1]).astype(BF16) for i in each]
+        out = [mm(hidden[i], w2_v[e]).astype(BF16) for i, e in enumerate(experts)]
+        for i in each:
+            dw2_v[slot, i] = mm_tn(hidden[i], q[i])
+        d_gate = [(d_hidden[i] * pre[i][1] * sig[i] * (1.0 + pre[i][0] * (1.0 - sig[i]))).astype(BF16) for i in each]
+        d_up = [(d_hidden[i] * act[i]).astype(BF16) for i in each]
+        for i, e in enumerate(experts):
+            dg_row = jnp.sum(dy[i].astype(F32) * out[i].astype(F32), axis=1, keepdims=True).reshape(n_dev, cap, 1)
+            dg_ref[e] = jnp.sum(jnp.where(holds[i], dg_row, 0.0), axis=1)
+        for i, e in enumerate(experts):
+            du = (mm_nt(d_gate[i], w1_v[e]) + mm_nt(d_up[i], w3_v[e])).astype(BF16)
+            du_ref[:, e] = du.reshape(n_dev, cap, width)
+        for i in each:
+            dw1_v[slot, i] = mm_tn(u[i], d_gate[i])
+            dw3_v[slot, i] = mm_tn(u[i], d_up[i])
+        for i in range(3):
+            store(g, i, slot).start()
+        return carry
+    steps = local // GROUPED
+    lax.fori_loop(0, steps, step, 0)
+
+    stack = scatter_lhs(s_map, None, tok)
+
+    def sums_of(d, carry):
+        part[d] = token_sums(stack, d, du_ref[d].reshape(local * cap, width), tok, cap)
+        return carry
+    lax.fori_loop(0, n_dev, sums_of, 0, unroll=2)
+    for d in range(n_dev):
+        total = jnp.zeros((top_k, LANES), F32)
+        for i in range(local):
+            total = jnp.where(rel_ref[d] == float(i), dg_ref[i, d : d + 1, :], total)
+        dgate[d] = total
+    for g in (steps - 2, steps - 1):
+        for i in range(3):
+            store(g, i, g % 2).wait()
 
 
 def middle_kernel(dims, part_b, dg_part, dy_ref, x_ref, mid_all, sb, gb, w1, w3, w2,
@@ -422,45 +454,56 @@
     links.greet()
     red = Reduce(links, part_b, (near, mine, got))
     dg = Reduce(links, dg_part, (dg_near, dg_mine, dg_got), split=False)
+    s_map = sb[...].reshape(local * n_dev, LANES)
+
+    def rows_of(d, carry):
+        fill_rows(s_map, d, ((mid_all, u_ref),), cap)
+        return carry
+
+    def sums_of(d, carry):
+        part_x[d] = token_sums(stack, d, o_ref[d].reshape(local * cap, width), tok, cap)
+        return carry
+
     red.start()
     dg.start()
     x_g = Gather(links, x_ref, x_all)
     x_all[me] = x_ref[...]
+    lax.fori_loop(0, 2, rows_of, 0, unroll=2)
     red.far()
     red.near_sends()
-    red.relay()
     dg.far()
     dg.near_sends()
+    lax.fori_loop(2, n_dev, rows_of, 0, unroll=2)
     x_g.pass_on()
+    red.relay()
+    dg.relay()
+    half = local // 2 // GROUPED * GROUPED
+    forward_experts(pairs, w_sems, u_ref, o_ref, cap, 0, half)
+    x_g.pass_far()
     dx = (dy_ref[...].astype(F32) + red.result()).astype(BF16)
     d_buf[...] = dx
     dmid_own[...] = dx
     d_all[me] = dx
     d_g = Gather(links, d_buf, d_all)
-    dg.relay()
-    x_g.pass_far()
+    forward_experts(pairs, w_sems, u_ref, o_ref, cap, half, local)
     d_g.pass_on()
+    stack = scatter_lhs(s_map, gb[...].reshape(local * n_dev, LANES), tok)
+    lax.fori_loop(0, n_dev, sums_of, 0, unroll=2)
     d_g.pass_far()
-
-    s_map = sb[...].reshape(local * n_dev, LANES)
-
-    def rows_of(d, carry):
-        u_ref[d] = expert_rows(s_map, d, mid_all[d], cap).reshape(local, cap, width)
-        return carry
-    lax.fori_loop(0, n_dev, rows_of, 0)
-    forward_experts(pairs, w_sems, u_ref, o_ref, cap)
-    stack = scatter_lhs(s_map, gb[...].reshape(local * n_dev, LANES), tok)
-
-    def sums_of(d, carry):
-        part_x[d] = token_sums(stack, d, o_ref[d].reshape(local * cap, width), tok, cap)
-        return carry
-    lax.fori_loop(0, n_dev, sums_of, 0)
     dgate[...] = dg.result()
     x_g.finish()
     x_again[...] = x_all[...]
     d_g.finish()
     dmid_all[...] = d_all[...]
     links.drain()
+
+
+def final_kernel(x_ref, dx_ref, dga_ref, dgb_ref, x_out, dx_out, dga_out, dgb_out):
+    x_out[...] = x_ref[...]
+    dx_out[...] = dx_ref[...]
+    tok = dga_out.shape[1]
+    dga_out[...] = dga_ref[:, :tok]
+    dgb_out[...] = dgb_ref[:, :tok]
 
 
 def last_kernel(dims, part_a, dg_part, part_x, dmid_ref, mid_ref, dx_out, dgate, x_out,
@@ -508,10 +551,6 @@
         map_s = sds((local, n_dev, LANES), F32)
         own = sds((tok, width), BF16)
 
-        def lanes(rows, fill):
-            return jnp.pad(rows.T.astype(F32), ((0, 0), (0, LANES - tok)), constant_values=fill)
-
-        meta = jnp.concatenate([lanes(idx_a, -1.0), lanes(gate_a, 0.0), lanes(idx_b, -1.0), lanes(gate_b, 0.0)])
         weights_v = [pltpu.VMEM((local, width, inner), BF16)] * 2 + [pltpu.VMEM((local, inner, width), BF16)]
         w_sems = pltpu.SemaphoreType.DMA((3, local))
         rows_v = pltpu.VMEM((n_dev, tok, width), BF16)
@@ -521,28 +560,25 @@
         mid_all, dy_all, mid_own, sa, ga, rela, sb, gb, relb = pl.pallas_call(
             functools.partial(first_kernel, dims),
             out_shape=(rows_all, rows_all, own, map_s, map_s, dg_all, map_s, map_s, dg_all),
-            in_specs=[VMEM] * 3 + [ANY] * 3,
+            in_specs=[VMEM] * 6 + [ANY] * 3,
             out_specs=[VMEM] * 9,
-            scratch_shapes=[rows_v, rows_v, rows_v, pltpu.VMEM((n_dev, 4 * top_k, LANES), F32), expert_v, expert_v,
+            scratch_shapes=[rows_v, rows_v, rows_v, pltpu.VMEM((4 * top_k, LANES), F32), pltpu.VMEM((n_dev, 4 * top_k, LANES), F32), expert_v, expert_v,
                             pltpu.VMEM((n_dev, tok, width), F32), *Reduce.scratch(tok, width),
                             pltpu.VMEM((tok, width), BF16), *weights_v, w_sems, *dma_sems(count)],
             compiler_params=remote_params(0), name="first",
-        )(x_in, dy_out, meta, w1_a, w3_a, w2_a)
+        )(x_in, dy_out, idx_a.T, gate_a.T, idx_b.T, gate_b.T, w1_a, w3_a, w2_a)
 
         def backward(x_all, d_all, s, g, rel, w1, w3, w2):
-            whole = pl.BlockSpec(memory_space=pltpu.VMEM)
-            w_in = pl.BlockSpec((1, width, inner), lambda e: (e, 0, 0))
-            w_out = pl.BlockSpec((1, inner, width), lambda e: (e, 0, 0))
             return pl.pallas_call(
                 functools.partial(backward_kernel, dims),
-                grid=(local,),
                 out_shape=(sds((local, width, inner), F32), sds((local, width, inner), F32),
                            sds((local, inner, width), F32), part_all, dg_all),
-                in_specs=[whole] * 5 + [w_in, w_in, w_out],
-                out_specs=[w_in, w_in, w_out, whole, whole],
-                scratch_shapes=[expert_v, expert_v, expert_v, pltpu.VMEM((local, n_dev, LANES), F32)],
-                compiler_params=pltpu.CompilerParams(dimension_semantics=("arbitrary",), vmem_limit_bytes=VMEM_LIMIT),
-                name="backward",
+                in_specs=[VMEM] * 5 + [ANY] * 3,
+                out_specs=[ANY] * 3 + [VMEM] * 2,
+                scratch_shapes=[expert_v, expert_v, expert_v, pltpu.VMEM((local, n_dev, LANES), F32), *weights_v,
+                                *[pltpu.VMEM((2, GROUPED, width, inner), F32)] * 2,
+                                pltpu.VMEM((2, GROUPED, inner, width), F32), w_sems, pltpu.SemaphoreType.DMA((3, 2))],
+                compiler_params=pltpu.CompilerParams(vmem_limit_bytes=VMEM_LIMIT), name="backward",
             )(x_all, d_all, s, g, rel, w1, w3, w2)
 
         *grads_b, part_b, dg_b = backward(mid_all, dy_all, sb, gb, relb, w1_b, w3_b, w2_b)
@@ -571,6 +607,10 @@
                             *dma_sems(count)],
             compiler_params=remote_params(2), name="last",
         )(part_a, dg_a, part_x, dmid_own, mid_own)
-        return (x_out, dx_in, *grads_a, *grads_b, dgate_a[:, :tok].T, dgate_b[:, :tok].T)
+        gates = sds((top_k, tok), F32)
+        x_out, dx_in, dgate_a, dgate_b = pl.pallas_call(
+            final_kernel, out_shape=(own, own, gates, gates), in_specs=[VMEM] * 4, out_specs=[VMEM] * 4, name="final",
+        )(x_out, dx_in, dgate_a, dgate_b)
+        return (x_out, dx_in, *grads_a, *grads_b, dgate_a.T, dgate_b.T)
 
     return jax.shard_map(device_program, mesh=mesh, in_specs=(tok_spec,) * 6 + (w_spec,) * 6, out_specs=(tok_spec,) * 10, check_vma=False)

time: 193 us -> 146 us (0.76)
  Pallas kernels: 183 us -> 145 us
  local copies, waits for them, and re-layouts: 5.61 us -> 0 us
  other arithmetic: 2.02 us -> 0 us
    pallas_call x2 -> x3, Pallas kernels: 74.7 us -> 50.9 us  [the longest x2 49.2 us: backward(): pl.pallas_call(functools.partial(backward_kernel, dims), out_shape=(sds((...]
    pallas_call x1, Pallas kernels: 37 us -> 27.7 us  [device_program(): pl.pallas_call(functools.partial(middle_kernel, dims), out_shape=(rows_al...]
    unnamed x2 -> x0, local copies, waits for them, and re-layouts: 3.08 us -> none
    transpose x2 -> x0, local copies, waits for them, and re-layouts: 2.53 us -> none  [the longest x1 1.28 us: device_program(): dgate_a[:, :tok]]
    pallas_call x1, Pallas kernels: 47.6 us -> 45.1 us  [device_program(): pl.pallas_call(functools.partial(first_kernel, dims), out_shape=(rows_all...]
    pallas_call x1, Pallas kernels: 23.2 us -> 20.9 us  [device_program(): pl.pallas_call(functools.partial(last_kernel, dims), out_shape=(own, sds(...]
where the time goes in v2:
time: 146 us; the launch traced here: 145 us
  Pallas kernels  145 us (99%)
    pallas_call x2, Pallas kernels, backward(): pl.pallas_call(functools.partial(backward_kernel, dims), out_shape=(sds((...  49.2 us
    pallas_call x1, Pallas kernels, device_program(): pl.pallas_call(functools.partial(first_kernel, dims), out_shape=(rows_all...  45.1 us
    pallas_call x1, Pallas kernels, device_program(): pl.pallas_call(functools.partial(middle_kernel, dims), out_shape=(rows_al...  27.7 us
    pallas_call x1, Pallas kernels, device_program(): pl.pallas_call(functools.partial(last_kernel, dims), out_shape=(own, sds(...  20.9 us

profile of v2, /device:TPU:113, one launch (start us, length us, event | category | flops | bytes accessed | tf_op | source)
XLA Modules:
  0.0 145.2 jit_solution(9410843999381463424)
XLA Ops:
  0.6 45.1 %first.1 = (bf16[8,64,768]{2,1,0:T(8,128)(2,1)}, bf16[8,64,768]{2,1,0:T(8,128)(2,1)}, bf16[64,768]{1,0:T(8,128)(2,1)}, f32[16,8,128]{2,1,0:T(8,128)}, f32[16,8,1...) custom-call(bf16[64,768]{1,0:T(8,128)(2,1)} %x_ref.3, ...), custom_call_target="tpu_custom_call" | custom-call | tf_op jit(solution)/shard_map/first/pallas_call | solution.py:560
  45.8 24.5 %backward.2 = (f32[16,768,256]{2,1,0:T(8,128)}, f32[16,768,256]{2,1,0:T(8,128)}, f32[16,256,768]{2,1,0:T(8,128)}, f32[8,64,768]{2,1,0:T(8,128)}, f32[8,8,128]{2,1,0:T(8,128)}) custom-call(bf16[8,64,768]{2,1,0:T(8,128)(2,1)} %get-tuple-element.41.x_all.mid_all, bf16[8,64,768]{2,1,0:T(8,128)(2,1)} %get-tuple-element.42.dy_all, ...), custom_call_target="tpu_custom_call" | custom-call | tf_op jit(solution)/shard_map/backward/pallas_call | solution.py:572
  70.3 27.7 %middle.1 = (bf16[8,64,768]{2,1,0:T(8,128)(2,1)}, bf16[8,64,768]{2,1,0:T(8,128)(2,1)}, bf16[64,768]{1,0:T(8,128)(2,1)}, f32[8,128]{1,0:T(8,128)}, f32[8,64,768]{2,1,0:T(8,128)}) custom-call(f32[8,64,768]{2,1,0:T(8,128)} %get-tuple-element.46.part_b, f32[8,8,128]{2,1,0:T(8,128)} %get-tuple-element.47.dg_part, bf16[64,768]{1,0:T(8,128)(2,1)} %dy_ref.3, ...), custom_call_target="tpu_custom_call" | custom-call | tf_op jit(solution)/shard_map/middle/pallas_call | solution.py:587
  98.0 24.7 %backward.3 = (f32[16,768,256]{2,1,0:T(8,128)}, f32[16,768,256]{2,1,0:T(8,128)}, f32[16,256,768]{2,1,0:T(8,128)}, f32[8,64,768]{2,1,0:T(8,128)}, f32[8,8,128]{2,1,0:T(8,128)}) custom-call(bf16[8,64,768]{2,1,0:T(8,128)(2,1)} %get-tuple-element.48.x_all, bf16[8,64,768]{2,1,0:T(8,128)(2,1)} %get-tuple-element.49.dy_all, f32[16,8,128]{2,1,0:T(8,128)} %get-tuple-element.50.s_ref, ...), custom_call_target="tpu_custom_call" | custom-call | tf_op jit(solution)/shard_map/backward/pallas_call | solution.py:572
  122.7 20.9 %last.1 = (bf16[64,768]{1,0:T(8,128)(2,1)}, f32[8,128]{1,0:T(8,128)}, bf16[64,768]{1,0:T(8,128)(2,1)}) custom-call(f32[8,64,768]{2,1,0:T(8,128)} %get-tuple-element.53.part_a, f32[8,8,128]{2,1,0:T(8,128)} %get-tuple-element.54.dg_part, f32[8,64,768]{2,1,0:T(8,128)} %get-tuple-element.55.part_x, bf16[64,768]{1,0:T(8,128)(2,1)} %get-tuple-element.56.dmid_ref, ...), custom_call_target="tpu_custom_call" | custom-call | tf_op jit(solution)/shard_map/last/pallas_call | solution.py:601
  143.6 1.6 %final.1 = (bf16[64,768]{1,0:T(8,128)(2,1)}, bf16[64,768]{1,0:T(8,128)(2,1)}, f32[8,64]{1,0:T(8,128)}, f32[8,64]{1,0:T(8,128)}) custom-call(bf16[64,768]{1,0:T(8,128)(2,1)} %get-tuple-element.58.x_ref, bf16[64,768]{1,0:T(8,128)(2,1)} %get-tuple-element.59.dx_ref, f32[8,128]{1,0:T(8,128)} %get-tuple-element.60.dga_ref, f32[8,128]{1,0:T(8,128)} %get-tuple-element.61.dgb_ref), custom_call_target="tpu_custom_call" | custom-call | tf_op jit(solution)/shard_map/final/pallas_call | solution.py:611

commit v3 on v2

--- a/solution.py
+++ b/solution.py
@@ -14,6 +14,7 @@
 CAP_FACTOR = 4
 BF16_MAX = 3.3895313892515355e38
 GROUPED = 2
+FORWARD_GROUPED = 4
 VMEM_LIMIT = 60 * 1024 * 1024
 VMEM = pl.BlockSpec(memory_space=pltpu.VMEM)
 ANY = pl.BlockSpec(memory_space=pl.ANY)
@@ -40,21 +41,18 @@
     base = (me * local).astype(F32)
     row = 2 * layer * top_k
     rel_ref[...] = meta[:, row : row + top_k, :] - base
-    hit = [jnp.zeros((n_dev, LANES), F32) for _ in range(local)]
-    gate = [jnp.zeros((n_dev, LANES), F32) for _ in range(local)]
+    shape = (local, n_dev, LANES)
+    expert = iota(shape, 0).astype(F32)
+    hit, gate = jnp.zeros(shape, F32), jnp.zeros(shape, F32)
     for j in range(top_k):
-        rel_j = meta[:, row + j, :] - base
-        gate_j = meta[:, row + top_k + j, :]
-        for e in range(local):
-            match = rel_j == float(e)
-            hit[e] = jnp.where(match, 1.0, hit[e])
-            gate[e] = jnp.where(match, gate_j, gate[e])
-    hit = jnp.concatenate(hit, axis=0)
+        match = (meta[:, row + j, :] - base)[None] == expert
+        hit = jnp.where(match, 1.0, hit)
+        gate = jnp.where(match, meta[:, row + top_k + j, :][None], gate)
+    hit = hit.reshape(local * n_dev, LANES)
     earlier = (iota((LANES, LANES), 0) < iota((LANES, LANES), 1)).astype(F32).astype(BF16)
     slot = jnp.where(hit > 0.0, mm(hit.astype(BF16), earlier), -1.0)
-    s_ref[...] = slot.reshape(local, n_dev, LANES)
-    for e in range(local):
-        g_ref[e] = gate[e]
+    s_ref[...] = slot.reshape(shape)
+    g_ref[...] = gate
 
 
 def row_picks(s_map, d, tok, n_dev, cap):
@@ -275,9 +273,10 @@
 
 def forward_experts(pairs, sems, u_ref, o_ref, cap, first, last):
     n_dev, _, _, width = u_ref.shape
+    few = min(FORWARD_GROUPED, last - first)
 
     def step(g, carry):
-        experts = [g * GROUPED + i for i in range(GROUPED)]
+        experts = [first + g * few + i for i in range(few)]
         for e in experts:
             wait_weights(pairs, sems, e)
         w_gate, w_up, w_down = (dst for _, dst in pairs)
@@ -287,7 +286,7 @@
         for h, e in zip(hidden, experts):
             o_ref[:, e] = mm(h, w_down[e]).astype(BF16).reshape(n_dev, cap, width)
         return carry
-    lax.fori_loop(first // GROUPED, last // GROUPED, step, 0)
+    lax.fori_loop(0, (last - first) // few, step, 0)
 
 
 def first_kernel(dims, x_ref, dy_ref, idx_a, gate_a, idx_b, gate_b, w1, w3, w2,
@@ -305,14 +304,13 @@
     links.greet()
     meta_g = Gather(links, meta_ref, meta_all)
     x_g = Gather(links, x_ref, x_all)
-    y_g = Gather(links, dy_ref, y_all)
     meta_all[me] = meta_ref[...]
     x_all[me] = x_ref[...]
     y_all[me] = dy_ref[...]
     meta_g.pass_on()
     x_g.pass_on()
+    y_g = Gather(links, dy_ref, y_all)
     meta_g.pass_far()
-    x_g.pass_far()
     meta_g.finish()
     meta = meta_all[...]
     routing_maps(me, meta, 0, sa, ga, rela, top_k, local)
@@ -325,14 +323,15 @@
     rows_of(me)
     rows_of(links.left)
     rows_of(links.right)
-    rows_of(links.opp)
-    y_g.pass_on()
     x_g.wait_partner()
     rows_of(links.partner)
+    x_g.pass_far()
     x_g.wait_sides()
     side = 1 - 2 * links.core
     rows_of(links.left + side)
     rows_of(links.right + side)
+    rows_of(links.opp)
+    y_g.pass_on()
     x_g.wait_last()
     rows_of(links.opp + side)
     forward_experts(pairs, w_sems, u_ref, o_ref, cap, 0, local)
@@ -375,10 +374,8 @@
     load_weights(pairs, w_sems, local)
     s_map = s_ref[...].reshape(local * n_dev, LANES)
 
-    def rows_of(d, carry):
+    for d in range(n_dev):
         fill_rows(s_map, d, ((x_all, u_ref), (dy_all, y_ref)), cap)
-        return carry
-    lax.fori_loop(0, n_dev, rows_of, 0, unroll=2)
 
     def store(g, i, slot):
         src, dst = outs[i]
@@ -427,11 +424,8 @@
     lax.fori_loop(0, steps, step, 0)
 
     stack = scatter_lhs(s_map, None, tok)
-
-    def sums_of(d, carry):
+    for d in range(n_dev):
         part[d] = token_sums(stack, d, du_ref[d].reshape(local * cap, width), tok, cap)
-        return carry
-    lax.fori_loop(0, n_dev, sums_of, 0, unroll=2)
     for d in range(n_dev):
         total = jnp.zeros((top_k, LANES), F32)
         for i in range(local):
@@ -456,28 +450,25 @@
     dg = Reduce(links, dg_part, (dg_near, dg_mine, dg_got), split=False)
     s_map = sb[...].reshape(local * n_dev, LANES)
 
-    def rows_of(d, carry):
+    def rows_of(d):
         fill_rows(s_map, d, ((mid_all, u_ref),), cap)
-        return carry
-
-    def sums_of(d, carry):
-        part_x[d] = token_sums(stack, d, o_ref[d].reshape(local * cap, width), tok, cap)
-        return carry
 
     red.start()
     dg.start()
     x_g = Gather(links, x_ref, x_all)
     x_all[me] = x_ref[...]
-    lax.fori_loop(0, 2, rows_of, 0, unroll=2)
+    for d in range(2):
+        rows_of(d)
     red.far()
     red.near_sends()
     dg.far()
     dg.near_sends()
-    lax.fori_loop(2, n_dev, rows_of, 0, unroll=2)
+    for d in range(2, n_dev):
+        rows_of(d)
     x_g.pass_on()
     red.relay()
     dg.relay()
-    half = local // 2 // GROUPED * GROUPED
+    half = local // 2 // FORWARD_GROUPED * FORWARD_GROUPED
     forward_experts(pairs, w_sems, u_ref, o_ref, cap, 0, half)
     x_g.pass_far()
     dx = (dy_ref[...].astype(F32) + red.result()).astype(BF16)
@@ -488,7 +479,8 @@
     forward_experts(pairs, w_sems, u_ref, o_ref, cap, half, local)
     d_g.pass_on()
     stack = scatter_lhs(s_map, gb[...].reshape(local * n_dev, LANES), tok)
-    lax.fori_loop(0, n_dev, sums_of, 0, unroll=2)
+    for d in range(n_dev):
+        part_x[d] = token_sums(stack, d, o_ref[d].reshape(local * cap, width), tok, cap)
     d_g.pass_far()
     dgate[...] = dg.result()
     x_g.finish()

time: 146 us -> 143 us (0.979)
  Pallas kernels: 145 us -> 142 us
    pallas_call x1, Pallas kernels: 45.1 us -> 42.1 us  [device_program(): pl.pallas_call(functools.partial(first_kernel, dims), out_shape=(rows_all...]
where the time goes in v3:
time: 143 us
  Pallas kernels  142 us (99%)
    pallas_call x2, Pallas kernels, backward(): pl.pallas_call(functools.partial(backward_kernel, dims), out_shape=(sds((...  48.5 us
    pallas_call x1, Pallas kernels, device_program(): pl.pallas_call(functools.partial(first_kernel, dims), out_shape=(rows_all...  42.1 us
    pallas_call x1, Pallas kernels, device_program(): pl.pallas_call(functools.partial(middle_kernel, dims), out_shape=(rows_al...  28.5 us
    pallas_call x1, Pallas kernels, device_program(): pl.pallas_call(functools.partial(last_kernel, dims), out_shape=(own, sds(...  21.3 us

profile of v3, /device:TPU:113, one launch (start us, length us, event | category | flops | bytes accessed | tf_op | source)
XLA Modules:
  0.0 142.6 jit_solution(13644285520008464162)
XLA Ops:
  0.6 42.1 %first.1 = (bf16[8,64,768]{2,1,0:T(8,128)(2,1)}, bf16[8,64,768]{2,1,0:T(8,128)(2,1)}, bf16[64,768]{1,0:T(8,128)(2,1)}, f32[16,8,128]{2,1,0:T(8,128)}, f32[16,8,1...) custom-call(bf16[64,768]{1,0:T(8,128)(2,1)} %x_ref.3, ...), custom_call_target="tpu_custom_call" | custom-call | tf_op jit(solution)/shard_map/first/pallas_call | solution.py:552
  42.8 24.2 %backward.2 = (f32[16,768,256]{2,1,0:T(8,128)}, f32[16,768,256]{2,1,0:T(8,128)}, f32[16,256,768]{2,1,0:T(8,128)}, f32[8,64,768]{2,1,0:T(8,128)}, f32[8,8,128]{2,1,0:T(8,128)}) custom-call(bf16[8,64,768]{2,1,0:T(8,128)(2,1)} %get-tuple-element.41.x_all.mid_all, bf16[8,64,768]{2,1,0:T(8,128)(2,1)} %get-tuple-element.42.dy_all, ...), custom_call_target="tpu_custom_call" | custom-call | tf_op jit(solution)/shard_map/backward/pallas_call | solution.py:564
  67.0 28.5 %middle.1 = (bf16[8,64,768]{2,1,0:T(8,128)(2,1)}, bf16[8,64,768]{2,1,0:T(8,128)(2,1)}, bf16[64,768]{1,0:T(8,128)(2,1)}, f32[8,128]{1,0:T(8,128)}, f32[8,64,768]{2,1,0:T(8,128)}) custom-call(f32[8,64,768]{2,1,0:T(8,128)} %get-tuple-element.46.part_b, f32[8,8,128]{2,1,0:T(8,128)} %get-tuple-element.47.dg_part, bf16[64,768]{1,0:T(8,128)(2,1)} %dy_ref.3, ...), custom_call_target="tpu_custom_call" | custom-call | tf_op jit(solution)/shard_map/middle/pallas_call | solution.py:579
  95.5 24.2 %backward.3 = (f32[16,768,256]{2,1,0:T(8,128)}, f32[16,768,256]{2,1,0:T(8,128)}, f32[16,256,768]{2,1,0:T(8,128)}, f32[8,64,768]{2,1,0:T(8,128)}, f32[8,8,128]{2,1,0:T(8,128)}) custom-call(bf16[8,64,768]{2,1,0:T(8,128)(2,1)} %get-tuple-element.48.x_all, bf16[8,64,768]{2,1,0:T(8,128)(2,1)} %get-tuple-element.49.dy_all, f32[16,8,128]{2,1,0:T(8,128)} %get-tuple-element.50.s_ref, ...), custom_call_target="tpu_custom_call" | custom-call | tf_op jit(solution)/shard_map/backward/pallas_call | solution.py:564
  119.7 21.3 %last.1 = (bf16[64,768]{1,0:T(8,128)(2,1)}, f32[8,128]{1,0:T(8,128)}, bf16[64,768]{1,0:T(8,128)(2,1)}) custom-call(f32[8,64,768]{2,1,0:T(8,128)} %get-tuple-element.53.part_a, f32[8,8,128]{2,1,0:T(8,128)} %get-tuple-element.54.dg_part, f32[8,64,768]{2,1,0:T(8,128)} %get-tuple-element.55.part_x, bf16[64,768]{1,0:T(8,128)(2,1)} %get-tuple-element.56.dmid_ref, ...), custom_call_target="tpu_custom_call" | custom-call | tf_op jit(solution)/shard_map/last/pallas_call | solution.py:593
  141.0 1.6 %final.1 = (bf16[64,768]{1,0:T(8,128)(2,1)}, bf16[64,768]{1,0:T(8,128)(2,1)}, f32[8,64]{1,0:T(8,128)}, f32[8,64]{1,0:T(8,128)}) custom-call(bf16[64,768]{1,0:T(8,128)(2,1)} %get-tuple-element.58.x_ref, bf16[64,768]{1,0:T(8,128)(2,1)} %get-tuple-element.59.dx_ref, f32[8,128]{1,0:T(8,128)} %get-tuple-element.60.dga_ref, f32[8,128]{1,0:T(8,128)} %get-tuple-element.61.dgb_ref), custom_call_target="tpu_custom_call" | custom-call | tf_op jit(solution)/shard_map/final/pallas_call | solution.py:603

commit v4 on v3

--- a/solution.py
+++ b/solution.py
@@ -16,6 +16,7 @@
 GROUPED = 2
 FORWARD_GROUPED = 4
 VMEM_LIMIT = 60 * 1024 * 1024
+SMALL_VMEM_LIMIT = 16 * 1024 * 1024
 VMEM = pl.BlockSpec(memory_space=pltpu.VMEM)
 ANY = pl.BlockSpec(memory_space=pl.ANY)
 
@@ -437,8 +438,8 @@
 
 
 def middle_kernel(dims, part_b, dg_part, dy_ref, x_ref, mid_all, sb, gb, w1, w3, w2,
-                  dmid_all, x_again, dmid_own, dgate, part_x,
-                  d_all, x_all, u_ref, o_ref, near, mine, got, dg_near, dg_mine, dg_got, d_buf, w1_v, w3_v, w2_v,
+                  dmid_all, x_again, dmid_own, dgate, own_x, right_x, opp_x, left_x,
+                  part_x, near_x, d_all, x_all, u_ref, o_ref, near, mine, got, dg_near, dg_mine, dg_got, d_buf, w1_v, w3_v, w2_v,
                   w_sems, send_sems, recv_sems):
     n_dev, tok, width, local, cap, top_k = dims
     pairs = ((w1, w1_v), (w3, w3_v), (w2, w2_v))
@@ -480,8 +481,13 @@
     d_g.pass_on()
     stack = scatter_lhs(s_map, gb[...].reshape(local * n_dev, LANES), tok)
     for d in range(n_dev):
-        part_x[d] = token_sums(stack, d, o_ref[d].reshape(local * cap, width), tok, cap)
+        part_x[d % 2, d // 2] = token_sums(stack, d, o_ref[d].reshape(local * cap, width), tok, cap)
+    side_x = links.copy(part_x.at[1 - links.core], near_x, links.partner)
     d_g.pass_far()
+    side_x.wait_recv()
+    for hop, out in enumerate((own_x, right_x, opp_x, left_x)):
+        chip = lax.rem((me - links.core) // 2 + hop, n_dev // 2)
+        out[...] = part_x[links.core, chip] + near_x[chip]
     dgate[...] = dg.result()
     x_g.finish()
     x_again[...] = x_all[...]
@@ -498,27 +504,29 @@
     dgb_out[...] = dgb_ref[:, :tok]
 
 
-def last_kernel(dims, part_a, dg_part, part_x, dmid_ref, mid_ref, dx_out, dgate, x_out,
-                near, mine, got, dg_near, dg_mine, dg_got, x_near, x_mine, x_got, send_sems, recv_sems):
+def last_kernel(dims, part_a, dg_part, dmid_ref, mid_ref, own_x, left_x, opp_x, right_x, dx_out, dgate, x_out,
+                near, mine, got, dg_near, dg_mine, dg_got, send_sems, recv_sems):
     links = Links(dims[0], send_sems, recv_sems)
     links.greet()
-    reds = (Reduce(links, part_a, (near, mine, got)), Reduce(links, part_x, (x_near, x_mine, x_got)),
-            Reduce(links, dg_part, (dg_near, dg_mine, dg_got), split=False))
-    for red in reds:
-        red.start()
-    for red in reds:
-        red.far()
-        red.near_sends()
-    for red in reds:
-        red.relay()
-    dx_out[...] = (dmid_ref[...].astype(F32) + reds[0].result()).astype(BF16)
-    x_out[...] = (mid_ref[...].astype(F32) + reds[1].result()).astype(BF16)
-    dgate[...] = reds[2].result()
+    red = Reduce(links, part_a, (near, mine, got))
+    dg = Reduce(links, dg_part, (dg_near, dg_mine, dg_got), split=False)
+    red.start()
+    dg.start()
+    red.far()
+    red.near_sends()
+    dg.far()
+    dg.near_sends()
+    total = own_x[...] + left_x[...] + opp_x[...] + right_x[...]
+    x_out[...] = (mid_ref[...].astype(F32) + total).astype(BF16)
+    red.relay()
+    dg.relay()
+    dx_out[...] = (dmid_ref[...].astype(F32) + red.result()).astype(BF16)
+    dgate[...] = dg.result()
     links.drain()
 
 
-def remote_params(ident):
-    return pltpu.CompilerParams(collective_id=ident, has_side_effects=True, vmem_limit_bytes=VMEM_LIMIT)
+def remote_params(ident, limit=VMEM_LIMIT):
+    return pltpu.CompilerParams(collective_id=ident, has_side_effects=True, vmem_limit_bytes=limit)
 
 
 def dma_sems(count):
@@ -571,34 +579,40 @@
                                 *[pltpu.VMEM((2, GROUPED, width, inner), F32)] * 2,
                                 pltpu.VMEM((2, GROUPED, inner, width), F32), w_sems, pltpu.SemaphoreType.DMA((3, 2))],
                 compiler_params=pltpu.CompilerParams(vmem_limit_bytes=VMEM_LIMIT), name="backward",
+                cost_estimate=pl.CostEstimate(flops=18 * local * n_dev * cap * width * inner, transcendentals=0,
+                                              bytes_accessed=18 * local * width * inner),
             )(x_all, d_all, s, g, rel, w1, w3, w2)
 
         *grads_b, part_b, dg_b = backward(mid_all, dy_all, sb, gb, relb, w1_b, w3_b, w2_b)
 
-        count = 2 * Gather.COPIES + 2 * Reduce.COPIES
-        dmid_all, x_again, dmid_own, dgate_b, part_x = pl.pallas_call(
+        count = 2 * Gather.COPIES + 2 * Reduce.COPIES + 1
+        sums = sds((tok, width), F32)
+        chip_sums = pltpu.VMEM((n_dev // 2, tok, width), F32)
+        dmid_all, x_again, dmid_own, dgate_b, own_x, right_x, opp_x, left_x = pl.pallas_call(
             functools.partial(middle_kernel, dims),
-            out_shape=(rows_all, rows_all, own, sds((top_k, LANES), F32), part_all),
+            out_shape=(rows_all, rows_all, own, sds((top_k, LANES), F32), sums, sums, sums, sums),
             in_specs=[VMEM] * 7 + [ANY] * 3,
-            out_specs=[VMEM] * 5,
-            scratch_shapes=[rows_v, rows_v, expert_v, expert_v, *Reduce.scratch(tok, width),
-                            *Reduce.scratch(top_k, LANES), pltpu.VMEM((tok, width), BF16), *weights_v, w_sems,
-                            *dma_sems(count)],
+            out_specs=[VMEM] * 8,
+            scratch_shapes=[pltpu.VMEM((2, n_dev // 2, tok, width), F32), chip_sums, rows_v, rows_v, expert_v, expert_v,
+                            *Reduce.scratch(tok, width), *Reduce.scratch(top_k, LANES), pltpu.VMEM((tok, width), BF16),
+                            *weights_v, w_sems, *dma_sems(count)],
             compiler_params=remote_params(1), name="middle",
         )(part_b, dg_b, dy_out, x_in, mid_all, sb, gb, w1_b, w3_b, w2_b)
 
+        def shift(rows, hop):
+            return lax.ppermute(rows, "ep", [(i, (i + 2 * hop) % n_dev) for i in range(n_dev)])
+
+        left_x, opp_x, right_x = shift(right_x, 1), shift(opp_x, 2), shift(left_x, 3)
         *grads_a, part_a, dg_a = backward(x_again, dmid_all, sa, ga, rela, w1_a, w3_a, w2_a)
 
-        count = 3 * Reduce.COPIES
         dx_in, dgate_a, x_out = pl.pallas_call(
             functools.partial(last_kernel, dims),
             out_shape=(own, sds((top_k, LANES), F32), own),
-            in_specs=[VMEM] * 5,
+            in_specs=[VMEM] * 8,
             out_specs=[VMEM] * 3,
-            scratch_shapes=[*Reduce.scratch(tok, width), *Reduce.scratch(top_k, LANES), *Reduce.scratch(tok, width),
-                            *dma_sems(count)],
-            compiler_params=remote_params(2), name="last",
-        )(part_a, dg_a, part_x, dmid_own, mid_own)
+            scratch_shapes=[*Reduce.scratch(tok, width), *Reduce.scratch(top_k, LANES), *dma_sems(2 * Reduce.COPIES)],
+            compiler_params=remote_params(2, SMALL_VMEM_LIMIT), name="last",
+        )(part_a, dg_a, dmid_own, mid_own, own_x, left_x, opp_x, right_x)
         gates = sds((top_k, tok), F32)
         x_out, dx_in, dgate_a, dgate_b = pl.pallas_call(
             final_kernel, out_shape=(own, own, gates, gates), in_specs=[VMEM] * 4, out_specs=[VMEM] * 4, name="final",

time: 143 us -> 142 us (level)
  Pallas kernels: 142 us -> 134 us
  local copies, waits for them, and re-layouts: 0 us -> 4.03 us
  starting transfers between devices: 0 us -> 3.04 us
    pallas_call x1, Pallas kernels: 21.3 us -> 12.5 us  [device_program(): pl.pallas_call(functools.partial(last_kernel, dims), out_shape=(own, sds(...]
    unnamed x0 -> x16, local copies, waits for them, and re-layouts: none -> 4.03 us
    ppermute x0 -> x3, starting transfers between devices: none -> 3.04 us  [shift(): lax.ppermute(rows, 'ep', [(i, (i + 2 * hop) % n_dev) for i in range(n_dev)])]
  transfers between devices with their start and end apart: 0 -> 3, of which waited for: 0 -> 0; matrix products, arithmetic and copies ran while one was open for 0% -> 0% of each run, Pallas kernels for 0% -> 17%
where the time goes in v4:
time: 142 us
  Pallas kernels  134 us (94%)
  local copies, waits for them, and re-layouts  4.03 us (3%)
  starting transfers between devices  3.04 us (2%)
    pallas_call x2, Pallas kernels, backward(): pl.pallas_call(functools.partial(backward_kernel, dims), out_shape=(sds((...  48.5 us
    pallas_call x1, Pallas kernels, device_program(): pl.pallas_call(functools.partial(first_kernel, dims), out_shape=(rows_all...  42.2 us
    pallas_call x1, Pallas kernels, device_program(): pl.pallas_call(functools.partial(middle_kernel, dims), out_shape=(rows_al...  29.5 us
    pallas_call x1, Pallas kernels, device_program(): pl.pallas_call(functools.partial(last_kernel, dims), out_shape=(own, sds(...  12.5 us
    unnamed x16, local copies, waits for them, and re-layouts  4.03 us
    ppermute x3, starting transfers between devices, shift(): lax.ppermute(rows, 'ep', [(i, (i + 2 * hop) % n_dev) for i in range(n_dev)])  3.04 us
  transfers between devices with their start and end apart: 3, of which 0 were waited for; matrix products, arithmetic and copies ran while one was open for 0% of the time, Pallas kernels for 17%

profile of v4, /device:TPU:113, one launch (start us, length us, event | category | flops | bytes accessed | tf_op | source)
XLA Modules:
  0.0 142.1 jit_solution(17906998404445761877)
XLA Ops:
  0.6 42.2 %first.1 = (bf16[8,64,768]{2,1,0:T(8,128)(2,1)}, bf16[8,64,768]{2,1,0:T(8,128)(2,1)}, bf16[64,768]{1,0:T(8,128)(2,1)}, f32[16,8,128]{2,1,0:T(8,128)}, f32[16,8,1...) custom-call(bf16[64,768]{1,0:T(8,128)(2,1)} %x_ref.3, ...), custom_call_target="tpu_custom_call" | custom-call | tf_op jit(solution)/shard_map/first/pallas_call | solution.py:560
  42.8 24.2 %backward.2 = (f32[16,768,256]{2,1,0:T(8,128)}, f32[16,768,256]{2,1,0:T(8,128)}, f32[16,256,768]{2,1,0:T(8,128)}, f32[8,64,768]{2,1,0:T(8,128)}, f32[8,8,128]{2,1,0:T(8,128)}) custom-call(bf16[8,64,768]{2,1,0:T(8,128)(2,1)} %get-tuple-element.44.x_all.mid_all, bf16[8,64,768]{2,1,0:T(8,128)(2,1)} %get-tuple-element.45.dy_all, ...), custom_call_target="tpu_custom_call" | custom-call | flops 7247757312 | bytes 56623104 | tf_op jit(solution)/shard_map/backward/pallas_call | solution.py:572
  67.1 29.5 %middle.1 = (bf16[8,64,768]{2,1,0:T(8,128)(2,1)}, bf16[8,64,768]{2,1,0:T(8,128)(2,1)}, bf16[64,768]{1,0:T(8,128)(2,1)}, f32[8,128]{1,0:T(8,128)}, f32[64,768]{1,...) custom-call(f32[8,64,768]{2,1,0:T(8,128)} %get-tuple-element.49.part_b, ...), custom_call_target="tpu_custom_call" | custom-call | tf_op jit(solution)/shard_map/middle/pallas_call | solution.py:591
  96.5 0.6 collective-permute-start
  97.1 2.3 %collective-permute-start.1 = (f32[64,768]{1,0:T(8,128)}, f32[64,768]{1,0:T(8,128)S(1)}, u32[]{:S(2)}, u32[]{:S(2)}) collective-permute-start(f32[64,768]{1,0:T(8,128)} %get-tuple-element.62), channel_id=1, source_target_pairs={{0,4},{1,5},{2,6},{3,7},{4,0},{5,1},{6,2},{7,3},{8,12},{9,13},{10,... | collective-permute-start | bytes 589832 | tf_op jit(solution)/shard_map/ppermute | solution.py:603
  99.4 0.2 collective-permute-start.2
  99.6 0.0 copy-start.1
  99.6 0.0 copy-start.2
  99.6 24.3 %backward.3 = (f32[16,768,256]{2,1,0:T(8,128)}, f32[16,768,256]{2,1,0:T(8,128)}, f32[16,256,768]{2,1,0:T(8,128)}, f32[8,64,768]{2,1,0:T(8,128)}, f32[8,8,128]{2,1,0:T(8,128)}) custom-call(bf16[8,64,768]{2,1,0:T(8,128)(2,1)} %get-tuple-element.51.x_all, bf16[8,64,768]{2,1,0:T(8,128)(2,1)} %get-tuple-element.52.dy_all, f32[16,8,128]{2,1,0:T(8,128)} %get-tuple-element.53.s_ref, ...), custom_call_target="tpu_custom_call" | custom-call | flops 7247757312 | bytes 56623104 | tf_op jit(solution)/shard_map/backward/pallas_call | solution.py:572
  123.9 0.0 collective-permute-done.left_x
  123.9 0.0 collective-permute-done.1.opp_x
  123.9 0.0 collective-permute-done.2.right_x
  123.9 0.0 copy-done.1
  123.9 0.0 copy-done.2
  124.0 0.0 copy-done.3
  124.0 0.0 copy-start
  124.0 1.4 copy-done
  125.4 0.8 copy-done.6
  126.1 12.5 %last.1 = (bf16[64,768]{1,0:T(8,128)(2,1)S(1)}, f32[8,128]{1,0:T(8,128)S(1)}, bf16[64,768]{1,0:T(8,128)(2,1)S(1)}) custom-call(f32[8,64,768]{2,1,0:T(8,128)S(1)} %copy-done, f32[8,8,128]{2,1,0:T(8,128)S(1)} %copy-done.6, bf16[64,768]{1,0:T(8,128)(2,1)S(1)} %copy-done.3, bf16[64,768]{1,0:T(8,128)(2,1)S(1)} %copy-done.2, f32[64,768]{1,0:T(8,128)S(1)} %copy-done.1, ...), custom_call_target="tpu_custom_call" | custom-call | tf_op jit(solution)/shard_map/last/pallas_call | solution.py:608
  138.6 0.0 copy-start.4
  138.6 0.6 copy-done.4
  139.2 0.6 copy-done.5
  139.9 0.6 copy-done.7
  140.5 1.6 %final.1 = (bf16[64,768]{1,0:T(8,128)(2,1)}, bf16[64,768]{1,0:T(8,128)(2,1)}, f32[8,64]{1,0:T(8,128)}, f32[8,64]{1,0:T(8,128)}) custom-call(bf16[64,768]{1,0:T(8,128)(2,1)} %copy-done.5, bf16[64,768]{1,0:T(8,128)(2,1)} %copy-done.4, f32[8,128]{1,0:T(8,128)} %copy-done.7, f32[8,128]{1,0:T(8,128)} %get-tuple-element.67.dgb_ref), custom_call_target="tpu_custom_call" | custom-call | tf_op jit(solution)/shard_map/final/pallas_call | solution.py:617
  (4 shorter events, 0.0 us)
Async XLA Ops:
  96.5 27.4 %collective-permute-start = (f32[64,768]{1,0:T(8,128)}, f32[64,768]{1,0:T(8,128)S(1)}, u32[]{:S(2)}, u32[]{:S(2)}) collective-permute-start(f32[64,768]{1,0:T(8,128)} %get-tuple-element.61), channel_id=1, source_target_pairs={{0,2},{1,3},{2,4},{3,5},{4,6},{5,7},{6,0},{7,1},{8,10},{9,11},{10,... | collective-permute-start | bytes 589832 | tf_op jit(solution)/shard_map/ppermute | solution.py:603
  97.1 26.8 %collective-permute-start.1 = (f32[64,768]{1,0:T(8,128)}, f32[64,768]{1,0:T(8,128)S(1)}, u32[]{:S(2)}, u32[]{:S(2)}) collective-permute-start(f32[64,768]{1,0:T(8,128)} %get-tuple-element.62), channel_id=1, source_target_pairs={{0,4},{1,5},{2,6},{3,7},{4,0},{5,1},{6,2},{7,3},{8,12},{9,13},{10,... | collective-permute-start | bytes 589832 | tf_op jit(solution)/shard_map/ppermute | solution.py:603
  99.4 24.5 %collective-permute-start.2 = (f32[64,768]{1,0:T(8,128)}, f32[64,768]{1,0:T(8,128)S(1)}, u32[]{:S(2)}, u32[]{:S(2)}) collective-permute-start(f32[64,768]{1,0:T(8,128)} %get-tuple-element.63), channel_id=1, source_target_pairs={{0,6},{1,7},{2,0},{3,1},{4,2},{5,3},{6,4},{7,5},{8,14},{9,15},{10,... | collective-permute-start | bytes 589832 | tf_op jit(solution)/shard_map/ppermute | solution.py:603
  99.6 24.4 %copy-start.1 = (f32[64,768]{1,0:T(8,128)S(1)}, f32[64,768]{1,0:T(8,128)}, u32[]{:S(2)}) copy-start(f32[64,768]{1,0:T(8,128)} %get-tuple-element.60.own_x) | copy-start | bytes 589828
  99.6 24.4 %copy-start.2 = (bf16[64,768]{1,0:T(8,128)(2,1)S(1)}, bf16[64,768]{1,0:T(8,128)(2,1)}, u32[]{:S(2)}) copy-start(bf16[64,768]{1,0:T(8,128)(2,1)} %get-tuple-element.59.mid_ref) | copy-start | bytes 294916
  99.6 24.4 %copy-start.3 = (bf16[64,768]{1,0:T(8,128)(2,1)S(1)}, bf16[64,768]{1,0:T(8,128)(2,1)}, u32[]{:S(2)}) copy-start(bf16[64,768]{1,0:T(8,128)(2,1)} %get-tuple-element.58.dmid_ref) | copy-start | bytes 294916
  124.0 1.4 copy-start
  125.4 0.8 copy-start.6
  138.6 0.6 copy-start.4
  139.2 0.6 copy-start.5
  139.9 0.6 copy-start.7

commit v5 on v4

--- a/solution.py
+++ b/solution.py
@@ -16,7 +16,7 @@
 GROUPED = 2
 FORWARD_GROUPED = 4
 VMEM_LIMIT = 60 * 1024 * 1024
-SMALL_VMEM_LIMIT = 16 * 1024 * 1024
+SMALL_VMEM_LIMIT = 8 * 1024 * 1024
 VMEM = pl.BlockSpec(memory_space=pltpu.VMEM)
 ANY = pl.BlockSpec(memory_space=pl.ANY)
 
@@ -27,10 +27,6 @@
 
 def mm_tn(lhs, rhs):
     return lax.dot_general(lhs, rhs, (((0,), (0,)), ((), ())), preferred_element_type=F32)
-
-
-def mm_nt(lhs, rhs):
-    return lax.dot_general(lhs, rhs, (((1,), (1,)), ((), ())), preferred_element_type=F32)
 
 
 def iota(shape, dim):
@@ -367,7 +363,8 @@
 
 def backward_kernel(dims, x_all, dy_all, s_ref, g_ref, rel_ref, w1, w3, w2,
                     dw1, dw3, dw2, part, dgate,
-                    u_ref, y_ref, du_ref, dg_ref, w1_v, w3_v, w2_v, dw1_v, dw3_v, dw2_v, w_sems, out_sems):
+                    u_ref, y_ref, du_ref, dg_ref, w1_v, w3_v, w2_v, w1_t, w3_t, w2_t, dw1_v, dw3_v, dw2_v, part_v,
+                    w_sems, out_sems, part_sems):
     n_dev, tok, width, local, cap, top_k = dims
     n_rows = n_dev * cap
     pairs = ((w1, w1_v), (w3, w3_v), (w2, w2_v))
@@ -393,6 +390,8 @@
         def _():
             for i in range(3):
                 store(g - 2, i, slot).wait()
+        for i, e in enumerate(experts):
+            w2_t[i] = w2_v[e].T
         u = [u_ref[:, e].reshape(n_rows, width) for e in experts]
         dy = [y_ref[:, e].reshape(n_rows, width) for e in experts]
         holds = [s_ref[e][:, None, :] == iota((n_dev, cap, LANES), 1).astype(F32) for e in experts]
@@ -400,7 +399,10 @@
                     for i, e in enumerate(experts)]
         q = [(gate_row[i] * dy[i].astype(F32)).astype(BF16) for i in each]
         pre = [(mm(u[i], w1_v[e]), mm(u[i], w3_v[e])) for i, e in enumerate(experts)]
-        d_hidden = [mm_nt(q[i], w2_v[e]) for i, e in enumerate(experts)]
+        for i, e in enumerate(experts):
+            w1_t[i] = w1_v[e].T
+            w3_t[i] = w3_v[e].T
+        d_hidden = [mm(q[i], w2_t[i]) for i in each]
         sig = [jax.nn.sigmoid(a) for a, _ in pre]
         act = [pre[i][0] * sig[i] for i in each]
         hidden = [(act[i] * pre[i][1]).astype(BF16) for i in each]
@@ -413,7 +415,7 @@
             dg_row = jnp.sum(dy[i].astype(F32) * out[i].astype(F32), axis=1, keepdims=True).reshape(n_dev, cap, 1)
             dg_ref[e] = jnp.sum(jnp.where(holds[i], dg_row, 0.0), axis=1)
         for i, e in enumerate(experts):
-            du = (mm_nt(d_gate[i], w1_v[e]) + mm_nt(d_up[i], w3_v[e])).astype(BF16)
+            du = (mm(d_gate[i], w1_t[i]) + mm(d_up[i], w3_t[i])).astype(BF16)
             du_ref[:, e] = du.reshape(n_dev, cap, width)
         for i in each:
             dw1_v[slot, i] = mm_tn(u[i], d_gate[i])
@@ -426,7 +428,8 @@
 
     stack = scatter_lhs(s_map, None, tok)
     for d in range(n_dev):
-        part[d] = token_sums(stack, d, du_ref[d].reshape(local * cap, width), tok, cap)
+        part_v[d] = token_sums(stack, d, du_ref[d].reshape(local * cap, width), tok, cap)
+        pltpu.make_async_copy(part_v.at[d], part.at[d], part_sems.at[d]).start()
     for d in range(n_dev):
         total = jnp.zeros((top_k, LANES), F32)
         for i in range(local):
@@ -435,18 +438,25 @@
     for g in (steps - 2, steps - 1):
         for i in range(3):
             store(g, i, g % 2).wait()
-
-
-def middle_kernel(dims, part_b, dg_part, dy_ref, x_ref, mid_all, sb, gb, w1, w3, w2,
-                  dmid_all, x_again, dmid_own, dgate, own_x, right_x, opp_x, left_x,
-                  part_x, near_x, d_all, x_all, u_ref, o_ref, near, mine, got, dg_near, dg_mine, dg_got, d_buf, w1_v, w3_v, w2_v,
+    for d in range(n_dev):
+        pltpu.make_async_copy(part_v.at[d], part.at[d], part_sems.at[d]).wait()
+
+
+def middle_kernel(dims, dg_part, dy_ref, x_ref, sb, gb, part_in, mid_in, w1, w3, w2,
+                  x_again, dmid_all, dmid_own, dgate, own_x, right_x, opp_x, left_x,
+                  part_b, mid_all, in_sems, part_x, near_x, d_all, x_all, u_ref, o_ref, near, mine, got, dg_near, dg_mine, dg_got, d_buf, w1_v, w3_v, w2_v,
                   w_sems, send_sems, recv_sems):
     n_dev, tok, width, local, cap, top_k = dims
     pairs = ((w1, w1_v), (w3, w3_v), (w2, w2_v))
+    part_load = pltpu.make_async_copy(part_in, part_b, in_sems.at[0])
+    mid_load = pltpu.make_async_copy(mid_in, mid_all, in_sems.at[1])
+    part_load.start()
+    mid_load.start()
     load_weights(pairs, w_sems, local)
     links = Links(n_dev, send_sems, recv_sems)
     me = links.me
     links.greet()
+    part_load.wait()
     red = Reduce(links, part_b, (near, mine, got))
     dg = Reduce(links, dg_part, (dg_near, dg_mine, dg_got), split=False)
     s_map = sb[...].reshape(local * n_dev, LANES)
@@ -458,6 +468,7 @@
     dg.start()
     x_g = Gather(links, x_ref, x_all)
     x_all[me] = x_ref[...]
+    mid_load.wait()
     for d in range(2):
         rows_of(d)
     red.far()
@@ -479,6 +490,9 @@
     d_g = Gather(links, d_buf, d_all)
     forward_experts(pairs, w_sems, u_ref, o_ref, cap, half, local)
     d_g.pass_on()
+    x_g.finish()
+    x_store = pltpu.make_async_copy(x_all, x_again, in_sems.at[2])
+    x_store.start()
     stack = scatter_lhs(s_map, gb[...].reshape(local * n_dev, LANES), tok)
     for d in range(n_dev):
         part_x[d % 2, d // 2] = token_sums(stack, d, o_ref[d].reshape(local * cap, width), tok, cap)
@@ -489,25 +503,28 @@
         chip = lax.rem((me - links.core) // 2 + hop, n_dev // 2)
         out[...] = part_x[links.core, chip] + near_x[chip]
     dgate[...] = dg.result()
-    x_g.finish()
-    x_again[...] = x_all[...]
     d_g.finish()
     dmid_all[...] = d_all[...]
+    x_store.wait()
     links.drain()
 
 
-def final_kernel(x_ref, dx_ref, dga_ref, dgb_ref, x_out, dx_out, dga_out, dgb_out):
-    x_out[...] = x_ref[...]
+def final_kernel(mid_ref, own_x, left_x, opp_x, right_x, dx_ref, dga_ref, dgb_ref, x_out, dx_out, dga_out, dgb_out):
+    total = own_x[...] + left_x[...] + opp_x[...] + right_x[...]
+    x_out[...] = (mid_ref[...].astype(F32) + total).astype(BF16)
     dx_out[...] = dx_ref[...]
     tok = dga_out.shape[1]
     dga_out[...] = dga_ref[:, :tok]
     dgb_out[...] = dgb_ref[:, :tok]
 
 
-def last_kernel(dims, part_a, dg_part, dmid_ref, mid_ref, own_x, left_x, opp_x, right_x, dx_out, dgate, x_out,
-                near, mine, got, dg_near, dg_mine, dg_got, send_sems, recv_sems):
+def last_kernel(dims, dg_part, dmid_ref, part_in, dx_out, dgate,
+                part_a, in_sem, near, mine, got, dg_near, dg_mine, dg_got, send_sems, recv_sems):
+    part_load = pltpu.make_async_copy(part_in, part_a, in_sem.at[0])
+    part_load.start()
     links = Links(dims[0], send_sems, recv_sems)
     links.greet()
+    part_load.wait()
     red = Reduce(links, part_a, (near, mine, got))
     dg = Reduce(links, dg_part, (dg_near, dg_mine, dg_got), split=False)
     red.start()
@@ -516,8 +533,6 @@
     red.near_sends()
     dg.far()
     dg.near_sends()
-    total = own_x[...] + left_x[...] + opp_x[...] + right_x[...]
-    x_out[...] = (mid_ref[...].astype(F32) + total).astype(BF16)
     red.relay()
     dg.relay()
     dx_out[...] = (dmid_ref[...].astype(F32) + red.result()).astype(BF16)
@@ -525,8 +540,8 @@
     links.drain()
 
 
-def remote_params(ident, limit=VMEM_LIMIT):
-    return pltpu.CompilerParams(collective_id=ident, has_side_effects=True, vmem_limit_bytes=limit)
+def remote_params(ident):
+    return pltpu.CompilerParams(collective_id=ident, has_side_effects=True, vmem_limit_bytes=VMEM_LIMIT)
 
 
 def dma_sems(count):
@@ -568,16 +583,20 @@
             compiler_params=remote_params(0), name="first",
         )(x_in, dy_out, idx_a.T, gate_a.T, idx_b.T, gate_b.T, w1_a, w3_a, w2_a)
 
+        part_v = pltpu.VMEM((n_dev, tok, width), F32)
+
         def backward(x_all, d_all, s, g, rel, w1, w3, w2):
             return pl.pallas_call(
                 functools.partial(backward_kernel, dims),
                 out_shape=(sds((local, width, inner), F32), sds((local, width, inner), F32),
                            sds((local, inner, width), F32), part_all, dg_all),
                 in_specs=[VMEM] * 5 + [ANY] * 3,
-                out_specs=[ANY] * 3 + [VMEM] * 2,
+                out_specs=[ANY] * 4 + [VMEM],
                 scratch_shapes=[expert_v, expert_v, expert_v, pltpu.VMEM((local, n_dev, LANES), F32), *weights_v,
+                                *[pltpu.VMEM((GROUPED, inner, width), BF16)] * 2, pltpu.VMEM((GROUPED, width, inner), BF16),
                                 *[pltpu.VMEM((2, GROUPED, width, inner), F32)] * 2,
-                                pltpu.VMEM((2, GROUPED, inner, width), F32), w_sems, pltpu.SemaphoreType.DMA((3, 2))],
+                                pltpu.VMEM((2, GROUPED, inner, width), F32), part_v, w_sems,
+                                pltpu.SemaphoreType.DMA((3, 2)), pltpu.SemaphoreType.DMA((n_dev,))],
                 compiler_params=pltpu.CompilerParams(vmem_limit_bytes=VMEM_LIMIT), name="backward",
                 cost_estimate=pl.CostEstimate(flops=18 * local * n_dev * cap * width * inner, transcendentals=0,
                                               bytes_accessed=18 * local * width * inner),
@@ -588,16 +607,17 @@
         count = 2 * Gather.COPIES + 2 * Reduce.COPIES + 1
         sums = sds((tok, width), F32)
         chip_sums = pltpu.VMEM((n_dev // 2, tok, width), F32)
-        dmid_all, x_again, dmid_own, dgate_b, own_x, right_x, opp_x, left_x = pl.pallas_call(
+        x_again, dmid_all, dmid_own, dgate_b, own_x, right_x, opp_x, left_x = pl.pallas_call(
             functools.partial(middle_kernel, dims),
             out_shape=(rows_all, rows_all, own, sds((top_k, LANES), F32), sums, sums, sums, sums),
-            in_specs=[VMEM] * 7 + [ANY] * 3,
-            out_specs=[VMEM] * 8,
-            scratch_shapes=[pltpu.VMEM((2, n_dev // 2, tok, width), F32), chip_sums, rows_v, rows_v, expert_v, expert_v,
+            in_specs=[VMEM] * 5 + [ANY] * 5,
+            out_specs=[ANY] + [VMEM] * 7,
+            scratch_shapes=[part_v, rows_v, pltpu.SemaphoreType.DMA((3,)),
+                            pltpu.VMEM((2, n_dev // 2, tok, width), F32), chip_sums, rows_v, rows_v, expert_v, expert_v,
                             *Reduce.scratch(tok, width), *Reduce.scratch(top_k, LANES), pltpu.VMEM((tok, width), BF16),
                             *weights_v, w_sems, *dma_sems(count)],
             compiler_params=remote_params(1), name="middle",
-        )(part_b, dg_b, dy_out, x_in, mid_all, sb, gb, w1_b, w3_b, w2_b)
+        )(dg_b, dy_out, x_in, sb, gb, part_b, mid_all, w1_b, w3_b, w2_b)
 
         def shift(rows, hop):
             return lax.ppermute(rows, "ep", [(i, (i + 2 * hop) % n_dev) for i in range(n_dev)])
@@ -605,18 +625,20 @@
         left_x, opp_x, right_x = shift(right_x, 1), shift(opp_x, 2), shift(left_x, 3)
         *grads_a, part_a, dg_a = backward(x_again, dmid_all, sa, ga, rela, w1_a, w3_a, w2_a)
 
-        dx_in, dgate_a, x_out = pl.pallas_call(
+        dx_in, dgate_a = pl.pallas_call(
             functools.partial(last_kernel, dims),
-            out_shape=(own, sds((top_k, LANES), F32), own),
-            in_specs=[VMEM] * 8,
-            out_specs=[VMEM] * 3,
-            scratch_shapes=[*Reduce.scratch(tok, width), *Reduce.scratch(top_k, LANES), *dma_sems(2 * Reduce.COPIES)],
-            compiler_params=remote_params(2, SMALL_VMEM_LIMIT), name="last",
-        )(part_a, dg_a, dmid_own, mid_own, own_x, left_x, opp_x, right_x)
+            out_shape=(own, sds((top_k, LANES), F32)),
+            in_specs=[VMEM] * 2 + [ANY],
+            out_specs=[VMEM] * 2,
+            scratch_shapes=[part_v, pltpu.SemaphoreType.DMA((1,)), *Reduce.scratch(tok, width),
+                            *Reduce.scratch(top_k, LANES), *dma_sems(2 * Reduce.COPIES)],
+            compiler_params=remote_params(2), name="last",
+        )(dg_a, dmid_own, part_a)
         gates = sds((top_k, tok), F32)
         x_out, dx_in, dgate_a, dgate_b = pl.pallas_call(
-            final_kernel, out_shape=(own, own, gates, gates), in_specs=[VMEM] * 4, out_specs=[VMEM] * 4, name="final",
-        )(x_out, dx_in, dgate_a, dgate_b)
+            final_kernel, out_shape=(own, own, gates, gates), in_specs=[VMEM] * 8, out_specs=[VMEM] * 4, name="final",
+            compiler_params=pltpu.CompilerParams(vmem_limit_bytes=SMALL_VMEM_LIMIT),
+        )(mid_own, own_x, left_x, opp_x, right_x, dx_in, dgate_a, dgate_b)
         return (x_out, dx_in, *grads_a, *grads_b, dgate_a.T, dgate_b.T)
 
     return jax.shard_map(device_program, mesh=mesh, in_specs=(tok_spec,) * 6 + (w_spec,) * 6, out_specs=(tok_spec,) * 10, check_vma=False)

time: 142 us -> 136 us (0.958)
  Pallas kernels: 134 us -> 130 us
  local copies, waits for them, and re-layouts: 4.03 us -> 1.58 us
    pallas_call x2, Pallas kernels: 48.5 us -> 44.8 us  [backward(): pl.pallas_call(functools.partial(backward_kernel, dims), out_shape=(sds((...]
    unnamed x16 -> x10, local copies, waits for them, and re-layouts: 4.03 us -> 1.58 us
    pallas_call x1, Pallas kernels: 12.5 us -> 14.2 us  [device_program(): pl.pallas_call(functools.partial(last_kernel, dims), out_shape=(own, sds(...]
  transfers between devices with their start and end apart: 3 -> 3, of which waited for: 0 -> 0; matrix products, arithmetic and copies ran while one was open for 0% -> 0% of each run, Pallas kernels for 17% -> 27%
where the time goes in v5:
time: 136 us
  Pallas kernels  130 us (96%)
  starting transfers between devices  3.15 us (2%)
  local copies, waits for them, and re-layouts  1.58 us (1%)
    pallas_call x2, Pallas kernels, backward(): pl.pallas_call(functools.partial(backward_kernel, dims), out_shape=(sds((...  44.8 us
    pallas_call x1, Pallas kernels, device_program(): pl.pallas_call(functools.partial(first_kernel, dims), out_shape=(rows_all...  42.2 us
    pallas_call x1, Pallas kernels, device_program(): pl.pallas_call(functools.partial(middle_kernel, dims), out_shape=(rows_al...  28.4 us
    pallas_call x1, Pallas kernels, device_program(): pl.pallas_call(functools.partial(last_kernel, dims), out_shape=(own, sds(...  14.2 us
    ppermute x3, starting transfers between devices, shift(): lax.ppermute(rows, 'ep', [(i, (i + 2 * hop) % n_dev) for i in range(n_dev)])  3.15 us
  transfers between devices with their start and end apart: 3, of which 0 were waited for; matrix products, arithmetic and copies ran while one was open for 0% of the time, Pallas kernels for 27%

profile of v5, /device:TPU:113, one launch (start us, length us, event | category | flops | bytes accessed | tf_op | source)
XLA Modules:
  0.0 135.7 jit_solution(5271764774165552328)
XLA Ops:
  0.6 42.2 %first.1 = (bf16[8,64,768]{2,1,0:T(8,128)(2,1)}, bf16[8,64,768]{2,1,0:T(8,128)(2,1)}, bf16[64,768]{1,0:T(8,128)(2,1)}, f32[16,8,128]{2,1,0:T(8,128)}, f32[16,8,1...) custom-call(bf16[64,768]{1,0:T(8,128)(2,1)} %x_ref.3, ...), custom_call_target="tpu_custom_call" | custom-call | tf_op jit(solution)/shard_map/first/pallas_call | solution.py:575
  42.8 22.4 %backward.2 = (f32[16,768,256]{2,1,0:T(8,128)}, f32[16,768,256]{2,1,0:T(8,128)}, f32[16,256,768]{2,1,0:T(8,128)}, f32[8,64,768]{2,1,0:T(8,128)}, f32[8,8,128]{2,1,0:T(8,128)}) custom-call(bf16[8,64,768]{2,1,0:T(8,128)(2,1)} %get-tuple-element.44.x_all.mid_in, bf16[8,64,768]{2,1,0:T(8,128)(2,1)} %get-tuple-element.45.dy_all, ...), custom_call_target="tpu_custom_call" | custom-call | flops 7247757312 | bytes 56623104 | tf_op jit(solution)/shard_map/backward/pallas_call | solution.py:589
  65.2 28.4 %middle.1 = (bf16[8,64,768]{2,1,0:T(8,128)(2,1)}, bf16[8,64,768]{2,1,0:T(8,128)(2,1)}, bf16[64,768]{1,0:T(8,128)(2,1)}, f32[8,128]{1,0:T(8,128)}, f32[64,768]{1,...) custom-call(f32[8,8,128]{2,1,0:T(8,128)} %get-tuple-element.49.dg_part, ...), custom_call_target="tpu_custom_call" | custom-call | tf_op jit(solution)/shard_map/middle/pallas_call | solution.py:610
  93.6 0.6 collective-permute-start
  94.2 2.3 %collective-permute-start.1 = (f32[64,768]{1,0:T(8,128)}, f32[64,768]{1,0:T(8,128)S(1)}, u32[]{:S(2)}, u32[]{:S(2)}) collective-permute-start(f32[64,768]{1,0:T(8,128)} %get-tuple-element.53), channel_id=1, source_target_pairs={{0,4},{1,5},{2,6},{3,7},{4,0},{5,1},{6,2},{7,3},{8,12},{9,13},{10,... | collective-permute-start | bytes 589832 | tf_op jit(solution)/shard_map/ppermute | solution.py:623
  96.5 0.3 collective-permute-start.2
  96.8 0.0 copy-start
  96.8 0.0 copy-start.1
  96.8 0.0 copy-start.3
  96.8 22.4 %backward.3 = (f32[16,768,256]{2,1,0:T(8,128)}, f32[16,768,256]{2,1,0:T(8,128)}, f32[16,256,768]{2,1,0:T(8,128)}, f32[8,64,768]{2,1,0:T(8,128)}, f32[8,8,128]{2,1,0:T(8,128)}) custom-call(bf16[8,64,768]{2,1,0:T(8,128)(2,1)} %get-tuple-element.55.x_all, bf16[8,64,768]{2,1,0:T(8,128)(2,1)} %get-tuple-element.56.dy_all, f32[16,8,128]{2,1,0:T(8,128)} %get-tuple-element.57.s_ref, ...), custom_call_target="tpu_custom_call" | custom-call | flops 7247757312 | bytes 56623104 | tf_op jit(solution)/shard_map/backward/pallas_call | solution.py:589
  119.2 14.2 %last.1 = (bf16[64,768]{1,0:T(8,128)(2,1)}, f32[8,128]{1,0:T(8,128)}) custom-call(f32[8,8,128]{2,1,0:T(8,128)} %get-tuple-element.60.dg_part, bf16[64,768]{1,0:T(8,128)(2,1)} %get-tuple-element.61.dmid_ref, f32[8,64,768]{2,1,0:T(8,128)} %get-tuple-element.62.part_in), custom_call_target="tpu_custom_call" | custom-call | tf_op jit(solution)/shard_map/last/pallas_call | solution.py:628
  133.3 0.0 collective-permute-done.left_x
  133.3 0.0 collective-permute-done.1.opp_x
  133.3 0.0 collective-permute-done.2.right_x
  133.4 0.0 copy-done
  133.4 0.0 copy-done.1
  133.4 0.0 copy-done.3
  133.4 0.0 copy-start.2
  133.4 0.9 copy-done.2
  134.3 0.0 copy-start.4
  134.3 0.7 copy-done.4
  135.0 0.7 final.1
Async XLA Ops:
  93.6 39.7 %collective-permute-start = (f32[64,768]{1,0:T(8,128)}, f32[64,768]{1,0:T(8,128)S(1)}, u32[]{:S(2)}, u32[]{:S(2)}) collective-permute-start(f32[64,768]{1,0:T(8,128)} %get-tuple-element.52), channel_id=1, source_target_pairs={{0,2},{1,3},{2,4},{3,5},{4,6},{5,7},{6,0},{7,1},{8,10},{9,11},{10,... | collective-permute-start | bytes 589832 | tf_op jit(solution)/shard_map/ppermute | solution.py:623
  94.2 39.2 %collective-permute-start.1 = (f32[64,768]{1,0:T(8,128)}, f32[64,768]{1,0:T(8,128)S(1)}, u32[]{:S(2)}, u32[]{:S(2)}) collective-permute-start(f32[64,768]{1,0:T(8,128)} %get-tuple-element.53), channel_id=1, source_target_pairs={{0,4},{1,5},{2,6},{3,7},{4,0},{5,1},{6,2},{7,3},{8,12},{9,13},{10,... | collective-permute-start | bytes 589832 | tf_op jit(solution)/shard_map/ppermute | solution.py:623
  96.5 36.9 %collective-permute-start.2 = (f32[64,768]{1,0:T(8,128)}, f32[64,768]{1,0:T(8,128)S(1)}, u32[]{:S(2)}, u32[]{:S(2)}) collective-permute-start(f32[64,768]{1,0:T(8,128)} %get-tuple-element.54), channel_id=1, source_target_pairs={{0,6},{1,7},{2,0},{3,1},{4,2},{5,3},{6,4},{7,5},{8,14},{9,15},{10,... | collective-permute-start | bytes 589832 | tf_op jit(solution)/shard_map/ppermute | solution.py:623
  96.8 36.6 %copy-start = (f32[64,768]{1,0:T(8,128)S(1)}, f32[64,768]{1,0:T(8,128)}, u32[]{:S(2)}) copy-start(f32[64,768]{1,0:T(8,128)} %get-tuple-element.51.own_x) | copy-start | bytes 589828
  96.8 36.6 %copy-start.1 = (bf16[64,768]{1,0:T(8,128)(2,1)S(1)}, bf16[64,768]{1,0:T(8,128)(2,1)}, u32[]{:S(2)}) copy-start(bf16[64,768]{1,0:T(8,128)(2,1)} %get-tuple-element.43.mid_ref) | copy-start | bytes 294916
  96.8 36.6 %copy-start.3 = (f32[8,128]{1,0:T(8,128)S(1)}, f32[8,128]{1,0:T(8,128)}, u32[]{:S(2)}) copy-start(f32[8,128]{1,0:T(8,128)} %get-tuple-element.65.dgb_ref) | copy-start | bytes 12292
  133.4 0.9 copy-start.2
  134.3 0.7 copy-start.4

commit v6 on v5

--- a/solution.py
+++ b/solution.py
@@ -15,10 +15,10 @@
 BF16_MAX = 3.3895313892515355e38
 GROUPED = 2
 FORWARD_GROUPED = 4
-VMEM_LIMIT = 60 * 1024 * 1024
-SMALL_VMEM_LIMIT = 8 * 1024 * 1024
+MIB = 1024 * 1024
+ALL_VMEM = 64 * MIB - 64 * 1024
 VMEM = pl.BlockSpec(memory_space=pltpu.VMEM)
-ANY = pl.BlockSpec(memory_space=pl.ANY)
+HBM = pl.BlockSpec(memory_space=pltpu.HBM)
 
 
 def mm(lhs, rhs):
@@ -268,15 +268,15 @@
         pltpu.make_async_copy(src.at[e], dst.at[e], sems.at[i, e]).wait()
 
 
-def forward_experts(pairs, sems, u_ref, o_ref, cap, first, last):
+def forward_experts(weights, ready, u_ref, o_ref, cap, first, last):
     n_dev, _, _, width = u_ref.shape
     few = min(FORWARD_GROUPED, last - first)
 
     def step(g, carry):
         experts = [first + g * few + i for i in range(few)]
         for e in experts:
-            wait_weights(pairs, sems, e)
-        w_gate, w_up, w_down = (dst for _, dst in pairs)
+            ready(e)
+        w_gate, w_up, w_down = weights
         rows = [u_ref[:, e].reshape(n_dev * cap, width) for e in experts]
         pre = [(mm(u, w_gate[e]), mm(u, w_up[e])) for u, e in zip(rows, experts)]
         hidden = [(gate * jax.nn.sigmoid(gate) * up).astype(BF16) for gate, up in pre]
@@ -287,9 +287,9 @@
 
 
 def first_kernel(dims, x_ref, dy_ref, idx_a, gate_a, idx_b, gate_b, w1, w3, w2,
-                 mid_all, dy_all, mid_own, sa, ga, rela, sb, gb, relb,
+                 dy_all, mid_all, mid_own, sa, ga, rela, sb, gb, relb,
                  x_all, y_all, m_all, meta_ref, meta_all, u_ref, o_ref, part, near, mine, got, mid_buf, w1_v, w3_v, w2_v,
-                 w_sems, send_sems, recv_sems):
+                 w_sems, out_sem, send_sems, recv_sems):
     n_dev, tok, width, local, cap, top_k = dims
     pairs = ((w1, w1_v), (w3, w3_v), (w2, w2_v))
     load_weights(pairs, w_sems, local)
@@ -311,7 +311,6 @@
     meta_g.finish()
     meta = meta_all[...]
     routing_maps(me, meta, 0, sa, ga, rela, top_k, local)
-    routing_maps(me, meta, 1, sb, gb, relb, top_k, local)
     s_map = sa[...].reshape(local * n_dev, LANES)
 
     def rows_of(d):
@@ -329,9 +328,10 @@
     rows_of(links.right + side)
     rows_of(links.opp)
     y_g.pass_on()
+    routing_maps(me, meta, 1, sb, gb, relb, top_k, local)
     x_g.wait_last()
     rows_of(links.opp + side)
-    forward_experts(pairs, w_sems, u_ref, o_ref, cap, 0, local)
+    forward_experts((w1_v, w3_v, w2_v), lambda e: wait_weights(pairs, w_sems, e), u_ref, o_ref, cap, 0, local)
     y_g.pass_far()
     stack = scatter_lhs(s_map, ga[...].reshape(local * n_dev, LANES), tok)
     red = Reduce(links, part, (near, mine, got))
@@ -339,14 +339,21 @@
     def sums_of(d):
         part[d] = token_sums(stack, d, o_ref[d].reshape(local * cap, width), tok, cap)
 
-    for hop in (2, 1, 3, 0):
+    sums_of(red.block(2, 1 - links.core))
+    red.start_side(2)
+    sums_of(red.block(2, links.core))
+    for hop in (1, 3, 0):
         sums_of(red.block(hop, 1 - links.core))
         red.start_side(hop)
-    for hop in (2, 1, 3, 0):
-        sums_of(red.block(hop, links.core))
     red.far()
+    sums_of(red.block(1, links.core))
+    sums_of(red.block(3, links.core))
     red.near_sends()
+    sums_of(red.block(0, links.core))
     red.relay()
+    y_g.finish()
+    y_store = pltpu.make_async_copy(y_all, dy_all, out_sem.at[0])
+    y_store.start()
     x_mid = (x_ref[...].astype(F32) + red.result()).astype(BF16)
     mid_buf[...] = x_mid
     mid_own[...] = x_mid
@@ -354,22 +361,21 @@
     m_g = Gather(links, mid_buf, m_all)
     m_g.pass_on()
     m_g.pass_far()
-    y_g.finish()
-    dy_all[...] = y_all[...]
     m_g.finish()
     mid_all[...] = m_all[...]
+    y_store.wait()
     links.drain()
 
 
 def backward_kernel(dims, x_all, dy_all, s_ref, g_ref, rel_ref, w1, w3, w2,
                     dw1, dw3, dw2, part, dgate,
-                    u_ref, y_ref, du_ref, dg_ref, w1_v, w3_v, w2_v, w1_t, w3_t, w2_t, dw1_v, dw3_v, dw2_v, part_v,
+                    u_ref, y_ref, dg_ref, w1_v, w3_v, w2_v, w1_t, w3_t, w2_t, dw1_v, dw3_v, dw2_v, part_v,
                     w_sems, out_sems, part_sems):
     n_dev, tok, width, local, cap, top_k = dims
+    pairs = ((w1, w1_v), (w3, w3_v), (w2, w2_v))
+    load_weights(pairs, w_sems, local)
     n_rows = n_dev * cap
-    pairs = ((w1, w1_v), (w3, w3_v), (w2, w2_v))
     outs = ((dw1_v, dw1), (dw3_v, dw3), (dw2_v, dw2))
-    load_weights(pairs, w_sems, local)
     s_map = s_ref[...].reshape(local * n_dev, LANES)
 
     for d in range(n_dev):
@@ -416,7 +422,7 @@
             dg_ref[e] = jnp.sum(jnp.where(holds[i], dg_row, 0.0), axis=1)
         for i, e in enumerate(experts):
             du = (mm(d_gate[i], w1_t[i]) + mm(d_up[i], w3_t[i])).astype(BF16)
-            du_ref[:, e] = du.reshape(n_dev, cap, width)
+            y_ref[:, e] = du.reshape(n_dev, cap, width)
         for i in each:
             dw1_v[slot, i] = mm_tn(u[i], d_gate[i])
             dw3_v[slot, i] = mm_tn(u[i], d_up[i])
@@ -428,7 +434,7 @@
 
     stack = scatter_lhs(s_map, None, tok)
     for d in range(n_dev):
-        part_v[d] = token_sums(stack, d, du_ref[d].reshape(local * cap, width), tok, cap)
+        part_v[d] = token_sums(stack, d, y_ref[d].reshape(local * cap, width), tok, cap)
         pltpu.make_async_copy(part_v.at[d], part.at[d], part_sems.at[d]).start()
     for d in range(n_dev):
         total = jnp.zeros((top_k, LANES), F32)
@@ -444,7 +450,7 @@
 
 def middle_kernel(dims, dg_part, dy_ref, x_ref, sb, gb, part_in, mid_in, w1, w3, w2,
                   x_again, dmid_all, dmid_own, dgate, own_x, right_x, opp_x, left_x,
-                  part_b, mid_all, in_sems, part_x, near_x, d_all, x_all, u_ref, o_ref, near, mine, got, dg_near, dg_mine, dg_got, d_buf, w1_v, w3_v, w2_v,
+                  part_b, mid_all, in_sems, part_x, near_x, d_all, x_all, u_ref, near, mine, got, dg_near, dg_mine, dg_got, d_buf, w1_v, w3_v, w2_v,
                   w_sems, send_sems, recv_sems):
     n_dev, tok, width, local, cap, top_k = dims
     pairs = ((w1, w1_v), (w3, w3_v), (w2, w2_v))
@@ -466,8 +472,6 @@
 
     red.start()
     dg.start()
-    x_g = Gather(links, x_ref, x_all)
-    x_all[me] = x_ref[...]
     mid_load.wait()
     for d in range(2):
         rows_of(d)
@@ -477,27 +481,29 @@
     dg.near_sends()
     for d in range(2, n_dev):
         rows_of(d)
-    x_g.pass_on()
     red.relay()
     dg.relay()
+    x_g = Gather(links, x_ref, x_all)
+    x_all[me] = x_ref[...]
     half = local // 2 // FORWARD_GROUPED * FORWARD_GROUPED
-    forward_experts(pairs, w_sems, u_ref, o_ref, cap, 0, half)
-    x_g.pass_far()
+    forward_experts((w1_v, w3_v, w2_v), lambda e: wait_weights(pairs, w_sems, e), u_ref, u_ref, cap, 0, half)
     dx = (dy_ref[...].astype(F32) + red.result()).astype(BF16)
     d_buf[...] = dx
     dmid_own[...] = dx
     d_all[me] = dx
     d_g = Gather(links, d_buf, d_all)
-    forward_experts(pairs, w_sems, u_ref, o_ref, cap, half, local)
+    x_g.pass_on()
+    forward_experts((w1_v, w3_v, w2_v), lambda e: wait_weights(pairs, w_sems, e), u_ref, u_ref, cap, half, local)
     d_g.pass_on()
+    x_g.pass_far()
+    stack = scatter_lhs(s_map, gb[...].reshape(local * n_dev, LANES), tok)
+    for d in range(n_dev):
+        part_x[d % 2, d // 2] = token_sums(stack, d, u_ref[d].reshape(local * cap, width), tok, cap)
+    side_x = links.copy(part_x.at[1 - links.core], near_x, links.partner)
+    d_g.pass_far()
     x_g.finish()
     x_store = pltpu.make_async_copy(x_all, x_again, in_sems.at[2])
     x_store.start()
-    stack = scatter_lhs(s_map, gb[...].reshape(local * n_dev, LANES), tok)
-    for d in range(n_dev):
-        part_x[d % 2, d // 2] = token_sums(stack, d, o_ref[d].reshape(local * cap, width), tok, cap)
-    side_x = links.copy(part_x.at[1 - links.core], near_x, links.partner)
-    d_g.pass_far()
     side_x.wait_recv()
     for hop, out in enumerate((own_x, right_x, opp_x, left_x)):
         chip = lax.rem((me - links.core) // 2 + hop, n_dev // 2)
@@ -541,7 +547,7 @@
 
 
 def remote_params(ident):
-    return pltpu.CompilerParams(collective_id=ident, has_side_effects=True, vmem_limit_bytes=VMEM_LIMIT)
+    return pltpu.CompilerParams(collective_id=ident, has_side_effects=True, vmem_limit_bytes=ALL_VMEM)
 
 
 def dma_sems(count):
@@ -572,14 +578,14 @@
         expert_v = pltpu.VMEM((n_dev, local, cap, width), BF16)
 
         count = 4 * Gather.COPIES + Reduce.COPIES
-        mid_all, dy_all, mid_own, sa, ga, rela, sb, gb, relb = pl.pallas_call(
+        dy_all, mid_all, mid_own, sa, ga, rela, sb, gb, relb = pl.pallas_call(
             functools.partial(first_kernel, dims),
             out_shape=(rows_all, rows_all, own, map_s, map_s, dg_all, map_s, map_s, dg_all),
-            in_specs=[VMEM] * 6 + [ANY] * 3,
-            out_specs=[VMEM] * 9,
+            in_specs=[VMEM] * 6 + [HBM] * 3,
+            out_specs=[HBM] + [VMEM] * 8,
             scratch_shapes=[rows_v, rows_v, rows_v, pltpu.VMEM((4 * top_k, LANES), F32), pltpu.VMEM((n_dev, 4 * top_k, LANES), F32), expert_v, expert_v,
                             pltpu.VMEM((n_dev, tok, width), F32), *Reduce.scratch(tok, width),
-                            pltpu.VMEM((tok, width), BF16), *weights_v, w_sems, *dma_sems(count)],
+                            pltpu.VMEM((tok, width), BF16), *weights_v, w_sems, pltpu.SemaphoreType.DMA((1,)), *dma_sems(count)],
             compiler_params=remote_params(0), name="first",
         )(x_in, dy_out, idx_a.T, gate_a.T, idx_b.T, gate_b.T, w1_a, w3_a, w2_a)
 
@@ -590,14 +596,14 @@
                 functools.partial(backward_kernel, dims),
                 out_shape=(sds((local, width, inner), F32), sds((local, width, inner), F32),
                            sds((local, inner, width), F32), part_all, dg_all),
-                in_specs=[VMEM] * 5 + [ANY] * 3,
-                out_specs=[ANY] * 4 + [VMEM],
-                scratch_shapes=[expert_v, expert_v, expert_v, pltpu.VMEM((local, n_dev, LANES), F32), *weights_v,
+                in_specs=[VMEM] * 5 + [HBM] * 3,
+                out_specs=[HBM] * 4 + [VMEM],
+                scratch_shapes=[expert_v, expert_v, pltpu.VMEM((local, n_dev, LANES), F32), *weights_v,
                                 *[pltpu.VMEM((GROUPED, inner, width), BF16)] * 2, pltpu.VMEM((GROUPED, width, inner), BF16),
                                 *[pltpu.VMEM((2, GROUPED, width, inner), F32)] * 2,
                                 pltpu.VMEM((2, GROUPED, inner, width), F32), part_v, w_sems,
                                 pltpu.SemaphoreType.DMA((3, 2)), pltpu.SemaphoreType.DMA((n_dev,))],
-                compiler_params=pltpu.CompilerParams(vmem_limit_bytes=VMEM_LIMIT), name="backward",
+                compiler_params=pltpu.CompilerParams(vmem_limit_bytes=ALL_VMEM), name="backward",
                 cost_estimate=pl.CostEstimate(flops=18 * local * n_dev * cap * width * inner, transcendentals=0,
                                               bytes_accessed=18 * local * width * inner),
             )(x_all, d_all, s, g, rel, w1, w3, w2)
@@ -610,10 +616,10 @@
         x_again, dmid_all, dmid_own, dgate_b, own_x, right_x, opp_x, left_x = pl.pallas_call(
             functools.partial(middle_kernel, dims),
             out_shape=(rows_all, rows_all, own, sds((top_k, LANES), F32), sums, sums, sums, sums),
-            in_specs=[VMEM] * 5 + [ANY] * 5,
-            out_specs=[ANY] + [VMEM] * 7,
+            in_specs=[VMEM] * 5 + [HBM] * 5,
+            out_specs=[HBM] + [VMEM] * 7,
             scratch_shapes=[part_v, rows_v, pltpu.SemaphoreType.DMA((3,)),
-                            pltpu.VMEM((2, n_dev // 2, tok, width), F32), chip_sums, rows_v, rows_v, expert_v, expert_v,
+                            pltpu.VMEM((2, n_dev // 2, tok, width), F32), chip_sums, rows_v, rows_v, expert_v,
                             *Reduce.scratch(tok, width), *Reduce.scratch(top_k, LANES), pltpu.VMEM((tok, width), BF16),
                             *weights_v, w_sems, *dma_sems(count)],
             compiler_params=remote_params(1), name="middle",
@@ -628,7 +634,7 @@
         dx_in, dgate_a = pl.pallas_call(
             functools.partial(last_kernel, dims),
             out_shape=(own, sds((top_k, LANES), F32)),
-            in_specs=[VMEM] * 2 + [ANY],
+            in_specs=[VMEM] * 2 + [HBM],
             out_specs=[VMEM] * 2,
             scratch_shapes=[part_v, pltpu.SemaphoreType.DMA((1,)), *Reduce.scratch(tok, width),
                             *Reduce.scratch(top_k, LANES), *dma_sems(2 * Reduce.COPIES)],
@@ -637,7 +643,7 @@
         gates = sds((top_k, tok), F32)
         x_out, dx_in, dgate_a, dgate_b = pl.pallas_call(
             final_kernel, out_shape=(own, own, gates, gates), in_specs=[VMEM] * 8, out_specs=[VMEM] * 4, name="final",
-            compiler_params=pltpu.CompilerParams(vmem_limit_bytes=SMALL_VMEM_LIMIT),
+            compiler_params=pltpu.CompilerParams(vmem_limit_bytes=60 * MIB),
         )(mid_own, own_x, left_x, opp_x, right_x, dx_in, dgate_a, dgate_b)
         return (x_out, dx_in, *grads_a, *grads_b, dgate_a.T, dgate_b.T)
 

time: 136 us -> 135 us (level)
  local copies, waits for them, and re-layouts: 1.58 us -> 0 us
    unnamed x10 -> x0, local copies, waits for them, and re-layouts: 1.58 us -> none
where the time goes in v6:
time: 135 us
  Pallas kernels  130 us (96%)
  starting transfers between devices  4.06 us (3%)
    pallas_call x2, Pallas kernels, backward(): pl.pallas_call(functools.partial(backward_kernel, dims), out_shape=(sds((...  44.7 us
    pallas_call x1, Pallas kernels, device_program(): pl.pallas_call(functools.partial(first_kernel, dims), out_shape=(rows_all...  41.4 us
    pallas_call x1, Pallas kernels, device_program(): pl.pallas_call(functools.partial(middle_kernel, dims), out_shape=(rows_al...  28 us
    pallas_call x1, Pallas kernels, device_program(): pl.pallas_call(functools.partial(last_kernel, dims), out_shape=(own, sds(...  13.7 us
    ppermute x3, starting transfers between devices, shift(): lax.ppermute(rows, 'ep', [(i, (i + 2 * hop) % n_dev) for i in range(n_dev)])  4.06 us
  transfers between devices with their start and end apart: 3, of which 0 were waited for; matrix products, arithmetic and copies ran while one was open for 0% of the time, Pallas kernels for 27%

profile of v6, /device:TPU:113, one launch (start us, length us, event | category | flops | bytes accessed | tf_op | source)
XLA Modules:
  0.0 134.6 jit_solution(6309005626002116966)
XLA Ops:
  0.6 41.4 %first.1 = (bf16[8,64,768]{2,1,0:T(8,128)(2,1)}, bf16[8,64,768]{2,1,0:T(8,128)(2,1)}, bf16[64,768]{1,0:T(8,128)(2,1)}, f32[16,8,128]{2,1,0:T(8,128)}, f32[16,8,1...) custom-call(bf16[64,768]{1,0:T(8,128)(2,1)} %x_ref.3, ...), custom_call_target="tpu_custom_call" | custom-call | tf_op jit(solution)/shard_map/first/pallas_call | solution.py:581
  42.0 22.4 %backward.2 = (f32[16,768,256]{2,1,0:T(8,128)}, f32[16,768,256]{2,1,0:T(8,128)}, f32[16,256,768]{2,1,0:T(8,128)}, f32[8,64,768]{2,1,0:T(8,128)}, f32[8,8,128]{2,1,0:T(8,128)}) custom-call(bf16[8,64,768]{2,1,0:T(8,128)(2,1)} %get-tuple-element.44.x_all.mid_in, bf16[8,64,768]{2,1,0:T(8,128)(2,1)} %get-tuple-element.45.dy_all, ...), custom_call_target="tpu_custom_call" | custom-call | flops 7247757312 | bytes 56623104 | tf_op jit(solution)/shard_map/backward/pallas_call | solution.py:595
  64.4 28.0 %middle.1 = (bf16[8,64,768]{2,1,0:T(8,128)(2,1)}, bf16[8,64,768]{2,1,0:T(8,128)(2,1)}, bf16[64,768]{1,0:T(8,128)(2,1)}, f32[8,128]{1,0:T(8,128)}, f32[64,768]{1,...) custom-call(f32[8,8,128]{2,1,0:T(8,128)} %get-tuple-element.49.dg_part, ...), custom_call_target="tpu_custom_call" | custom-call | tf_op jit(solution)/shard_map/middle/pallas_call | solution.py:616
  92.4 0.2 collective-permute-start
  92.6 2.3 %collective-permute-start.1 = (f32[64,768]{1,0:T(8,128)}, f32[64,768]{1,0:T(8,128)}, u32[]{:S(2)}, u32[]{:S(2)}) collective-permute-start(f32[64,768]{1,0:T(8,128)} %get-tuple-element.53), channel_id=1, source_target_pairs={{0,4},{1,5},{2,6},{3,7},{4,0},{5,1},{6,2},{7,3},{8,12},{9,13},{10,... | collective-permute-start | bytes 589832 | tf_op jit(solution)/shard_map/ppermute | solution.py:629
  95.0 1.5 %collective-permute-start.2 = (f32[64,768]{1,0:T(8,128)}, f32[64,768]{1,0:T(8,128)}, u32[]{:S(2)}, u32[]{:S(2)}) collective-permute-start(f32[64,768]{1,0:T(8,128)} %get-tuple-element.54), channel_id=1, source_target_pairs={{0,6},{1,7},{2,0},{3,1},{4,2},{5,3},{6,4},{7,5},{8,14},{9,15},{10,... | collective-permute-start | bytes 589832 | tf_op jit(solution)/shard_map/ppermute | solution.py:629
  96.5 22.3 %backward.3 = (f32[16,768,256]{2,1,0:T(8,128)}, f32[16,768,256]{2,1,0:T(8,128)}, f32[16,256,768]{2,1,0:T(8,128)}, f32[8,64,768]{2,1,0:T(8,128)}, f32[8,8,128]{2,1,0:T(8,128)}) custom-call(bf16[8,64,768]{2,1,0:T(8,128)(2,1)} %get-tuple-element.55.x_all, bf16[8,64,768]{2,1,0:T(8,128)(2,1)} %get-tuple-element.56.dy_all, f32[16,8,128]{2,1,0:T(8,128)} %get-tuple-element.57.s_ref, ...), custom_call_target="tpu_custom_call" | custom-call | flops 7247757312 | bytes 56623104 | tf_op jit(solution)/shard_map/backward/pallas_call | solution.py:595
  118.8 13.7 %last.1 = (bf16[64,768]{1,0:T(8,128)(2,1)}, f32[8,128]{1,0:T(8,128)}) custom-call(f32[8,8,128]{2,1,0:T(8,128)} %get-tuple-element.60.dg_part, bf16[64,768]{1,0:T(8,128)(2,1)} %get-tuple-element.61.dmid_ref, f32[8,64,768]{2,1,0:T(8,128)} %get-tuple-element.62.part_in), custom_call_target="tpu_custom_call" | custom-call | tf_op jit(solution)/shard_map/last/pallas_call | solution.py:634
  132.6 0.0 collective-permute-done.left_x
  132.6 0.0 collective-permute-done.1.opp_x
  132.6 0.0 collective-permute-done.2.right_x
  132.6 2.0 %final.1 = (bf16[64,768]{1,0:T(8,128)(2,1)}, bf16[64,768]{1,0:T(8,128)(2,1)}, f32[8,64]{1,0:T(8,128)}, f32[8,64]{1,0:T(8,128)}) custom-call(bf16[64,768]{1,0:T(8,128)(2,1)} %get-tuple-element.43.mid_ref, f32[64,768]{1,0:T(8,128)} %get-tuple-element.51.own_x, f32[64,768]{1,0:T(8,128)} %collective-permute-done.left_x, f32[64,768]{1,0:T(8,128)} %collective-permute-done.1.opp_x, ...), custom_call_target="tpu_custom_call" | custom-call | tf_op jit(solution)/shard_map/final/pallas_call | solution.py:644
Async XLA Ops:
  92.4 40.2 %collective-permute-start = (f32[64,768]{1,0:T(8,128)}, f32[64,768]{1,0:T(8,128)}, u32[]{:S(2)}, u32[]{:S(2)}) collective-permute-start(f32[64,768]{1,0:T(8,128)} %get-tuple-element.52), channel_id=1, source_target_pairs={{0,2},{1,3},{2,4},{3,5},{4,6},{5,7},{6,0},{7,1},{8,10},{9,11},{10,... | collective-permute-start | bytes 589832 | tf_op jit(solution)/shard_map/ppermute | solution.py:629
  92.6 39.9 %collective-permute-start.1 = (f32[64,768]{1,0:T(8,128)}, f32[64,768]{1,0:T(8,128)}, u32[]{:S(2)}, u32[]{:S(2)}) collective-permute-start(f32[64,768]{1,0:T(8,128)} %get-tuple-element.53), channel_id=1, source_target_pairs={{0,4},{1,5},{2,6},{3,7},{4,0},{5,1},{6,2},{7,3},{8,12},{9,13},{10,... | collective-permute-start | bytes 589832 | tf_op jit(solution)/shard_map/ppermute | solution.py:629
  95.0 37.6 %collective-permute-start.2 = (f32[64,768]{1,0:T(8,128)}, f32[64,768]{1,0:T(8,128)}, u32[]{:S(2)}, u32[]{:S(2)}) collective-permute-start(f32[64,768]{1,0:T(8,128)} %get-tuple-element.54), channel_id=1, source_target_pairs={{0,6},{1,7},{2,0},{3,1},{4,2},{5,3},{6,4},{7,5},{8,14},{9,15},{10,... | collective-permute-start | bytes 589832 | tf_op jit(solution)/shard_map/ppermute | solution.py:629

commit v7 on v6

--- a/solution.py
+++ b/solution.py
@@ -14,6 +14,7 @@
 CAP_FACTOR = 4
 BF16_MAX = 3.3895313892515355e38
 GROUPED = 2
+SLOTS = 3
 FORWARD_GROUPED = 4
 MIB = 1024 * 1024
 ALL_VMEM = 64 * MIB - 64 * 1024
@@ -386,16 +387,16 @@
         return pltpu.make_async_copy(src.at[slot], dst.at[pl.ds(g * GROUPED, GROUPED)], out_sems.at[i, slot])
 
     def step(g, carry):
-        slot = lax.rem(g, 2)
+        slot = lax.rem(g, SLOTS)
         experts = [g * GROUPED + i for i in range(GROUPED)]
         each = range(GROUPED)
         for e in experts:
             wait_weights(pairs, w_sems, e)
 
-        @pl.when(g >= 2)
+        @pl.when(g >= SLOTS)
         def _():
             for i in range(3):
-                store(g - 2, i, slot).wait()
+                store(g - SLOTS, i, slot).wait()
         for i, e in enumerate(experts):
             w2_t[i] = w2_v[e].T
         u = [u_ref[:, e].reshape(n_rows, width) for e in experts]
@@ -441,16 +442,16 @@
         for i in range(local):
             total = jnp.where(rel_ref[d] == float(i), dg_ref[i, d : d + 1, :], total)
         dgate[d] = total
-    for g in (steps - 2, steps - 1):
+    for g in range(max(steps - SLOTS, 0), steps):
         for i in range(3):
-            store(g, i, g % 2).wait()
+            store(g, i, g % SLOTS).wait()
     for d in range(n_dev):
         pltpu.make_async_copy(part_v.at[d], part.at[d], part_sems.at[d]).wait()
 
 
-def middle_kernel(dims, dg_part, dy_ref, x_ref, sb, gb, part_in, mid_in, w1, w3, w2,
-                  x_again, dmid_all, dmid_own, dgate, own_x, right_x, opp_x, left_x,
-                  part_b, mid_all, in_sems, part_x, near_x, d_all, x_all, u_ref, near, mine, got, dg_near, dg_mine, dg_got, d_buf, w1_v, w3_v, w2_v,
+def middle_kernel(dims, dy_ref, x_ref, sb, gb, part_in, mid_in, w1, w3, w2,
+                  x_again, dmid_all, dmid_own, own_x, right_x, opp_x, left_x,
+                  part_b, mid_all, in_sems, part_x, near_x, d_all, x_all, u_ref, near, mine, got, d_buf, w1_v, w3_v, w2_v,
                   w_sems, send_sems, recv_sems):
     n_dev, tok, width, local, cap, top_k = dims
     pairs = ((w1, w1_v), (w3, w3_v), (w2, w2_v))
@@ -464,25 +465,20 @@
     links.greet()
     part_load.wait()
     red = Reduce(links, part_b, (near, mine, got))
-    dg = Reduce(links, dg_part, (dg_near, dg_mine, dg_got), split=False)
     s_map = sb[...].reshape(local * n_dev, LANES)
 
     def rows_of(d):
         fill_rows(s_map, d, ((mid_all, u_ref),), cap)
 
     red.start()
-    dg.start()
     mid_load.wait()
     for d in range(2):
         rows_of(d)
     red.far()
     red.near_sends()
-    dg.far()
-    dg.near_sends()
     for d in range(2, n_dev):
         rows_of(d)
     red.relay()
-    dg.relay()
     x_g = Gather(links, x_ref, x_all)
     x_all[me] = x_ref[...]
     half = local // 2 // FORWARD_GROUPED * FORWARD_GROUPED
@@ -508,26 +504,28 @@
     for hop, out in enumerate((own_x, right_x, opp_x, left_x)):
         chip = lax.rem((me - links.core) // 2 + hop, n_dev // 2)
         out[...] = part_x[links.core, chip] + near_x[chip]
-    dgate[...] = dg.result()
     d_g.finish()
     dmid_all[...] = d_all[...]
     x_store.wait()
     links.drain()
 
 
-def final_kernel(mid_ref, own_x, left_x, opp_x, right_x, dx_ref, dga_ref, dgb_ref, x_out, dx_out, dga_out, dgb_out):
+def final_kernel(mid_ref, own_x, left_x, opp_x, right_x, dx_ref, dgate_ref, x_out, dx_out, dga_out, dgb_out):
     total = own_x[...] + left_x[...] + opp_x[...] + right_x[...]
     x_out[...] = (mid_ref[...].astype(F32) + total).astype(BF16)
     dx_out[...] = dx_ref[...]
-    tok = dga_out.shape[1]
-    dga_out[...] = dga_ref[:, :tok]
-    dgb_out[...] = dgb_ref[:, :tok]
-
-
-def last_kernel(dims, dg_part, dmid_ref, part_in, dx_out, dgate,
-                part_a, in_sem, near, mine, got, dg_near, dg_mine, dg_got, send_sems, recv_sems):
+    top_k, tok = dga_out.shape
+    dga_out[...] = dgate_ref[:top_k, :tok]
+    dgb_out[...] = dgate_ref[top_k:, :tok]
+
+
+def last_kernel(dims, dg_a, dg_b, dmid_ref, part_in, dx_out, dgate,
+                part_a, in_sem, dg_part, near, mine, got, dg_near, dg_mine, dg_got, send_sems, recv_sems):
     part_load = pltpu.make_async_copy(part_in, part_a, in_sem.at[0])
     part_load.start()
+    top_k = dims[-1]
+    dg_part[:, :top_k, :] = dg_a[...]
+    dg_part[:, top_k:, :] = dg_b[...]
     links = Links(dims[0], send_sems, recv_sems)
     links.greet()
     part_load.wait()
@@ -600,9 +598,9 @@
                 out_specs=[HBM] * 4 + [VMEM],
                 scratch_shapes=[expert_v, expert_v, pltpu.VMEM((local, n_dev, LANES), F32), *weights_v,
                                 *[pltpu.VMEM((GROUPED, inner, width), BF16)] * 2, pltpu.VMEM((GROUPED, width, inner), BF16),
-                                *[pltpu.VMEM((2, GROUPED, width, inner), F32)] * 2,
-                                pltpu.VMEM((2, GROUPED, inner, width), F32), part_v, w_sems,
-                                pltpu.SemaphoreType.DMA((3, 2)), pltpu.SemaphoreType.DMA((n_dev,))],
+                                *[pltpu.VMEM((SLOTS, GROUPED, width, inner), F32)] * 2,
+                                pltpu.VMEM((SLOTS, GROUPED, inner, width), F32), part_v, w_sems,
+                                pltpu.SemaphoreType.DMA((3, SLOTS)), pltpu.SemaphoreType.DMA((n_dev,))],
                 compiler_params=pltpu.CompilerParams(vmem_limit_bytes=ALL_VMEM), name="backward",
                 cost_estimate=pl.CostEstimate(flops=18 * local * n_dev * cap * width * inner, transcendentals=0,
                                               bytes_accessed=18 * local * width * inner),
@@ -610,20 +608,20 @@
 
         *grads_b, part_b, dg_b = backward(mid_all, dy_all, sb, gb, relb, w1_b, w3_b, w2_b)
 
-        count = 2 * Gather.COPIES + 2 * Reduce.COPIES + 1
+        count = 2 * Gather.COPIES + Reduce.COPIES + 1
         sums = sds((tok, width), F32)
         chip_sums = pltpu.VMEM((n_dev // 2, tok, width), F32)
-        x_again, dmid_all, dmid_own, dgate_b, own_x, right_x, opp_x, left_x = pl.pallas_call(
+        x_again, dmid_all, dmid_own, own_x, right_x, opp_x, left_x = pl.pallas_call(
             functools.partial(middle_kernel, dims),
-            out_shape=(rows_all, rows_all, own, sds((top_k, LANES), F32), sums, sums, sums, sums),
-            in_specs=[VMEM] * 5 + [HBM] * 5,
-            out_specs=[HBM] + [VMEM] * 7,
+            out_shape=(rows_all, rows_all, own, sums, sums, sums, sums),
+            in_specs=[VMEM] * 4 + [HBM] * 5,
+            out_specs=[HBM] + [VMEM] * 6,
             scratch_shapes=[part_v, rows_v, pltpu.SemaphoreType.DMA((3,)),
                             pltpu.VMEM((2, n_dev // 2, tok, width), F32), chip_sums, rows_v, rows_v, expert_v,
-                            *Reduce.scratch(tok, width), *Reduce.scratch(top_k, LANES), pltpu.VMEM((tok, width), BF16),
+                            *Reduce.scratch(tok, width), pltpu.VMEM((tok, width), BF16),
                             *weights_v, w_sems, *dma_sems(count)],
             compiler_params=remote_params(1), name="middle",
-        )(dg_b, dy_out, x_in, sb, gb, part_b, mid_all, w1_b, w3_b, w2_b)
+        )(dy_out, x_in, sb, gb, part_b, mid_all, w1_b, w3_b, w2_b)
 
         def shift(rows, hop):
             return lax.ppermute(rows, "ep", [(i, (i + 2 * hop) % n_dev) for i in range(n_dev)])
@@ -631,20 +629,20 @@
         left_x, opp_x, right_x = shift(right_x, 1), shift(opp_x, 2), shift(left_x, 3)
         *grads_a, part_a, dg_a = backward(x_again, dmid_all, sa, ga, rela, w1_a, w3_a, w2_a)
 
-        dx_in, dgate_a = pl.pallas_call(
+        dx_in, dgates = pl.pallas_call(
             functools.partial(last_kernel, dims),
-            out_shape=(own, sds((top_k, LANES), F32)),
-            in_specs=[VMEM] * 2 + [HBM],
+            out_shape=(own, sds((2 * top_k, LANES), F32)),
+            in_specs=[VMEM] * 3 + [HBM],
             out_specs=[VMEM] * 2,
-            scratch_shapes=[part_v, pltpu.SemaphoreType.DMA((1,)), *Reduce.scratch(tok, width),
-                            *Reduce.scratch(top_k, LANES), *dma_sems(2 * Reduce.COPIES)],
+            scratch_shapes=[part_v, pltpu.SemaphoreType.DMA((1,)), pltpu.VMEM((n_dev, 2 * top_k, LANES), F32),
+                            *Reduce.scratch(tok, width), *Reduce.scratch(2 * top_k, LANES), *dma_sems(2 * Reduce.COPIES)],
             compiler_params=remote_params(2), name="last",
-        )(dg_a, dmid_own, part_a)
+        )(dg_a, dg_b, dmid_own, part_a)
         gates = sds((top_k, tok), F32)
         x_out, dx_in, dgate_a, dgate_b = pl.pallas_call(
-            final_kernel, out_shape=(own, own, gates, gates), in_specs=[VMEM] * 8, out_specs=[VMEM] * 4, name="final",
+            final_kernel, out_shape=(own, own, gates, gates), in_specs=[VMEM] * 7, out_specs=[VMEM] * 4, name="final",
             compiler_params=pltpu.CompilerParams(vmem_limit_bytes=60 * MIB),
-        )(mid_own, own_x, left_x, opp_x, right_x, dx_in, dgate_a, dgate_b)
+        )(mid_own, own_x, left_x, opp_x, right_x, dx_in, dgates)
         return (x_out, dx_in, *grads_a, *grads_b, dgate_a.T, dgate_b.T)
 
     return jax.shard_map(device_program, mesh=mesh, in_specs=(tok_spec,) * 6 + (w_spec,) * 6, out_specs=(tok_spec,) * 10, check_vma=False)

time: 135 us -> 130 us (0.963)
  Pallas kernels: 130 us -> 126 us
    pallas_call x2, Pallas kernels: 44.7 us -> 40.4 us  [backward(): pl.pallas_call(functools.partial(backward_kernel, dims), out_shape=(sds((...]
  transfers between devices with their start and end apart: 3 -> 3, of which waited for: 0 -> 0; matrix products, arithmetic and copies ran while one was open for 0% -> 0% of each run, Pallas kernels for 27% -> 26%
where the time goes in v7:
time: 130 us
  Pallas kernels  126 us (97%)
  starting transfers between devices  3.58 us (3%)
    pallas_call x1, Pallas kernels, device_program(): pl.pallas_call(functools.partial(first_kernel, dims), out_shape=(rows_all...  41.4 us
    pallas_call x2, Pallas kernels, backward(): pl.pallas_call(functools.partial(backward_kernel, dims), out_shape=(sds((...  40.4 us
    pallas_call x1, Pallas kernels, device_program(): pl.pallas_call(functools.partial(middle_kernel, dims), out_shape=(rows_al...  28 us
    pallas_call x1, Pallas kernels, device_program(): pl.pallas_call(functools.partial(last_kernel, dims), out_shape=(own, sds(...  14.2 us
    ppermute x3, starting transfers between devices, shift(): lax.ppermute(rows, 'ep', [(i, (i + 2 * hop) % n_dev) for i in range(n_dev)])  3.58 us
  transfers between devices with their start and end apart: 3, of which 0 were waited for; matrix products, arithmetic and copies ran while one was open for 0% of the time, Pallas kernels for 26%

profile of v7, /device:TPU:113, one launch (start us, length us, event | category | flops | bytes accessed | tf_op | source)
XLA Modules:
  0.0 130.2 jit_solution(1324198495118544287)
XLA Ops:
  0.6 41.4 %first.1 = (bf16[8,64,768]{2,1,0:T(8,128)(2,1)}, bf16[8,64,768]{2,1,0:T(8,128)(2,1)}, bf16[64,768]{1,0:T(8,128)(2,1)}, f32[16,8,128]{2,1,0:T(8,128)}, f32[16,8,1...) custom-call(bf16[64,768]{1,0:T(8,128)(2,1)} %x_ref.3, ...), custom_call_target="tpu_custom_call" | custom-call | tf_op jit(solution)/shard_map/first/pallas_call | solution.py:579
  42.0 20.2 %backward.2 = (f32[16,768,256]{2,1,0:T(8,128)}, f32[16,768,256]{2,1,0:T(8,128)}, f32[16,256,768]{2,1,0:T(8,128)}, f32[8,64,768]{2,1,0:T(8,128)}, f32[8,8,128]{2,1,0:T(8,128)}) custom-call(bf16[8,64,768]{2,1,0:T(8,128)(2,1)} %get-tuple-element.45.x_all.mid_in, bf16[8,64,768]{2,1,0:T(8,128)(2,1)} %get-tuple-element.46.dy_all, ...), custom_call_target="tpu_custom_call" | custom-call | flops 7247757312 | bytes 56623104 | tf_op jit(solution)/shard_map/backward/pallas_call | solution.py:593
  62.2 28.0 %middle.1 = (bf16[8,64,768]{2,1,0:T(8,128)(2,1)}, bf16[8,64,768]{2,1,0:T(8,128)(2,1)}, bf16[64,768]{1,0:T(8,128)(2,1)}, f32[64,768]{1,0:T(8,128)}, f32[64,768]{1...) custom-call(bf16[64,768]{1,0:T(8,128)(2,1)} %dy_ref.3, bf16[64,768]{1,0:T(8,128)(2,1)} %x_ref.3, ...), custom_call_target="tpu_custom_call" | custom-call | tf_op jit(solution)/shard_map/middle/pallas_call | solution.py:614
  90.2 0.1 collective-permute-start
  90.3 2.0 %collective-permute-start.1 = (f32[64,768]{1,0:T(8,128)}, f32[64,768]{1,0:T(8,128)}, u32[]{:S(2)}, u32[]{:S(2)}) collective-permute-start(f32[64,768]{1,0:T(8,128)} %get-tuple-element.51), channel_id=1, source_target_pairs={{0,4},{1,5},{2,6},{3,7},{4,0},{5,1},{6,2},{7,3},{8,12},{9,13},{10,... | collective-permute-start | bytes 589832 | tf_op jit(solution)/shard_map/ppermute | solution.py:627
  92.3 1.5 %collective-permute-start.2 = (f32[64,768]{1,0:T(8,128)}, f32[64,768]{1,0:T(8,128)}, u32[]{:S(2)}, u32[]{:S(2)}) collective-permute-start(f32[64,768]{1,0:T(8,128)} %get-tuple-element.52), channel_id=1, source_target_pairs={{0,6},{1,7},{2,0},{3,1},{4,2},{5,3},{6,4},{7,5},{8,14},{9,15},{10,... | collective-permute-start | bytes 589832 | tf_op jit(solution)/shard_map/ppermute | solution.py:627
  93.8 20.2 %backward.3 = (f32[16,768,256]{2,1,0:T(8,128)}, f32[16,768,256]{2,1,0:T(8,128)}, f32[16,256,768]{2,1,0:T(8,128)}, f32[8,64,768]{2,1,0:T(8,128)}, f32[8,8,128]{2,1,0:T(8,128)}) custom-call(bf16[8,64,768]{2,1,0:T(8,128)(2,1)} %get-tuple-element.53.x_all, bf16[8,64,768]{2,1,0:T(8,128)(2,1)} %get-tuple-element.54.dy_all, f32[16,8,128]{2,1,0:T(8,128)} %get-tuple-element.55.s_ref, ...), custom_call_target="tpu_custom_call" | custom-call | flops 7247757312 | bytes 56623104 | tf_op jit(solution)/shard_map/backward/pallas_call | solution.py:593
  114.0 14.2 %last.1 = (bf16[64,768]{1,0:T(8,128)(2,1)}, f32[16,128]{1,0:T(8,128)}) custom-call(f32[8,8,128]{2,1,0:T(8,128)} %get-tuple-element.58.dg_a, f32[8,8,128]{2,1,0:T(8,128)} %get-tuple-element.59.dg_b, bf16[64,768]{1,0:T(8,128)(2,1)} %get-tuple-element.60.dmid_ref, f32[8,64,768]{2,1,0:T(8,128)} %get-tuple-element.61.part_in), custom_call_target="tpu_custom_call" | custom-call | tf_op jit(solution)/shard_map/last/pallas_call | solution.py:632
  128.2 0.0 collective-permute-done.left_x
  128.2 0.0 collective-permute-done.1.opp_x
  128.2 0.0 collective-permute-done.2.right_x
  128.2 2.0 %final.1 = (bf16[64,768]{1,0:T(8,128)(2,1)}, bf16[64,768]{1,0:T(8,128)(2,1)}, f32[8,64]{1,0:T(8,128)}, f32[8,64]{1,0:T(8,128)}) custom-call(bf16[64,768]{1,0:T(8,128)(2,1)} %get-tuple-element.42.mid_ref, f32[64,768]{1,0:T(8,128)} %get-tuple-element.49.own_x, f32[64,768]{1,0:T(8,128)} %collective-permute-done.left_x, f32[64,768]{1,0:T(8,128)} %collective-permute-done.1.opp_x, ...), custom_call_target="tpu_custom_call" | custom-call | tf_op jit(solution)/shard_map/final/pallas_call | solution.py:642
Async XLA Ops:
  90.2 38.0 %collective-permute-start = (f32[64,768]{1,0:T(8,128)}, f32[64,768]{1,0:T(8,128)}, u32[]{:S(2)}, u32[]{:S(2)}) collective-permute-start(f32[64,768]{1,0:T(8,128)} %get-tuple-element.50), channel_id=1, source_target_pairs={{0,2},{1,3},{2,4},{3,5},{4,6},{5,7},{6,0},{7,1},{8,10},{9,11},{10,... | collective-permute-start | bytes 589832 | tf_op jit(solution)/shard_map/ppermute | solution.py:627
  90.3 37.9 %collective-permute-start.1 = (f32[64,768]{1,0:T(8,128)}, f32[64,768]{1,0:T(8,128)}, u32[]{:S(2)}, u32[]{:S(2)}) collective-permute-start(f32[64,768]{1,0:T(8,128)} %get-tuple-element.51), channel_id=1, source_target_pairs={{0,4},{1,5},{2,6},{3,7},{4,0},{5,1},{6,2},{7,3},{8,12},{9,13},{10,... | collective-permute-start | bytes 589832 | tf_op jit(solution)/shard_map/ppermute | solution.py:627
  92.3 35.9 %collective-permute-start.2 = (f32[64,768]{1,0:T(8,128)}, f32[64,768]{1,0:T(8,128)}, u32[]{:S(2)}, u32[]{:S(2)}) collective-permute-start(f32[64,768]{1,0:T(8,128)} %get-tuple-element.52), channel_id=1, source_target_pairs={{0,6},{1,7},{2,0},{3,1},{4,2},{5,3},{6,4},{7,5},{8,14},{9,15},{10,... | collective-permute-start | bytes 589832 | tf_op jit(solution)/shard_map/ppermute | solution.py:627

commit v8 on v7

--- a/solution.py
+++ b/solution.py
@@ -108,15 +108,18 @@
         self.right = lax.rem(me + 2, n_dev)
         self.left = lax.rem(me + n_dev - 2, n_dev)
         self.opp = lax.rem(me + 4, n_dev)
+        side = self.partner - me
+        self.right_side, self.left_side = self.right + side, self.left + side
         self.send_sems, self.recv_sems = send_sems, recv_sems
         self.used = 0
         self.started = []
 
     def greet(self):
         barrier = pltpu.get_barrier_semaphore()
-        for peer in (self.partner, self.left, self.right):
+        peers = (self.partner, self.left, self.right, self.left_side, self.right_side)
+        for peer in peers:
             pl.semaphore_signal(barrier, inc=1, device_id={"ep": peer}, device_id_type=MESH)
-        pl.semaphore_wait(barrier, 3)
+        pl.semaphore_wait(barrier, len(peers))
 
     def copy(self, src, dst, peer):
         slot = self.used
@@ -144,36 +147,33 @@
         self.to_partner = k.copy(own, full.at[k.me], k.partner)
 
     def pass_on(self):
-        k, full, half = self.k, self.full, self.half
+        k, half = self.k, self.half
+        upper, lower = pl.ds(0, half), pl.ds(half, half)
         self.to_right.wait_recv()
-        self.far_a = k.copy(full.at[k.left, pl.ds(0, half)], full.at[k.left, pl.ds(0, half)], k.right)
-        self.side_a = k.copy(full.at[k.left], full.at[k.left], k.partner)
+        self.far = [self.forward(k.left, upper, k.right), self.forward(k.left, upper, k.right_side)]
+        side_a = self.forward(k.left, pl.ds(0, 2 * half), k.partner)
         self.to_left.wait_recv()
-        self.far_b = k.copy(full.at[k.right, pl.ds(half, half)], full.at[k.right, pl.ds(half, half)], k.left)
-        self.side_b = k.copy(full.at[k.right], full.at[k.right], k.partner)
-
-    def pass_far(self):
-        k, full, half = self.k, self.full, self.half
-        self.far_a.wait_recv()
-        self.last_a = k.copy(full.at[k.opp, pl.ds(0, half)], full.at[k.opp, pl.ds(0, half)], k.partner)
-        self.far_b.wait_recv()
-        self.last_b = k.copy(full.at[k.opp, pl.ds(half, half)], full.at[k.opp, pl.ds(half, half)], k.partner)
+        self.far += [self.forward(k.right, lower, k.left), self.forward(k.right, lower, k.left_side)]
+        self.sides = [side_a, self.forward(k.right, pl.ds(0, 2 * half), k.partner)]
+
+    def forward(self, block, at, peer):
+        return self.k.copy(self.full.at[block, at], self.full.at[block, at], peer)
 
     def wait_partner(self):
         self.to_partner.wait_recv()
 
     def wait_sides(self):
-        self.side_a.wait_recv()
-        self.side_b.wait_recv()
-
-    def wait_last(self):
-        self.last_a.wait_recv()
-        self.last_b.wait_recv()
+        for copy in self.sides:
+            copy.wait_recv()
+
+    def wait_far(self):
+        for copy in self.far:
+            copy.wait_recv()
 
     def finish(self):
         self.wait_partner()
         self.wait_sides()
-        self.wait_last()
+        self.wait_far()
 
 
 class Reduce:
@@ -308,7 +308,6 @@
     meta_g.pass_on()
     x_g.pass_on()
     y_g = Gather(links, dy_ref, y_all)
-    meta_g.pass_far()
     meta_g.finish()
     meta = meta_all[...]
     routing_maps(me, meta, 0, sa, ga, rela, top_k, local)
@@ -322,18 +321,16 @@
     rows_of(links.right)
     x_g.wait_partner()
     rows_of(links.partner)
-    x_g.pass_far()
     x_g.wait_sides()
     side = 1 - 2 * links.core
     rows_of(links.left + side)
     rows_of(links.right + side)
-    rows_of(links.opp)
     y_g.pass_on()
     routing_maps(me, meta, 1, sb, gb, relb, top_k, local)
-    x_g.wait_last()
+    x_g.wait_far()
+    rows_of(links.opp)
     rows_of(links.opp + side)
     forward_experts((w1_v, w3_v, w2_v), lambda e: wait_weights(pairs, w_sems, e), u_ref, o_ref, cap, 0, local)
-    y_g.pass_far()
     stack = scatter_lhs(s_map, ga[...].reshape(local * n_dev, LANES), tok)
     red = Reduce(links, part, (near, mine, got))
 
@@ -361,7 +358,6 @@
     m_all[me] = x_mid
     m_g = Gather(links, mid_buf, m_all)
     m_g.pass_on()
-    m_g.pass_far()
     m_g.finish()
     mid_all[...] = m_all[...]
     y_store.wait()
@@ -491,12 +487,10 @@
     x_g.pass_on()
     forward_experts((w1_v, w3_v, w2_v), lambda e: wait_weights(pairs, w_sems, e), u_ref, u_ref, cap, half, local)
     d_g.pass_on()
-    x_g.pass_far()
     stack = scatter_lhs(s_map, gb[...].reshape(local * n_dev, LANES), tok)
     for d in range(n_dev):
         part_x[d % 2, d // 2] = token_sums(stack, d, u_ref[d].reshape(local * cap, width), tok, cap)
     side_x = links.copy(part_x.at[1 - links.core], near_x, links.partner)
-    d_g.pass_far()
     x_g.finish()
     x_store = pltpu.make_async_copy(x_all, x_again, in_sems.at[2])
     x_store.start()

time: 130 us -> 130 us (level)
  transfers between devices with their start and end apart: 3 -> 3, of which waited for: 0 -> 0; matrix products, arithmetic and copies ran while one was open for 0% -> 0% of each run, Pallas kernels for 26% -> 27%
where the time goes in v8:
time: 130 us
  Pallas kernels  125 us (96%)
  starting transfers between devices  4.11 us (3%)
    pallas_call x1, Pallas kernels, device_program(): pl.pallas_call(functools.partial(first_kernel, dims), out_shape=(rows_all...  41.4 us
    pallas_call x2, Pallas kernels, backward(): pl.pallas_call(functools.partial(backward_kernel, dims), out_shape=(sds((...  40.4 us
    pallas_call x1, Pallas kernels, device_program(): pl.pallas_call(functools.partial(middle_kernel, dims), out_shape=(rows_al...  27.2 us
    pallas_call x1, Pallas kernels, device_program(): pl.pallas_call(functools.partial(last_kernel, dims), out_shape=(own, sds(...  14.3 us
    ppermute x3, starting transfers between devices, shift(): lax.ppermute(rows, 'ep', [(i, (i + 2 * hop) % n_dev) for i in range(n_dev)])  4.11 us
  transfers between devices with their start and end apart: 3, of which 0 were waited for; matrix products, arithmetic and copies ran while one was open for 0% of the time, Pallas kernels for 27%

profile of v8, /device:TPU:113, one launch (start us, length us, event | category | flops | bytes accessed | tf_op | source)
XLA Modules:
  0.0 130.1 jit_solution(301829413633361901)
XLA Ops:
  0.6 41.4 %first.1 = (bf16[8,64,768]{2,1,0:T(8,128)(2,1)}, bf16[8,64,768]{2,1,0:T(8,128)(2,1)}, bf16[64,768]{1,0:T(8,128)(2,1)}, f32[16,8,128]{2,1,0:T(8,128)}, f32[16,8,1...) custom-call(bf16[64,768]{1,0:T(8,128)(2,1)} %x_ref.3, ...), custom_call_target="tpu_custom_call" | custom-call | tf_op jit(solution)/shard_map/first/pallas_call | solution.py:573
  42.0 20.2 %backward.2 = (f32[16,768,256]{2,1,0:T(8,128)}, f32[16,768,256]{2,1,0:T(8,128)}, f32[16,256,768]{2,1,0:T(8,128)}, f32[8,64,768]{2,1,0:T(8,128)}, f32[8,8,128]{2,1,0:T(8,128)}) custom-call(bf16[8,64,768]{2,1,0:T(8,128)(2,1)} %get-tuple-element.45.x_all.mid_in, bf16[8,64,768]{2,1,0:T(8,128)(2,1)} %get-tuple-element.46.dy_all, ...), custom_call_target="tpu_custom_call" | custom-call | flops 7247757312 | bytes 56623104 | tf_op jit(solution)/shard_map/backward/pallas_call | solution.py:587
  62.2 27.2 %middle.1 = (bf16[8,64,768]{2,1,0:T(8,128)(2,1)}, bf16[8,64,768]{2,1,0:T(8,128)(2,1)}, bf16[64,768]{1,0:T(8,128)(2,1)}, f32[64,768]{1,0:T(8,128)}, f32[64,768]{1...) custom-call(bf16[64,768]{1,0:T(8,128)(2,1)} %dy_ref.3, bf16[64,768]{1,0:T(8,128)(2,1)} %x_ref.3, ...), custom_call_target="tpu_custom_call" | custom-call | tf_op jit(solution)/shard_map/middle/pallas_call | solution.py:608
  89.4 0.4 collective-permute-start
  89.8 2.4 %collective-permute-start.1 = (f32[64,768]{1,0:T(8,128)}, f32[64,768]{1,0:T(8,128)}, u32[]{:S(2)}, u32[]{:S(2)}) collective-permute-start(f32[64,768]{1,0:T(8,128)} %get-tuple-element.51), channel_id=1, source_target_pairs={{0,4},{1,5},{2,6},{3,7},{4,0},{5,1},{6,2},{7,3},{8,12},{9,13},{10,... | collective-permute-start | bytes 589832 | tf_op jit(solution)/shard_map/ppermute | solution.py:621
  92.2 1.3 %collective-permute-start.2 = (f32[64,768]{1,0:T(8,128)}, f32[64,768]{1,0:T(8,128)}, u32[]{:S(2)}, u32[]{:S(2)}) collective-permute-start(f32[64,768]{1,0:T(8,128)} %get-tuple-element.52), channel_id=1, source_target_pairs={{0,6},{1,7},{2,0},{3,1},{4,2},{5,3},{6,4},{7,5},{8,14},{9,15},{10,... | collective-permute-start | bytes 589832 | tf_op jit(solution)/shard_map/ppermute | solution.py:621
  93.5 20.2 %backward.3 = (f32[16,768,256]{2,1,0:T(8,128)}, f32[16,768,256]{2,1,0:T(8,128)}, f32[16,256,768]{2,1,0:T(8,128)}, f32[8,64,768]{2,1,0:T(8,128)}, f32[8,8,128]{2,1,0:T(8,128)}) custom-call(bf16[8,64,768]{2,1,0:T(8,128)(2,1)} %get-tuple-element.53.x_all, bf16[8,64,768]{2,1,0:T(8,128)(2,1)} %get-tuple-element.54.dy_all, f32[16,8,128]{2,1,0:T(8,128)} %get-tuple-element.55.s_ref, ...), custom_call_target="tpu_custom_call" | custom-call | flops 7247757312 | bytes 56623104 | tf_op jit(solution)/shard_map/backward/pallas_call | solution.py:587
  113.8 14.3 %last.1 = (bf16[64,768]{1,0:T(8,128)(2,1)}, f32[16,128]{1,0:T(8,128)}) custom-call(f32[8,8,128]{2,1,0:T(8,128)} %get-tuple-element.58.dg_a, f32[8,8,128]{2,1,0:T(8,128)} %get-tuple-element.59.dg_b, bf16[64,768]{1,0:T(8,128)(2,1)} %get-tuple-element.60.dmid_ref, f32[8,64,768]{2,1,0:T(8,128)} %get-tuple-element.61.part_in), custom_call_target="tpu_custom_call" | custom-call | tf_op jit(solution)/shard_map/last/pallas_call | solution.py:626
  128.1 0.0 collective-permute-done.left_x
  128.1 0.0 collective-permute-done.1.opp_x
  128.1 0.0 collective-permute-done.2.right_x
  128.1 2.0 %final.1 = (bf16[64,768]{1,0:T(8,128)(2,1)}, bf16[64,768]{1,0:T(8,128)(2,1)}, f32[8,64]{1,0:T(8,128)}, f32[8,64]{1,0:T(8,128)}) custom-call(bf16[64,768]{1,0:T(8,128)(2,1)} %get-tuple-element.42.mid_ref, f32[64,768]{1,0:T(8,128)} %get-tuple-element.49.own_x, f32[64,768]{1,0:T(8,128)} %collective-permute-done.left_x, f32[64,768]{1,0:T(8,128)} %collective-permute-done.1.opp_x, ...), custom_call_target="tpu_custom_call" | custom-call | tf_op jit(solution)/shard_map/final/pallas_call | solution.py:636
Async XLA Ops:
  89.4 38.7 %collective-permute-start = (f32[64,768]{1,0:T(8,128)}, f32[64,768]{1,0:T(8,128)}, u32[]{:S(2)}, u32[]{:S(2)}) collective-permute-start(f32[64,768]{1,0:T(8,128)} %get-tuple-element.50), channel_id=1, source_target_pairs={{0,2},{1,3},{2,4},{3,5},{4,6},{5,7},{6,0},{7,1},{8,10},{9,11},{10,... | collective-permute-start | bytes 589832 | tf_op jit(solution)/shard_map/ppermute | solution.py:621
  89.8 38.3 %collective-permute-start.1 = (f32[64,768]{1,0:T(8,128)}, f32[64,768]{1,0:T(8,128)}, u32[]{:S(2)}, u32[]{:S(2)}) collective-permute-start(f32[64,768]{1,0:T(8,128)} %get-tuple-element.51), channel_id=1, source_target_pairs={{0,4},{1,5},{2,6},{3,7},{4,0},{5,1},{6,2},{7,3},{8,12},{9,13},{10,... | collective-permute-start | bytes 589832 | tf_op jit(solution)/shard_map/ppermute | solution.py:621
  92.2 35.9 %collective-permute-start.2 = (f32[64,768]{1,0:T(8,128)}, f32[64,768]{1,0:T(8,128)}, u32[]{:S(2)}, u32[]{:S(2)}) collective-permute-start(f32[64,768]{1,0:T(8,128)} %get-tuple-element.52), channel_id=1, source_target_pairs={{0,6},{1,7},{2,0},{3,1},{4,2},{5,3},{6,4},{7,5},{8,14},{9,15},{10,... | collective-permute-start | bytes 589832 | tf_op jit(solution)/shard_map/ppermute | solution.py:621

commit v9 on v8

--- a/solution.py
+++ b/solution.py
@@ -114,9 +114,9 @@
         self.used = 0
         self.started = []
 
-    def greet(self):
+    def greet(self, sides=True):
         barrier = pltpu.get_barrier_semaphore()
-        peers = (self.partner, self.left, self.right, self.left_side, self.right_side)
+        peers = (self.partner, self.left, self.right) + ((self.left_side, self.right_side) if sides else ())
         for peer in peers:
             pl.semaphore_signal(barrier, inc=1, device_id={"ep": peer}, device_id_type=MESH)
         pl.semaphore_wait(barrier, len(peers))
@@ -139,8 +139,8 @@
 class Gather:
     COPIES = 9
 
-    def __init__(self, links, own, full):
-        k, self.k, self.full = links, links, full
+    def __init__(self, links, own, full, both=False):
+        k, self.k, self.full, self.both = links, links, full, both
         self.half = own.shape[0] // 2
         self.to_right = k.copy(own, full.at[k.me], k.right)
         self.to_left = k.copy(own, full.at[k.me], k.left)
@@ -148,13 +148,24 @@
 
     def pass_on(self):
         k, half = self.k, self.half
-        upper, lower = pl.ds(0, half), pl.ds(half, half)
+        self.upper, self.lower = pl.ds(0, half), pl.ds(half, half)
         self.to_right.wait_recv()
-        self.far = [self.forward(k.left, upper, k.right), self.forward(k.left, upper, k.right_side)]
+        self.far_up = [self.forward(k.left, self.upper, k.right)]
+        if self.both:
+            self.far_up.append(self.forward(k.left, self.upper, k.right_side))
         side_a = self.forward(k.left, pl.ds(0, 2 * half), k.partner)
         self.to_left.wait_recv()
-        self.far += [self.forward(k.right, lower, k.left), self.forward(k.right, lower, k.left_side)]
+        self.far_low = [self.forward(k.right, self.lower, k.left)]
+        if self.both:
+            self.far_low.append(self.forward(k.right, self.lower, k.left_side))
         self.sides = [side_a, self.forward(k.right, pl.ds(0, 2 * half), k.partner)]
+
+    def pass_far(self):
+        k = self.k
+        self.far_up[0].wait_recv()
+        self.far_up = [self.forward(k.opp, self.upper, k.partner)]
+        self.far_low[0].wait_recv()
+        self.far_low = [self.forward(k.opp, self.lower, k.partner)]
 
     def forward(self, block, at, peer):
         return self.k.copy(self.full.at[block, at], self.full.at[block, at], peer)
@@ -167,7 +178,7 @@
             copy.wait_recv()
 
     def wait_far(self):
-        for copy in self.far:
+        for copy in self.far_up + self.far_low:
             copy.wait_recv()
 
     def finish(self):
@@ -308,6 +319,7 @@
     meta_g.pass_on()
     x_g.pass_on()
     y_g = Gather(links, dy_ref, y_all)
+    meta_g.pass_far()
     meta_g.finish()
     meta = meta_all[...]
     routing_maps(me, meta, 0, sa, ga, rela, top_k, local)
@@ -321,16 +333,18 @@
     rows_of(links.right)
     x_g.wait_partner()
     rows_of(links.partner)
+    x_g.pass_far()
     x_g.wait_sides()
     side = 1 - 2 * links.core
     rows_of(links.left + side)
     rows_of(links.right + side)
+    rows_of(links.opp)
     y_g.pass_on()
     routing_maps(me, meta, 1, sb, gb, relb, top_k, local)
     x_g.wait_far()
-    rows_of(links.opp)
     rows_of(links.opp + side)
     forward_experts((w1_v, w3_v, w2_v), lambda e: wait_weights(pairs, w_sems, e), u_ref, o_ref, cap, 0, local)
+    y_g.pass_far()
     stack = scatter_lhs(s_map, ga[...].reshape(local * n_dev, LANES), tok)
     red = Reduce(links, part, (near, mine, got))
 
@@ -356,7 +370,7 @@
     mid_buf[...] = x_mid
     mid_own[...] = x_mid
     m_all[me] = x_mid
-    m_g = Gather(links, mid_buf, m_all)
+    m_g = Gather(links, mid_buf, m_all, both=True)
     m_g.pass_on()
     m_g.finish()
     mid_all[...] = m_all[...]
@@ -483,10 +497,11 @@
     d_buf[...] = dx
     dmid_own[...] = dx
     d_all[me] = dx
-    d_g = Gather(links, d_buf, d_all)
+    d_g = Gather(links, d_buf, d_all, both=True)
     x_g.pass_on()
     forward_experts((w1_v, w3_v, w2_v), lambda e: wait_weights(pairs, w_sems, e), u_ref, u_ref, cap, half, local)
     d_g.pass_on()
+    x_g.pass_far()
     stack = scatter_lhs(s_map, gb[...].reshape(local * n_dev, LANES), tok)
     for d in range(n_dev):
         part_x[d % 2, d // 2] = token_sums(stack, d, u_ref[d].reshape(local * cap, width), tok, cap)
@@ -521,7 +536,7 @@
     dg_part[:, :top_k, :] = dg_a[...]
     dg_part[:, top_k:, :] = dg_b[...]
     links = Links(dims[0], send_sems, recv_sems)
-    links.greet()
+    links.greet(sides=False)
     part_load.wait()
     red = Reduce(links, part_a, (near, mine, got))
     dg = Reduce(links, dg_part, (dg_near, dg_mine, dg_got), split=False)

time: 130 us -> 130 us (level)
  transfers between devices with their start and end apart: 3 -> 3, of which waited for: 0 -> 0; matrix products, arithmetic and copies ran while one was open for 0% -> 0% of each run, Pallas kernels for 27% -> 26%
where the time goes in v9:
time: 130 us
  Pallas kernels  125 us (96%)
  starting transfers between devices  4.05 us (3%)
    pallas_call x1, Pallas kernels, device_program(): pl.pallas_call(functools.partial(first_kernel, dims), out_shape=(rows_all...  40.6 us
    pallas_call x2, Pallas kernels, backward(): pl.pallas_call(functools.partial(backward_kernel, dims), out_shape=(sds((...  40.4 us
    pallas_call x1, Pallas kernels, device_program(): pl.pallas_call(functools.partial(middle_kernel, dims), out_shape=(rows_al...  28.1 us
    pallas_call x1, Pallas kernels, device_program(): pl.pallas_call(functools.partial(last_kernel, dims), out_shape=(own, sds(...  14 us
    ppermute x3, starting transfers between devices, shift(): lax.ppermute(rows, 'ep', [(i, (i + 2 * hop) % n_dev) for i in range(n_dev)])  4.05 us
  transfers between devices with their start and end apart: 3, of which 0 were waited for; matrix products, arithmetic and copies ran while one was open for 0% of the time, Pallas kernels for 26%

profile of v9, /device:TPU:113, one launch (start us, length us, event | category | flops | bytes accessed | tf_op | source)
XLA Modules:
  0.0 129.8 jit_solution(13790676503463192096)
XLA Ops:
  0.6 40.6 %first.1 = (bf16[8,64,768]{2,1,0:T(8,128)(2,1)}, bf16[8,64,768]{2,1,0:T(8,128)(2,1)}, bf16[64,768]{1,0:T(8,128)(2,1)}, f32[16,8,128]{2,1,0:T(8,128)}, f32[16,8,1...) custom-call(bf16[64,768]{1,0:T(8,128)(2,1)} %x_ref.3, ...), custom_call_target="tpu_custom_call" | custom-call | tf_op jit(solution)/shard_map/first/pallas_call | solution.py:588
  41.3 20.2 %backward.2 = (f32[16,768,256]{2,1,0:T(8,128)}, f32[16,768,256]{2,1,0:T(8,128)}, f32[16,256,768]{2,1,0:T(8,128)}, f32[8,64,768]{2,1,0:T(8,128)}, f32[8,8,128]{2,1,0:T(8,128)}) custom-call(bf16[8,64,768]{2,1,0:T(8,128)(2,1)} %get-tuple-element.45.x_all.mid_in, bf16[8,64,768]{2,1,0:T(8,128)(2,1)} %get-tuple-element.46.dy_all, ...), custom_call_target="tpu_custom_call" | custom-call | flops 7247757312 | bytes 56623104 | tf_op jit(solution)/shard_map/backward/pallas_call | solution.py:602
  61.5 28.1 %middle.1 = (bf16[8,64,768]{2,1,0:T(8,128)(2,1)}, bf16[8,64,768]{2,1,0:T(8,128)(2,1)}, bf16[64,768]{1,0:T(8,128)(2,1)}, f32[64,768]{1,0:T(8,128)}, f32[64,768]{1...) custom-call(bf16[64,768]{1,0:T(8,128)(2,1)} %dy_ref.3, bf16[64,768]{1,0:T(8,128)(2,1)} %x_ref.3, ...), custom_call_target="tpu_custom_call" | custom-call | tf_op jit(solution)/shard_map/middle/pallas_call | solution.py:623
  89.6 0.4 collective-permute-start
  90.0 1.7 %collective-permute-start.1 = (f32[64,768]{1,0:T(8,128)}, f32[64,768]{1,0:T(8,128)}, u32[]{:S(2)}, u32[]{:S(2)}) collective-permute-start(f32[64,768]{1,0:T(8,128)} %get-tuple-element.51), channel_id=1, source_target_pairs={{0,4},{1,5},{2,6},{3,7},{4,0},{5,1},{6,2},{7,3},{8,12},{9,13},{10,... | collective-permute-start | bytes 589832 | tf_op jit(solution)/shard_map/ppermute | solution.py:636
  91.7 1.9 %collective-permute-start.2 = (f32[64,768]{1,0:T(8,128)}, f32[64,768]{1,0:T(8,128)}, u32[]{:S(2)}, u32[]{:S(2)}) collective-permute-start(f32[64,768]{1,0:T(8,128)} %get-tuple-element.52), channel_id=1, source_target_pairs={{0,6},{1,7},{2,0},{3,1},{4,2},{5,3},{6,4},{7,5},{8,14},{9,15},{10,... | collective-permute-start | bytes 589832 | tf_op jit(solution)/shard_map/ppermute | solution.py:636
  93.6 20.2 %backward.3 = (f32[16,768,256]{2,1,0:T(8,128)}, f32[16,768,256]{2,1,0:T(8,128)}, f32[16,256,768]{2,1,0:T(8,128)}, f32[8,64,768]{2,1,0:T(8,128)}, f32[8,8,128]{2,1,0:T(8,128)}) custom-call(bf16[8,64,768]{2,1,0:T(8,128)(2,1)} %get-tuple-element.53.x_all, bf16[8,64,768]{2,1,0:T(8,128)(2,1)} %get-tuple-element.54.dy_all, f32[16,8,128]{2,1,0:T(8,128)} %get-tuple-element.55.s_ref, ...), custom_call_target="tpu_custom_call" | custom-call | flops 7247757312 | bytes 56623104 | tf_op jit(solution)/shard_map/backward/pallas_call | solution.py:602
  113.8 14.0 %last.1 = (bf16[64,768]{1,0:T(8,128)(2,1)}, f32[16,128]{1,0:T(8,128)}) custom-call(f32[8,8,128]{2,1,0:T(8,128)} %get-tuple-element.58.dg_a, f32[8,8,128]{2,1,0:T(8,128)} %get-tuple-element.59.dg_b, bf16[64,768]{1,0:T(8,128)(2,1)} %get-tuple-element.60.dmid_ref, f32[8,64,768]{2,1,0:T(8,128)} %get-tuple-element.61.part_in), custom_call_target="tpu_custom_call" | custom-call | tf_op jit(solution)/shard_map/last/pallas_call | solution.py:641
  127.8 0.0 collective-permute-done.left_x
  127.8 0.0 collective-permute-done.1.opp_x
  127.8 0.0 collective-permute-done.2.right_x
  127.9 2.0 %final.1 = (bf16[64,768]{1,0:T(8,128)(2,1)}, bf16[64,768]{1,0:T(8,128)(2,1)}, f32[8,64]{1,0:T(8,128)}, f32[8,64]{1,0:T(8,128)}) custom-call(bf16[64,768]{1,0:T(8,128)(2,1)} %get-tuple-element.42.mid_ref, f32[64,768]{1,0:T(8,128)} %get-tuple-element.49.own_x, f32[64,768]{1,0:T(8,128)} %collective-permute-done.left_x, f32[64,768]{1,0:T(8,128)} %collective-permute-done.1.opp_x, ...), custom_call_target="tpu_custom_call" | custom-call | tf_op jit(solution)/shard_map/final/pallas_call | solution.py:651
Async XLA Ops:
  89.6 38.2 %collective-permute-start = (f32[64,768]{1,0:T(8,128)}, f32[64,768]{1,0:T(8,128)}, u32[]{:S(2)}, u32[]{:S(2)}) collective-permute-start(f32[64,768]{1,0:T(8,128)} %get-tuple-element.50), channel_id=1, source_target_pairs={{0,2},{1,3},{2,4},{3,5},{4,6},{5,7},{6,0},{7,1},{8,10},{9,11},{10,... | collective-permute-start | bytes 589832 | tf_op jit(solution)/shard_map/ppermute | solution.py:636
  90.0 37.9 %collective-permute-start.1 = (f32[64,768]{1,0:T(8,128)}, f32[64,768]{1,0:T(8,128)}, u32[]{:S(2)}, u32[]{:S(2)}) collective-permute-start(f32[64,768]{1,0:T(8,128)} %get-tuple-element.51), channel_id=1, source_target_pairs={{0,4},{1,5},{2,6},{3,7},{4,0},{5,1},{6,2},{7,3},{8,12},{9,13},{10,... | collective-permute-start | bytes 589832 | tf_op jit(solution)/shard_map/ppermute | solution.py:636
  91.7 36.1 %collective-permute-start.2 = (f32[64,768]{1,0:T(8,128)}, f32[64,768]{1,0:T(8,128)}, u32[]{:S(2)}, u32[]{:S(2)}) collective-permute-start(f32[64,768]{1,0:T(8,128)} %get-tuple-element.52), channel_id=1, source_target_pairs={{0,6},{1,7},{2,0},{3,1},{4,2},{5,3},{6,4},{7,5},{8,14},{9,15},{10,... | collective-permute-start | bytes 589832 | tf_op jit(solution)/shard_map/ppermute | solution.py:636

commit v10 on v9

--- a/solution.py
+++ b/solution.py
@@ -489,7 +489,7 @@
     for d in range(2, n_dev):
         rows_of(d)
     red.relay()
-    x_g = Gather(links, x_ref, x_all)
+    x_g = Gather(links, x_ref, x_all, both=True)
     x_all[me] = x_ref[...]
     half = local // 2 // FORWARD_GROUPED * FORWARD_GROUPED
     forward_experts((w1_v, w3_v, w2_v), lambda e: wait_weights(pairs, w_sems, e), u_ref, u_ref, cap, 0, half)
@@ -501,7 +501,6 @@
     x_g.pass_on()
     forward_experts((w1_v, w3_v, w2_v), lambda e: wait_weights(pairs, w_sems, e), u_ref, u_ref, cap, half, local)
     d_g.pass_on()
-    x_g.pass_far()
     stack = scatter_lhs(s_map, gb[...].reshape(local * n_dev, LANES), tok)
     for d in range(n_dev):
         part_x[d % 2, d // 2] = token_sums(stack, d, u_ref[d].reshape(local * cap, width), tok, cap)

time: 130 us -> 129 us (level)
  transfers between devices with their start and end apart: 3 -> 3, of which waited for: 0 -> 0; matrix products, arithmetic and copies ran while one was open for 0% -> 0% of each run, Pallas kernels for 26% -> 27%
where the time goes in v10:
time: 129 us
  Pallas kernels  124 us (96%)
  starting transfers between devices  4.1 us (3%)
    pallas_call x1, Pallas kernels, device_program(): pl.pallas_call(functools.partial(first_kernel, dims), out_shape=(rows_all...  40.6 us
    pallas_call x2, Pallas kernels, backward(): pl.pallas_call(functools.partial(backward_kernel, dims), out_shape=(sds((...  40.4 us
    pallas_call x1, Pallas kernels, device_program(): pl.pallas_call(functools.partial(middle_kernel, dims), out_shape=(rows_al...  27 us
    pallas_call x1, Pallas kernels, device_program(): pl.pallas_call(functools.partial(last_kernel, dims), out_shape=(own, sds(...  13.9 us
    ppermute x3, starting transfers between devices, shift(): lax.ppermute(rows, 'ep', [(i, (i + 2 * hop) % n_dev) for i in range(n_dev)])  4.1 us
  transfers between devices with their start and end apart: 3, of which 0 were waited for; matrix products, arithmetic and copies ran while one was open for 0% of the time, Pallas kernels for 27%

profile of v10, /device:TPU:113, one launch (start us, length us, event | category | flops | bytes accessed | tf_op | source)
XLA Modules:
  0.0 128.8 jit_solution(14961745134350112819)
XLA Ops:
  0.6 40.6 %first.1 = (bf16[8,64,768]{2,1,0:T(8,128)(2,1)}, bf16[8,64,768]{2,1,0:T(8,128)(2,1)}, bf16[64,768]{1,0:T(8,128)(2,1)}, f32[16,8,128]{2,1,0:T(8,128)}, f32[16,8,1...) custom-call(bf16[64,768]{1,0:T(8,128)(2,1)} %x_ref.3, ...), custom_call_target="tpu_custom_call" | custom-call | tf_op jit(solution)/shard_map/first/pallas_call | solution.py:587
  41.3 20.2 %backward.2 = (f32[16,768,256]{2,1,0:T(8,128)}, f32[16,768,256]{2,1,0:T(8,128)}, f32[16,256,768]{2,1,0:T(8,128)}, f32[8,64,768]{2,1,0:T(8,128)}, f32[8,8,128]{2,1,0:T(8,128)}) custom-call(bf16[8,64,768]{2,1,0:T(8,128)(2,1)} %get-tuple-element.45.x_all.mid_in, bf16[8,64,768]{2,1,0:T(8,128)(2,1)} %get-tuple-element.46.dy_all, ...), custom_call_target="tpu_custom_call" | custom-call | flops 7247757312 | bytes 56623104 | tf_op jit(solution)/shard_map/backward/pallas_call | solution.py:601
  61.5 27.0 %middle.1 = (bf16[8,64,768]{2,1,0:T(8,128)(2,1)}, bf16[8,64,768]{2,1,0:T(8,128)(2,1)}, bf16[64,768]{1,0:T(8,128)(2,1)}, f32[64,768]{1,0:T(8,128)}, f32[64,768]{1...) custom-call(bf16[64,768]{1,0:T(8,128)(2,1)} %dy_ref.3, bf16[64,768]{1,0:T(8,128)(2,1)} %x_ref.3, ...), custom_call_target="tpu_custom_call" | custom-call | tf_op jit(solution)/shard_map/middle/pallas_call | solution.py:622
  88.5 0.4 collective-permute-start
  88.9 2.4 %collective-permute-start.1 = (f32[64,768]{1,0:T(8,128)}, f32[64,768]{1,0:T(8,128)}, u32[]{:S(2)}, u32[]{:S(2)}) collective-permute-start(f32[64,768]{1,0:T(8,128)} %get-tuple-element.51), channel_id=1, source_target_pairs={{0,4},{1,5},{2,6},{3,7},{4,0},{5,1},{6,2},{7,3},{8,12},{9,13},{10,... | collective-permute-start | bytes 589832 | tf_op jit(solution)/shard_map/ppermute | solution.py:635
  91.3 1.3 %collective-permute-start.2 = (f32[64,768]{1,0:T(8,128)}, f32[64,768]{1,0:T(8,128)}, u32[]{:S(2)}, u32[]{:S(2)}) collective-permute-start(f32[64,768]{1,0:T(8,128)} %get-tuple-element.52), channel_id=1, source_target_pairs={{0,6},{1,7},{2,0},{3,1},{4,2},{5,3},{6,4},{7,5},{8,14},{9,15},{10,... | collective-permute-start | bytes 589832 | tf_op jit(solution)/shard_map/ppermute | solution.py:635
  92.6 20.2 %backward.3 = (f32[16,768,256]{2,1,0:T(8,128)}, f32[16,768,256]{2,1,0:T(8,128)}, f32[16,256,768]{2,1,0:T(8,128)}, f32[8,64,768]{2,1,0:T(8,128)}, f32[8,8,128]{2,1,0:T(8,128)}) custom-call(bf16[8,64,768]{2,1,0:T(8,128)(2,1)} %get-tuple-element.53.x_all, bf16[8,64,768]{2,1,0:T(8,128)(2,1)} %get-tuple-element.54.dy_all, f32[16,8,128]{2,1,0:T(8,128)} %get-tuple-element.55.s_ref, ...), custom_call_target="tpu_custom_call" | custom-call | flops 7247757312 | bytes 56623104 | tf_op jit(solution)/shard_map/backward/pallas_call | solution.py:601
  112.9 13.9 %last.1 = (bf16[64,768]{1,0:T(8,128)(2,1)}, f32[16,128]{1,0:T(8,128)}) custom-call(f32[8,8,128]{2,1,0:T(8,128)} %get-tuple-element.58.dg_a, f32[8,8,128]{2,1,0:T(8,128)} %get-tuple-element.59.dg_b, bf16[64,768]{1,0:T(8,128)(2,1)} %get-tuple-element.60.dmid_ref, f32[8,64,768]{2,1,0:T(8,128)} %get-tuple-element.61.part_in), custom_call_target="tpu_custom_call" | custom-call | tf_op jit(solution)/shard_map/last/pallas_call | solution.py:640
  126.8 0.0 collective-permute-done.left_x
  126.8 0.0 collective-permute-done.1.opp_x
  126.8 0.0 collective-permute-done.2.right_x
  126.8 2.0 %final.1 = (bf16[64,768]{1,0:T(8,128)(2,1)}, bf16[64,768]{1,0:T(8,128)(2,1)}, f32[8,64]{1,0:T(8,128)}, f32[8,64]{1,0:T(8,128)}) custom-call(bf16[64,768]{1,0:T(8,128)(2,1)} %get-tuple-element.42.mid_ref, f32[64,768]{1,0:T(8,128)} %get-tuple-element.49.own_x, f32[64,768]{1,0:T(8,128)} %collective-permute-done.left_x, f32[64,768]{1,0:T(8,128)} %collective-permute-done.1.opp_x, ...), custom_call_target="tpu_custom_call" | custom-call | tf_op jit(solution)/shard_map/final/pallas_call | solution.py:650
Async XLA Ops:
  88.5 38.3 %collective-permute-start = (f32[64,768]{1,0:T(8,128)}, f32[64,768]{1,0:T(8,128)}, u32[]{:S(2)}, u32[]{:S(2)}) collective-permute-start(f32[64,768]{1,0:T(8,128)} %get-tuple-element.50), channel_id=1, source_target_pairs={{0,2},{1,3},{2,4},{3,5},{4,6},{5,7},{6,0},{7,1},{8,10},{9,11},{10,... | collective-permute-start | bytes 589832 | tf_op jit(solution)/shard_map/ppermute | solution.py:635
  88.9 37.9 %collective-permute-start.1 = (f32[64,768]{1,0:T(8,128)}, f32[64,768]{1,0:T(8,128)}, u32[]{:S(2)}, u32[]{:S(2)}) collective-permute-start(f32[64,768]{1,0:T(8,128)} %get-tuple-element.51), channel_id=1, source_target_pairs={{0,4},{1,5},{2,6},{3,7},{4,0},{5,1},{6,2},{7,3},{8,12},{9,13},{10,... | collective-permute-start | bytes 589832 | tf_op jit(solution)/shard_map/ppermute | solution.py:635
  91.3 35.5 %collective-permute-start.2 = (f32[64,768]{1,0:T(8,128)}, f32[64,768]{1,0:T(8,128)}, u32[]{:S(2)}, u32[]{:S(2)}) collective-permute-start(f32[64,768]{1,0:T(8,128)} %get-tuple-element.52), channel_id=1, source_target_pairs={{0,6},{1,7},{2,0},{3,1},{4,2},{5,3},{6,4},{7,5},{8,14},{9,15},{10,... | collective-permute-start | bytes 589832 | tf_op jit(solution)/shard_map/ppermute | solution.py:635
